TPU v7x, 128 devices: a whole 4x4x4 slice. The times are simulated.
128 devices in a mesh: gx: 32 (over x, y, core), gy: 4 (over z).
Axes of the slice: x: 4, y: 4, z: 4, core: 2. Of those that a mesh axis runs over, the one named last changes fastest.
Arguments:
- signals: float32 [64, 32, 16, 128], P('gx', 'gy'), may hold values from -6 to 6
- tiles: bfloat16 [64, 32, 4, 128, 128], P('gx', 'gy'), may hold values from 0 to 0.00390625
- tile_dir: int32 [64, 32, 4], P('gx', 'gy'), may hold values from 0 to 8
- tile_mask: int32 [64, 32, 4], P('gx', 'gy'), may hold values 0 or 1
- live_rows: int32 [64, 32], P('gx', 'gy'), may hold values from 32 to 128
- bound_rows: int32 [64, 32], P('gx', 'gy'), may hold values from 1 to 32, as said below
- scale_coeffs: float32 [6, 5], replicated, may hold values from -1 to 1
- spectral_bound: float32 [1], replicated, may hold values from 2.5 to 4
Outputs:
- coefficients: float32 [6, 64, 32, 16, 128], P(None, 'gx', 'gy')
- energy: float32 [6, 16], replicated
Inputs may be any that keep to these rules, and one draw needn't show every extreme that they name: `bound_rows`: in every draw, some blocks on every device have exactly 32 boundary rows.
All inputs are finite; a program needn't handle non-finite values. No bound on the sum of `tile_mask` on one device may be relied on, other than what follows from the above.
Results may differ from a plain program's by a relative error of at most 0.0003.
Values may be sent and summed in bfloat16 or wider, within the bound.
No kernel may reach another device: no remote copies, remote signals or barrier semaphores. Data moves between devices by JAX's collectives and lax.ppermute only.
A program may use at most 64 MiB of HBM per device.

v0:
```python
import jax
import jax.numpy as jnp
from jax import lax
from jax.sharding import Mesh
from jax.sharding import PartitionSpec as P

DEG = 4
GX_GY = ("gx_0", "gx_1", "gx_2", "gy")
GX = ("gx_0", "gx_1", "gx_2")


def with_halo(array, sides, width):
    for axis, dim in sides:
        devices, length = (lax.axis_size(axis), array.shape[dim])
        up = [(i, (i + 1) % devices) for i in range(devices - 1)]
        down = [(j, i) for i, j in up]
        last = lax.slice_in_dim(array, length - width, length, axis=dim)
        first = lax.slice_in_dim(array, 0, width, axis=dim)
        before = lax.ppermute(last, axis, up)
        after = lax.ppermute(first, axis, down)
        array = jnp.concatenate([before, array, after], axis=dim)
    return array


def over_axes(array, axes):
    for axis in axes:
        array = lax.psum(array, axis)
    return array


def scaled_laplacian(values, adjacent, degree, factor):
    return factor * (degree * values - adjacent) - values


def shards(
    signals, tiles, tile_dir, tile_mask, live_rows, bound_rows, scale_coeffs, spectral_bound
):
    tile_size = signals.shape[3]
    extent_x = signals.shape[0]
    extent_y = signals.shape[1]
    slot_count = tiles.shape[2]
    block_count = extent_x * extent_y
    positions = lax.broadcasted_iota(jnp.int32, (1, 1, tile_size), 2)
    live_ind = (positions < live_rows[:, :, None]).astype(jnp.float32)
    bound_ind = (positions < bound_rows[:, :, None]).astype(jnp.float32)
    flat_tiles = tiles.reshape(block_count, slot_count, tile_size, tile_size)

    def adjacency(values):
        own_rows = values.astype(jnp.bfloat16)
        edge_rows = (values * bound_ind[:, :, None, :]).astype(jnp.bfloat16)
        padded = with_halo(edge_rows, ((GX, 0), ("gy", 1)), 1)
        slot_list = []
        for slot_index in range(slot_count):
            picked = jnp.zeros_like(own_rows)
            for direction in range(9):
                step_x = direction // 3 - 1
                step_y = direction % 3 - 1
                if direction == 4:
                    source = own_rows
                else:
                    source = padded[
                        1 + step_x : 1 + step_x + extent_x, 1 + step_y : 1 + step_y + extent_y
                    ]
                matches = (tile_dir[:, :, slot_index] == direction)[:, :, None, None]
                picked = jnp.where(matches, source, picked)
            kept = (tile_mask[:, :, slot_index] == 1)[:, :, None, None]
            picked = jnp.where(kept, picked, jnp.zeros_like(picked))
            slot_list.append(picked)
        inputs = jnp.stack(slot_list, axis=1 + 1)
        flat_inputs = inputs.reshape(block_count, slot_count, inputs.shape[3], tile_size)
        product = lax.dot_general(
            flat_inputs,
            flat_tiles,
            (((1, 3), (1, 3)), ((0,), (0,))),
            preferred_element_type=jnp.float32,
        )
        product = product.reshape(extent_x, extent_y, inputs.shape[3], tile_size)
        return product * live_ind[:, :, None, :]

    channels = signals.shape[2]
    initial = signals * live_ind[:, :, None, :]
    joined = jnp.concatenate([initial, live_ind[:, :, None, :]], axis=2)
    first_pass = adjacency(joined)
    degree = first_pass[:, :, channels:, :]
    factor = 2.0 / spectral_bound[0]
    previous = initial
    current = scaled_laplacian(initial, first_pass[:, :, :channels, :], degree, factor)
    totals = 0.5 * scale_coeffs[:, 0][:, None, None, None, None] * initial[None]
    totals = totals + scale_coeffs[:, 1][:, None, None, None, None] * current[None]
    for degree_index in range(2, DEG + 1):
        adjacent = adjacency(current)
        following = 2.0 * scaled_laplacian(current, adjacent, degree, factor) - previous
        previous = current
        current = following
        totals = totals + scale_coeffs[:, degree_index][:, None, None, None, None] * current[None]
    nodes = extent_x * extent_y * tile_size * lax.axis_size(GX) * lax.axis_size("gy")
    local_sums = jnp.sum(totals * totals, axis=(1, 2, 4))
    energy = over_axes(local_sums, GX_GY) / nodes
    return (totals, energy)


def solution(mesh):
    torus = Mesh(mesh.devices.reshape(4, 4, 2, mesh.shape["gy"]), ("gx_0", "gx_1", "gx_2", "gy"))
    placed = (
        P(GX, "gy", None, None),
        P(GX, "gy", None, None, None),
        P(GX, "gy", None),
        P(GX, "gy", None),
        P(GX, "gy"),
        P(GX, "gy"),
        P(),
        P(),
    )
    return jax.shard_map(
        shards,
        mesh=torus,
        in_specs=placed,
        out_specs=(P(None, GX, "gy", None, None), P()),
        check_vma=False,
    )
```

profile of v0, /device:TPU:1, one launch (start us, length us, event | category | flops | bytes accessed | tf_op | source)
XLA Modules:
  0.0 113.1 jit_solution(3090985521356103053)
XLA Ops:
  3.3 4.6 %collective-permute-start = (bf16[1,8,17,128]{3,2,1,0:T(8,128)(2,1)S(1)}, bf16[1,8,17,128]{3,2,1,0:T(8,128)(2,1)S(1)}, u32[]{:S(2)}, u32[]{:S(2)}) collective-permute-start(bf16[1,8,17,128]{3,2,1,0:T(8,128)(2,1)S(1)} %get-tuple-element.37), channel_id=1, source_target_pairs={{0,4},{4,8},{8,12},{12,16},{16,20},{20,24},{24,28},{28,32},{32,36}... | collective-permute-start | bytes 104456 | tf_op jit(solution)/shard_map/ppermute | solution.py:19
  7.9 1.9 %collective-permute-start.1 = (bf16[1,8,17,128]{3,2,1,0:T(8,128)(2,1)S(1)}, bf16[1,8,17,128]{3,2,1,0:T(8,128)(2,1)S(1)}, u32[]{:S(2)}, u32[]{:S(2)}) collective-permute-start(bf16[1,8,17,128]{3,2,1,0:T(8,128)(2,1)S(1)} %get-tuple-element.38), channel_id=1, source_target_pairs={{4,0},{8,4},{12,8},{16,12},{20,16},{24,20},{28,24},{32,28},{36,32}... | collective-permute-start | bytes 104456 | tf_op jit(solution)/shard_map/ppermute | solution.py:20
  13.3 1.3 %collective-permute-start.2 = (bf16[4,1,17,128]{3,2,1,0:T(8,128)(2,1)S(1)}, bf16[4,1,17,128]{3,2,1,0:T(8,128)(2,1)S(1)}, u32[]{:S(2)}, u32[]{:S(2)}) collective-permute-start(bf16[4,1,17,128]{3,2,1,0:T(8,128)(2,1)S(1)} %get-tuple-element.23), channel_id=1, source_target_pairs={{1,0},{2,1},{3,2},{5,4},{6,5},{7,6},{9,8},{10,9},{11,10},{13,12},{... | collective-permute-start | bytes 52232 | tf_op jit(solution)/shard_map/ppermute | solution.py:20
  14.6 4.2 %collective-permute-start.3 = (bf16[4,1,17,128]{3,2,1,0:T(8,128)(2,1)S(1)}, bf16[4,1,17,128]{3,2,1,0:T(8,128)(2,1)S(1)}, u32[]{:S(2)}, u32[]{:S(2)}) collective-permute-start(bf16[4,1,17,128]{3,2,1,0:T(8,128)(2,1)S(1)} %get-tuple-element.24), channel_id=1, source_target_pairs={{0,1},{1,2},{2,3},{4,5},{5,6},{6,7},{8,9},{9,10},{10,11},{12,13},{... | collective-permute-start | bytes 52232 | tf_op jit(solution)/shard_map/ppermute | solution.py:19
  21.7 3.9 %collective-permute-start.4 = (bf16[1,8,16,128]{3,2,1,0:T(8,128)(2,1)S(1)}, bf16[1,8,16,128]{3,2,1,0:T(8,128)(2,1)S(1)}, u32[]{:S(2)}, u32[]{:S(2)}) collective-permute-start(bf16[1,8,16,128]{3,2,1,0:T(8,128)(2,1)S(1)} %get-tuple-element.43), channel_id=1, source_target_pairs={{0,4},{4,8},{8,12},{12,16},{16,20},{20,24},{24,28},{28,32},{32,36}... | collective-permute-start | bytes 98312 | tf_op jit(solution)/shard_map/ppermute | solution.py:19
  25.6 1.9 %collective-permute-start.5 = (bf16[1,8,16,128]{3,2,1,0:T(8,128)(2,1)S(1)}, bf16[1,8,16,128]{3,2,1,0:T(8,128)(2,1)S(1)}, u32[]{:S(2)}, u32[]{:S(2)}) collective-permute-start(bf16[1,8,16,128]{3,2,1,0:T(8,128)(2,1)S(1)} %get-tuple-element.44), channel_id=1, source_target_pairs={{4,0},{8,4},{12,8},{16,12},{20,16},{24,20},{28,24},{32,28},{36,32}... | collective-permute-start | bytes 98312 | tf_op jit(solution)/shard_map/ppermute | solution.py:20
  27.5 3.3 %collective-permute-done.5 = bf16[1,8,16,128]{3,2,1,0:T(8,128)(2,1)S(1)} collective-permute-done((bf16[1,8,16,128]{3,2,1,0:T(8,128)(2,1)S(1)}, bf16[1,8,16,128]{3,2,1,0:T(8,128)(2,1)S(1)}, u32[]{:S(2)}, u32[]{:S(2)}) %collective-permute-start.5) | collective-permute-done | bytes 32800 | tf_op jit(solution)/shard_map/ppermute | solution.py:20
  30.8 1.3 %collective-permute-start.6 = (bf16[4,1,16,128]{3,2,1,0:T(8,128)(2,1)S(1)}, bf16[4,1,16,128]{3,2,1,0:T(8,128)(2,1)S(1)}, u32[]{:S(2)}, u32[]{:S(2)}) collective-permute-start(bf16[4,1,16,128]{3,2,1,0:T(8,128)(2,1)S(1)} %get-tuple-element.35), channel_id=1, source_target_pairs={{1,0},{2,1},{3,2},{5,4},{6,5},{7,6},{9,8},{10,9},{11,10},{13,12},{... | collective-permute-start | bytes 49160 | tf_op jit(solution)/shard_map/ppermute | solution.py:20
  32.1 4.6 %collective-permute-start.7 = (bf16[4,1,16,128]{3,2,1,0:T(8,128)(2,1)S(1)}, bf16[4,1,16,128]{3,2,1,0:T(8,128)(2,1)S(1)}, u32[]{:S(2)}, u32[]{:S(2)}) collective-permute-start(bf16[4,1,16,128]{3,2,1,0:T(8,128)(2,1)S(1)} %get-tuple-element.36), channel_id=1, source_target_pairs={{0,1},{1,2},{2,3},{4,5},{5,6},{6,7},{8,9},{9,10},{10,11},{12,13},{... | collective-permute-start | bytes 49160 | tf_op jit(solution)/shard_map/ppermute | solution.py:19
  39.3 2.8 %collective-permute-start.8 = (bf16[1,8,16,128]{3,2,1,0:T(8,128)(2,1)S(1)}, bf16[1,8,16,128]{3,2,1,0:T(8,128)(2,1)S(1)}, u32[]{:S(2)}, u32[]{:S(2)}) collective-permute-start(bf16[1,8,16,128]{3,2,1,0:T(8,128)(2,1)S(1)} %get-tuple-element.41), channel_id=1, source_target_pairs={{0,4},{4,8},{8,12},{12,16},{16,20},{20,24},{24,28},{28,32},{32,36}... | collective-permute-start | bytes 98312 | tf_op jit(solution)/shard_map/ppermute | solution.py:19
  42.1 1.9 %collective-permute-start.9 = (bf16[1,8,16,128]{3,2,1,0:T(8,128)(2,1)S(1)}, bf16[1,8,16,128]{3,2,1,0:T(8,128)(2,1)S(1)}, u32[]{:S(2)}, u32[]{:S(2)}) collective-permute-start(bf16[1,8,16,128]{3,2,1,0:T(8,128)(2,1)S(1)} %get-tuple-element.42), channel_id=1, source_target_pairs={{4,0},{8,4},{12,8},{16,12},{20,16},{24,20},{28,24},{32,28},{36,32}... | collective-permute-start | bytes 98312 | tf_op jit(solution)/shard_map/ppermute | solution.py:20
  44.0 3.3 %collective-permute-done.9 = bf16[1,8,16,128]{3,2,1,0:T(8,128)(2,1)S(1)} collective-permute-done((bf16[1,8,16,128]{3,2,1,0:T(8,128)(2,1)S(1)}, bf16[1,8,16,128]{3,2,1,0:T(8,128)(2,1)S(1)}, u32[]{:S(2)}, u32[]{:S(2)}) %collective-permute-start.9) | collective-permute-done | bytes 32800 | tf_op jit(solution)/shard_map/ppermute | solution.py:20
  47.3 1.3 %collective-permute-start.10 = (bf16[4,1,16,128]{3,2,1,0:T(8,128)(2,1)S(1)}, bf16[4,1,16,128]{3,2,1,0:T(8,128)(2,1)S(1)}, u32[]{:S(2)}, u32[]{:S(2)}) collective-permute-start(bf16[4,1,16,128]{3,2,1,0:T(8,128)(2,1)S(1)} %get-tuple-element.31), channel_id=1, source_target_pairs={{1,0},{2,1},{3,2},{5,4},{6,5},{7,6},{9,8},{10,9},{11,10},{13,12},{... | collective-permute-start | bytes 49160 | tf_op jit(solution)/shard_map/ppermute | solution.py:20
  48.6 4.5 %collective-permute-start.11 = (bf16[4,1,16,128]{3,2,1,0:T(8,128)(2,1)S(1)}, bf16[4,1,16,128]{3,2,1,0:T(8,128)(2,1)S(1)}, u32[]{:S(2)}, u32[]{:S(2)}) collective-permute-start(bf16[4,1,16,128]{3,2,1,0:T(8,128)(2,1)S(1)} %get-tuple-element.32), channel_id=1, source_target_pairs={{0,1},{1,2},{2,3},{4,5},{5,6},{6,7},{8,9},{9,10},{10,11},{12,13},{... | collective-permute-start | bytes 49160 | tf_op jit(solution)/shard_map/ppermute | solution.py:19
  55.8 2.8 %collective-permute-start.12 = (bf16[1,8,16,128]{3,2,1,0:T(8,128)(2,1)S(1)}, bf16[1,8,16,128]{3,2,1,0:T(8,128)(2,1)S(1)}, u32[]{:S(2)}, u32[]{:S(2)}) collective-permute-start(bf16[1,8,16,128]{3,2,1,0:T(8,128)(2,1)S(1)} %get-tuple-element.39), channel_id=1, source_target_pairs={{0,4},{4,8},{8,12},{12,16},{16,20},{20,24},{24,28},{28,32},{32,36}... | collective-permute-start | bytes 98312 | tf_op jit(solution)/shard_map/ppermute | solution.py:19
  58.6 1.9 %collective-permute-start.13 = (bf16[1,8,16,128]{3,2,1,0:T(8,128)(2,1)S(1)}, bf16[1,8,16,128]{3,2,1,0:T(8,128)(2,1)S(1)}, u32[]{:S(2)}, u32[]{:S(2)}) collective-permute-start(bf16[1,8,16,128]{3,2,1,0:T(8,128)(2,1)S(1)} %get-tuple-element.40), channel_id=1, source_target_pairs={{4,0},{8,4},{12,8},{16,12},{20,16},{24,20},{28,24},{32,28},{36,32}... | collective-permute-start | bytes 98312 | tf_op jit(solution)/shard_map/ppermute | solution.py:20
  60.5 3.3 %collective-permute-done.13 = bf16[1,8,16,128]{3,2,1,0:T(8,128)(2,1)S(1)} collective-permute-done((bf16[1,8,16,128]{3,2,1,0:T(8,128)(2,1)S(1)}, bf16[1,8,16,128]{3,2,1,0:T(8,128)(2,1)S(1)}, u32[]{:S(2)}, u32[]{:S(2)}) %collective-permute-start.13) | collective-permute-done | bytes 32800 | tf_op jit(solution)/shard_map/ppermute | solution.py:20
  63.8 1.3 %collective-permute-start.14 = (bf16[4,1,16,128]{3,2,1,0:T(8,128)(2,1)S(1)}, bf16[4,1,16,128]{3,2,1,0:T(8,128)(2,1)S(1)}, u32[]{:S(2)}, u32[]{:S(2)}) collective-permute-start(bf16[4,1,16,128]{3,2,1,0:T(8,128)(2,1)S(1)} %get-tuple-element.27), channel_id=1, source_target_pairs={{1,0},{2,1},{3,2},{5,4},{6,5},{7,6},{9,8},{10,9},{11,10},{13,12},{... | collective-permute-start | bytes 49160 | tf_op jit(solution)/shard_map/ppermute | solution.py:20
  65.1 4.5 %collective-permute-start.15 = (bf16[4,1,16,128]{3,2,1,0:T(8,128)(2,1)S(1)}, bf16[4,1,16,128]{3,2,1,0:T(8,128)(2,1)S(1)}, u32[]{:S(2)}, u32[]{:S(2)}) collective-permute-start(bf16[4,1,16,128]{3,2,1,0:T(8,128)(2,1)S(1)} %get-tuple-element.28), channel_id=1, source_target_pairs={{0,1},{1,2},{2,3},{4,5},{5,6},{6,7},{8,9},{9,10},{10,11},{12,13},{... | collective-permute-start | bytes 49160 | tf_op jit(solution)/shard_map/ppermute | solution.py:19
  72.2 1.3 %multiply_reduce_fusion = (f32[6,16]{1,0:T(8,128)S(1)}, f32[6,2,8,16,128]{4,3,2,1,0:T(8,128)}) fusion(f32[2,8,16,128]{3,2,1,0:T(8,128)S(1)} %multiply_subtract_fusion, f32[6]{0:T(128)S(1)} %get-tuple-element.5, f32[2,8,16,128]{3,2,1,0:T(8,128)S(1)} %get-tuple-element.12, f32[6]{0:T(128)S(1)} %get-tuple-element.6, f32[2,8,16,128]{3,2,1,0:T(8,128)S(1)} %get-tuple-element.16, ...), kind=kLoop, calls=%fused_computation | loop fusion | flops 2162592 | bytes 1442296 | tf_op jit(solution)/shard_map/reduce_sum | solution.py:97
  73.5 11.1 %psum.28 = f32[6,16]{1,0:T(8,128)S(1)} all-reduce(f32[6,16]{1,0:T(8,128)S(1)} %get-tuple-element.7), channel_id=1, replica_groups=mesh['gx_0'=4,'gx_1'=4,'gx_2'=2,'gy'=4] {'gx_0'}, use_global_device_ids=true, to_apply=%region_1.2 | all-reduce | flops 96 | bytes 768 | tf_op jit(solution)/shard_map/psum | solution.py:27
  84.6 12.8 %psum.29 = f32[6,16]{1,0:T(8,128)S(1)} all-reduce(f32[6,16]{1,0:T(8,128)S(1)} %psum.28), channel_id=1, replica_groups=mesh['gx_0'=4,'gx_1'=4,'gx_2'=2,'gy'=4] {'gx_1'}, use_global_device_ids=true, to_apply=%region_2.3 | all-reduce | flops 96 | bytes 768 | tf_op jit(solution)/shard_map/psum | solution.py:27
  97.4 4.5 %psum.30 = f32[6,16]{1,0:T(8,128)S(1)} all-reduce(f32[6,16]{1,0:T(8,128)S(1)} %psum.29), channel_id=1, replica_groups=mesh['gx_0'=4,'gx_1'=4,'gx_2'=2,'gy'=4] {'gx_2'}, use_global_device_ids=true, to_apply=%region_3.4 | all-reduce | flops 96 | bytes 768 | tf_op jit(solution)/shard_map/psum | solution.py:27
  101.9 10.6 %psum.31 = f32[6,16]{1,0:T(8,128)S(1)} all-reduce(f32[6,16]{1,0:T(8,128)S(1)} %psum.30), channel_id=1, replica_groups=mesh['gx_0'=4,'gx_1'=4,'gx_2'=2,'gy'=4] {'gy'}, use_global_device_ids=true, to_apply=%region_4.5 | all-reduce | flops 96 | bytes 768 | tf_op jit(solution)/shard_map/psum | solution.py:27
  (87 shorter events, 16.3 us)
Async XLA Ops:
  0.6 20.2 %copy-start = (bf16[2,8,4,128,128]{4,3,2,1,0:T(8,128)(2,1)S(1)}, bf16[2,8,4,128,128]{4,3,2,1,0:T(8,128)(2,1)}, u32[]{:S(2)}) copy-start(bf16[2,8,4,128,128]{4,3,2,1,0:T(8,128)(2,1)} %param.9) | copy-start | bytes 6291460
  3.3 9.3 %collective-permute-start = (bf16[1,8,17,128]{3,2,1,0:T(8,128)(2,1)S(1)}, bf16[1,8,17,128]{3,2,1,0:T(8,128)(2,1)S(1)}, u32[]{:S(2)}, u32[]{:S(2)}) collective-permute-start(bf16[1,8,17,128]{3,2,1,0:T(8,128)(2,1)S(1)} %get-tuple-element.37), channel_id=1, source_target_pairs={{0,4},{4,8},{8,12},{12,16},{16,20},{20,24},{24,28},{28,32},{32,36}... | collective-permute-start | bytes 104456 | tf_op jit(solution)/shard_map/ppermute | solution.py:19
  7.9 5.4 %collective-permute-start.1 = (bf16[1,8,17,128]{3,2,1,0:T(8,128)(2,1)S(1)}, bf16[1,8,17,128]{3,2,1,0:T(8,128)(2,1)S(1)}, u32[]{:S(2)}, u32[]{:S(2)}) collective-permute-start(bf16[1,8,17,128]{3,2,1,0:T(8,128)(2,1)S(1)} %get-tuple-element.38), channel_id=1, source_target_pairs={{4,0},{8,4},{12,8},{16,12},{20,16},{24,20},{28,24},{32,28},{36,32}... | collective-permute-start | bytes 104456 | tf_op jit(solution)/shard_map/ppermute | solution.py:20
  13.3 6.2 %collective-permute-start.2 = (bf16[4,1,17,128]{3,2,1,0:T(8,128)(2,1)S(1)}, bf16[4,1,17,128]{3,2,1,0:T(8,128)(2,1)S(1)}, u32[]{:S(2)}, u32[]{:S(2)}) collective-permute-start(bf16[4,1,17,128]{3,2,1,0:T(8,128)(2,1)S(1)} %get-tuple-element.23), channel_id=1, source_target_pairs={{1,0},{2,1},{3,2},{5,4},{6,5},{7,6},{9,8},{10,9},{11,10},{13,12},{... | collective-permute-start | bytes 52232 | tf_op jit(solution)/shard_map/ppermute | solution.py:20
  14.6 5.1 %collective-permute-start.3 = (bf16[4,1,17,128]{3,2,1,0:T(8,128)(2,1)S(1)}, bf16[4,1,17,128]{3,2,1,0:T(8,128)(2,1)S(1)}, u32[]{:S(2)}, u32[]{:S(2)}) collective-permute-start(bf16[4,1,17,128]{3,2,1,0:T(8,128)(2,1)S(1)} %get-tuple-element.24), channel_id=1, source_target_pairs={{0,1},{1,2},{2,3},{4,5},{5,6},{6,7},{8,9},{9,10},{10,11},{12,13},{... | collective-permute-start | bytes 52232 | tf_op jit(solution)/shard_map/ppermute | solution.py:19
  20.6 1.0 copy-start.1
  21.7 5.9 %collective-permute-start.4 = (bf16[1,8,16,128]{3,2,1,0:T(8,128)(2,1)S(1)}, bf16[1,8,16,128]{3,2,1,0:T(8,128)(2,1)S(1)}, u32[]{:S(2)}, u32[]{:S(2)}) collective-permute-start(bf16[1,8,16,128]{3,2,1,0:T(8,128)(2,1)S(1)} %get-tuple-element.43), channel_id=1, source_target_pairs={{0,4},{4,8},{8,12},{12,16},{16,20},{20,24},{24,28},{28,32},{32,36}... | collective-permute-start | bytes 98312 | tf_op jit(solution)/shard_map/ppermute | solution.py:19
  25.6 5.2 %collective-permute-start.5 = (bf16[1,8,16,128]{3,2,1,0:T(8,128)(2,1)S(1)}, bf16[1,8,16,128]{3,2,1,0:T(8,128)(2,1)S(1)}, u32[]{:S(2)}, u32[]{:S(2)}) collective-permute-start(bf16[1,8,16,128]{3,2,1,0:T(8,128)(2,1)S(1)} %get-tuple-element.44), channel_id=1, source_target_pairs={{4,0},{8,4},{12,8},{16,12},{20,16},{24,20},{28,24},{32,28},{36,32}... | collective-permute-start | bytes 98312 | tf_op jit(solution)/shard_map/ppermute | solution.py:20
  30.8 5.9 %collective-permute-start.6 = (bf16[4,1,16,128]{3,2,1,0:T(8,128)(2,1)S(1)}, bf16[4,1,16,128]{3,2,1,0:T(8,128)(2,1)S(1)}, u32[]{:S(2)}, u32[]{:S(2)}) collective-permute-start(bf16[4,1,16,128]{3,2,1,0:T(8,128)(2,1)S(1)} %get-tuple-element.35), channel_id=1, source_target_pairs={{1,0},{2,1},{3,2},{5,4},{6,5},{7,6},{9,8},{10,9},{11,10},{13,12},{... | collective-permute-start | bytes 49160 | tf_op jit(solution)/shard_map/ppermute | solution.py:20
  32.1 5.4 %collective-permute-start.7 = (bf16[4,1,16,128]{3,2,1,0:T(8,128)(2,1)S(1)}, bf16[4,1,16,128]{3,2,1,0:T(8,128)(2,1)S(1)}, u32[]{:S(2)}, u32[]{:S(2)}) collective-permute-start(bf16[4,1,16,128]{3,2,1,0:T(8,128)(2,1)S(1)} %get-tuple-element.36), channel_id=1, source_target_pairs={{0,1},{1,2},{2,3},{4,5},{5,6},{6,7},{8,9},{9,10},{10,11},{12,13},{... | collective-permute-start | bytes 49160 | tf_op jit(solution)/shard_map/ppermute | solution.py:19
  39.3 4.7 %collective-permute-start.8 = (bf16[1,8,16,128]{3,2,1,0:T(8,128)(2,1)S(1)}, bf16[1,8,16,128]{3,2,1,0:T(8,128)(2,1)S(1)}, u32[]{:S(2)}, u32[]{:S(2)}) collective-permute-start(bf16[1,8,16,128]{3,2,1,0:T(8,128)(2,1)S(1)} %get-tuple-element.41), channel_id=1, source_target_pairs={{0,4},{4,8},{8,12},{12,16},{16,20},{20,24},{24,28},{28,32},{32,36}... | collective-permute-start | bytes 98312 | tf_op jit(solution)/shard_map/ppermute | solution.py:19
  42.1 5.2 %collective-permute-start.9 = (bf16[1,8,16,128]{3,2,1,0:T(8,128)(2,1)S(1)}, bf16[1,8,16,128]{3,2,1,0:T(8,128)(2,1)S(1)}, u32[]{:S(2)}, u32[]{:S(2)}) collective-permute-start(bf16[1,8,16,128]{3,2,1,0:T(8,128)(2,1)S(1)} %get-tuple-element.42), channel_id=1, source_target_pairs={{4,0},{8,4},{12,8},{16,12},{20,16},{24,20},{28,24},{32,28},{36,32}... | collective-permute-start | bytes 98312 | tf_op jit(solution)/shard_map/ppermute | solution.py:20
  47.3 5.8 %collective-permute-start.10 = (bf16[4,1,16,128]{3,2,1,0:T(8,128)(2,1)S(1)}, bf16[4,1,16,128]{3,2,1,0:T(8,128)(2,1)S(1)}, u32[]{:S(2)}, u32[]{:S(2)}) collective-permute-start(bf16[4,1,16,128]{3,2,1,0:T(8,128)(2,1)S(1)} %get-tuple-element.31), channel_id=1, source_target_pairs={{1,0},{2,1},{3,2},{5,4},{6,5},{7,6},{9,8},{10,9},{11,10},{13,12},{... | collective-permute-start | bytes 49160 | tf_op jit(solution)/shard_map/ppermute | solution.py:20
  48.6 5.4 %collective-permute-start.11 = (bf16[4,1,16,128]{3,2,1,0:T(8,128)(2,1)S(1)}, bf16[4,1,16,128]{3,2,1,0:T(8,128)(2,1)S(1)}, u32[]{:S(2)}, u32[]{:S(2)}) collective-permute-start(bf16[4,1,16,128]{3,2,1,0:T(8,128)(2,1)S(1)} %get-tuple-element.32), channel_id=1, source_target_pairs={{0,1},{1,2},{2,3},{4,5},{5,6},{6,7},{8,9},{9,10},{10,11},{12,13},{... | collective-permute-start | bytes 49160 | tf_op jit(solution)/shard_map/ppermute | solution.py:19
  54.8 14.9 %copy-start.2 = (f32[6,5]{1,0:T(8,128)S(1)}, f32[6,5]{1,0:T(8,128)}, u32[]{:S(2)}) copy-start(f32[6,5]{1,0:T(8,128)} %param.14) | copy-start | bytes 364
  55.8 4.7 %collective-permute-start.12 = (bf16[1,8,16,128]{3,2,1,0:T(8,128)(2,1)S(1)}, bf16[1,8,16,128]{3,2,1,0:T(8,128)(2,1)S(1)}, u32[]{:S(2)}, u32[]{:S(2)}) collective-permute-start(bf16[1,8,16,128]{3,2,1,0:T(8,128)(2,1)S(1)} %get-tuple-element.39), channel_id=1, source_target_pairs={{0,4},{4,8},{8,12},{12,16},{16,20},{20,24},{24,28},{28,32},{32,36}... | collective-permute-start | bytes 98312 | tf_op jit(solution)/shard_map/ppermute | solution.py:19
  58.6 5.2 %collective-permute-start.13 = (bf16[1,8,16,128]{3,2,1,0:T(8,128)(2,1)S(1)}, bf16[1,8,16,128]{3,2,1,0:T(8,128)(2,1)S(1)}, u32[]{:S(2)}, u32[]{:S(2)}) collective-permute-start(bf16[1,8,16,128]{3,2,1,0:T(8,128)(2,1)S(1)} %get-tuple-element.40), channel_id=1, source_target_pairs={{4,0},{8,4},{12,8},{16,12},{20,16},{24,20},{28,24},{32,28},{36,32}... | collective-permute-start | bytes 98312 | tf_op jit(solution)/shard_map/ppermute | solution.py:20
  63.8 6.1 %collective-permute-start.14 = (bf16[4,1,16,128]{3,2,1,0:T(8,128)(2,1)S(1)}, bf16[4,1,16,128]{3,2,1,0:T(8,128)(2,1)S(1)}, u32[]{:S(2)}, u32[]{:S(2)}) collective-permute-start(bf16[4,1,16,128]{3,2,1,0:T(8,128)(2,1)S(1)} %get-tuple-element.27), channel_id=1, source_target_pairs={{1,0},{2,1},{3,2},{5,4},{6,5},{7,6},{9,8},{10,9},{11,10},{13,12},{... | collective-permute-start | bytes 49160 | tf_op jit(solution)/shard_map/ppermute | solution.py:20
  65.1 5.4 %collective-permute-start.15 = (bf16[4,1,16,128]{3,2,1,0:T(8,128)(2,1)S(1)}, bf16[4,1,16,128]{3,2,1,0:T(8,128)(2,1)S(1)}, u32[]{:S(2)}, u32[]{:S(2)}) collective-permute-start(bf16[4,1,16,128]{3,2,1,0:T(8,128)(2,1)S(1)} %get-tuple-element.28), channel_id=1, source_target_pairs={{0,1},{1,2},{2,3},{4,5},{5,6},{6,7},{8,9},{9,10},{10,11},{12,13},{... | collective-permute-start | bytes 49160 | tf_op jit(solution)/shard_map/ppermute | solution.py:19
where the time goes:
time: 115 us; the launch traced here: 113 us
  starting transfers between devices  44.7 us (39%)
  blocking collectives  39 us (34%)
  waiting for transfers between devices  13.1 us (11%)
  other arithmetic  11.6 us (10%)
  matrix products  2.6 us (2%)
  between operations  1.97 us (2%)
    psum x4, blocking collectives, over_axes(): array = lax.psum(array, axis)  39 us
    ppermute x8, starting transfers between devices, with_halo(): before = lax.ppermute(last, axis, up)  31.9 us
    ppermute x8, starting transfers between devices, with_halo(): after = lax.ppermute(first, axis, down)  12.8 us
    ppermute x8, waiting for transfers between devices, with_halo(): after = lax.ppermute(first, axis, down)  10.6 us
    select_n x16, other arithmetic, adjacency(): picked = jnp.where(kept, picked, jnp.zeros_like(picked))  3.91 us
    dot_general x4, matrix products, adjacency(): lax.dot_general(flat_inputs, flat_tiles, (((1, 3), (1, 3)), ((0,), (0,)))...  2.6 us
    ppermute x8, waiting for transfers between devices, with_halo(): before = lax.ppermute(last, axis, up)  2.49 us
  transfers between devices with their start and end apart: 16, of which 8 were waited for; matrix products, arithmetic and copies ran while one was open for 3% of the time, Pallas kernels for 0%

commit v1 on v0

--- a/solution.py
+++ b/solution.py
@@ -9,23 +9,30 @@
 GX = ("gx_0", "gx_1", "gx_2")
 
 
+def neighbour_pairs(devices, first):
+    pairs = [(i, i + 1) for i in range(first, devices - 1, 2)]
+    return pairs + [(j, i) for i, j in pairs]
+
+
 def with_halo(array, sides, width):
     for axis, dim in sides:
         devices, length = (lax.axis_size(axis), array.shape[dim])
-        up = [(i, (i + 1) % devices) for i in range(devices - 1)]
-        down = [(j, i) for i, j in up]
+        is_even = lax.axis_index(axis) % 2 == 0
         last = lax.slice_in_dim(array, length - width, length, axis=dim)
         first = lax.slice_in_dim(array, 0, width, axis=dim)
-        before = lax.ppermute(last, axis, up)
-        after = lax.ppermute(first, axis, down)
+        from_a = lax.ppermute(jnp.where(is_even, last, first), axis, neighbour_pairs(devices, 0))
+        from_b = lax.ppermute(jnp.where(is_even, first, last), axis, neighbour_pairs(devices, 1))
+        before = jnp.where(is_even, from_b, from_a)
+        after = jnp.where(is_even, from_a, from_b)
         array = jnp.concatenate([before, array, after], axis=dim)
     return array
 
 
-def over_axes(array, axes):
-    for axis in axes:
-        array = lax.psum(array, axis)
-    return array
+def sum_over(array, axes, devices):
+    row = jnp.pad(array.reshape(1, -1), ((0, 0), (0, -array.size % 128)))
+    spread = jnp.broadcast_to(row[None], (devices,) + row.shape)
+    gathered = lax.all_to_all(spread, axes, 0, 0)
+    return jnp.sum(gathered, axis=0).reshape(-1)[: array.size].reshape(array.shape)
 
 
 def scaled_laplacian(values, adjacent, degree, factor):
@@ -48,7 +55,7 @@
     def adjacency(values):
         own_rows = values.astype(jnp.bfloat16)
         edge_rows = (values * bound_ind[:, :, None, :]).astype(jnp.bfloat16)
-        padded = with_halo(edge_rows, ((GX, 0), ("gy", 1)), 1)
+        padded = with_halo(edge_rows, (("gy", 1), (GX, 0)), 1)
         slot_list = []
         for slot_index in range(slot_count):
             picked = jnp.zeros_like(own_rows)
@@ -93,9 +100,10 @@
         previous = current
         current = following
         totals = totals + scale_coeffs[:, degree_index][:, None, None, None, None] * current[None]
-    nodes = extent_x * extent_y * tile_size * lax.axis_size(GX) * lax.axis_size("gy")
+    devices = lax.axis_size(GX) * lax.axis_size("gy")
+    nodes = extent_x * extent_y * tile_size * devices
     local_sums = jnp.sum(totals * totals, axis=(1, 2, 4))
-    energy = over_axes(local_sums, GX_GY) / nodes
+    energy = sum_over(local_sums, GX_GY, devices) / nodes
     return (totals, energy)
 
 

time: 115 us -> 88.6 us (0.77); the launches traced: 113 us -> 88.1 us
  blocking collectives: 39 us -> 25.8 us
  starting transfers between devices: 44.7 us -> 35.9 us
  waiting for transfers between devices: 13.1 us -> 9.57 us
    psum x4 -> x0, blocking collectives: 39 us -> none  [over_axes(): array = lax.psum(array, axis)]
    all_to_all x0 -> x1, blocking collectives: none -> 25.8 us  [sum_over(): gathered = lax.all_to_all(spread, axes, 0, 0)]
    ppermute x16, starting transfers between devices: 44.7 us -> 35.9 us  [the longest x8 19.2 us: with_halo(): lax.ppermute(jnp.where(is_even, first, last), axis, neighbour_pairs(devic...]
    ppermute x16, waiting for transfers between devices: 13.1 us -> 9.57 us  [the longest x8 6.44 us: with_halo(): lax.ppermute(jnp.where(is_even, first, last), axis, neighbour_pairs(devic...]
  transfers between devices with their start and end apart: 16 -> 16, of which waited for: 8 -> 7; matrix products, arithmetic and copies ran while one was open for 3% -> 3% of each run, Pallas kernels for 0% -> 0%
where the time goes in v1:
time: 88.6 us; the launch traced here: 88.1 us
  starting transfers between devices  35.9 us (41%)
  blocking collectives  25.8 us (29%)
  other arithmetic  11.2 us (13%)
  waiting for transfers between devices  9.57 us (11%)
  matrix products  2.6 us (3%)
  between operations  2.03 us (2%)
  local copies, waits for them, and re-layouts  0.97 us (1%)
    all_to_all x1, blocking collectives, sum_over(): gathered = lax.all_to_all(spread, axes, 0, 0)  25.8 us
    ppermute x8, starting transfers between devices, with_halo(): lax.ppermute(jnp.where(is_even, first, last), axis, neighbour_pairs(devic...  19.2 us
    ppermute x8, starting transfers between devices, with_halo(): lax.ppermute(jnp.where(is_even, last, first), axis, neighbour_pairs(devic...  16.7 us
    ppermute x8, waiting for transfers between devices, with_halo(): lax.ppermute(jnp.where(is_even, first, last), axis, neighbour_pairs(devic...  6.44 us
    select_n x16, other arithmetic, adjacency(): picked = jnp.where(kept, picked, jnp.zeros_like(picked))  3.91 us
    ppermute x8, waiting for transfers between devices, with_halo(): lax.ppermute(jnp.where(is_even, last, first), axis, neighbour_pairs(devic...  3.13 us
    dot_general x4, matrix products, adjacency(): lax.dot_general(flat_inputs, flat_tiles, (((1, 3), (1, 3)), ((0,), (0,)))...  2.6 us
  transfers between devices with their start and end apart: 16, of which 7 were waited for; matrix products, arithmetic and copies ran while one was open for 3% of the time, Pallas kernels for 0%

profile of v1, /device:TPU:1, one launch (start us, length us, event | category | flops | bytes accessed | tf_op | source)
XLA Modules:
  0.0 88.1 jit_solution(7839250057469804815)
XLA Ops:
  0.7 0.9 %compare_convert_fusion = f32[2,8,1,128]{3,2,1,0:T(1,128)S(1)} fusion(s32[2,8]{1,0:T(2,128)} %param.12), kind=kLoop, calls=%fused_computation.100 | loop fusion | flops 4096 | bytes 8256 | tf_op jit(solution)/shard_map/convert_element_type | solution.py:51
  1.6 0.8 fusion.35
  2.3 0.9 %broadcast_multiply_fusion.1 = f32[2,8,16,128]{3,2,1,0:T(8,128)S(1)} fusion(f32[2,8,16,128]{3,2,1,0:T(8,128)} %param.8, f32[2,8,128]{2,1,0:T(8,128)S(1)} %get-tuple-element.139), kind=kLoop, calls=%fused_computation.83 | loop fusion | flops 32768 | bytes 270336 | tf_op jit(solution)/shard_map/mul | solution.py:88
  4.0 5.4 %collective-permute-start.1 = (bf16[2,1,17,128]{3,2,1,0:T(8,128)(2,1)S(1)}, bf16[2,1,17,128]{3,2,1,0:T(8,128)(2,1)S(1)}, u32[]{:S(2)}, u32[]{:S(2)}) collective-permute-start(bf16[2,1,17,128]{3,2,1,0:T(8,128)(2,1)S(1)} %get-tuple-element.28), channel_id=1, source_target_pairs={{0,1},{2,3},{1,0},{3,2},{4,5},{6,7},{5,4},{7,6},{8,9},{10,11},{9,8... | collective-permute-start | bytes 26120 | tf_op jit(solution)/shard_map/ppermute | solution.py:23
  9.4 0.8 broadcast_compare_fusion.30
  10.2 0.8 broadcast_compare_fusion.31
  11.1 0.8 slice_compare_fusion.3
  12.3 1.3 %collective-permute-start.2 = (bf16[1,10,17,128]{3,2,1,0:T(8,128)(2,1)S(1)}, bf16[1,10,17,128]{3,2,1,0:T(8,128)(2,1)S(1)}, u32[]{:S(2)}, u32[]{:S(2)}) collective-permute-start(bf16[1,10,17,128]{3,2,1,0:T(8,128)(2,1)S(1)} %get-tuple-element.25), channel_id=1, source_target_pairs={{0,4},{8,12},{16,20},{24,28},{32,36},{40,44},{48,52},{56,60},{64,6... | collective-permute-start | bytes 130568 | tf_op jit(solution)/shard_map/ppermute | solution.py:23
  13.6 3.1 %collective-permute-start.3 = (bf16[1,10,17,128]{3,2,1,0:T(8,128)(2,1)S(1)}, bf16[1,10,17,128]{3,2,1,0:T(8,128)(2,1)S(1)}, u32[]{:S(2)}, u32[]{:S(2)}) collective-permute-start(bf16[1,10,17,128]{3,2,1,0:T(8,128)(2,1)S(1)} %get-tuple-element.26), channel_id=1, source_target_pairs={{4,8},{12,16},{20,24},{28,32},{36,40},{44,48},{52,56},{60,64},{68,... | collective-permute-start | bytes 130568 | tf_op jit(solution)/shard_map/ppermute | solution.py:24
  17.4 1.7 %collective-permute-done.3 = bf16[1,10,17,128]{3,2,1,0:T(8,128)(2,1)S(1)} collective-permute-done((bf16[1,10,17,128]{3,2,1,0:T(8,128)(2,1)S(1)}, bf16[1,10,17,128]{3,2,1,0:T(8,128)(2,1)S(1)}, u32[]{:S(2)}, u32[]{:S(2)}) %collective-permute-start.3) | collective-permute-done | bytes 43552 | tf_op jit(solution)/shard_map/ppermute | solution.py:24
  21.7 1.9 %collective-permute-start.5 = (bf16[2,1,16,128]{3,2,1,0:T(8,128)(2,1)S(1)}, bf16[2,1,16,128]{3,2,1,0:T(8,128)(2,1)S(1)}, u32[]{:S(2)}, u32[]{:S(2)}) collective-permute-start(bf16[2,1,16,128]{3,2,1,0:T(8,128)(2,1)S(1)} %get-tuple-element.52), channel_id=1, source_target_pairs={{0,1},{2,3},{1,0},{3,2},{4,5},{6,7},{5,4},{7,6},{8,9},{10,11},{9,8... | collective-permute-start | bytes 24584 | tf_op jit(solution)/shard_map/ppermute | solution.py:23
  23.6 1.0 %collective-permute-done.5 = bf16[2,1,16,128]{3,2,1,0:T(8,128)(2,1)S(1)} collective-permute-done((bf16[2,1,16,128]{3,2,1,0:T(8,128)(2,1)S(1)}, bf16[2,1,16,128]{3,2,1,0:T(8,128)(2,1)S(1)}, u32[]{:S(2)}, u32[]{:S(2)}) %collective-permute-start.5) | collective-permute-done | bytes 8224 | tf_op jit(solution)/shard_map/ppermute | solution.py:23
  24.8 4.1 %collective-permute-start.7 = (bf16[1,10,16,128]{3,2,1,0:T(8,128)(2,1)S(1)}, bf16[1,10,16,128]{3,2,1,0:T(8,128)(2,1)S(1)}, u32[]{:S(2)}, u32[]{:S(2)}) collective-permute-start(bf16[1,10,16,128]{3,2,1,0:T(8,128)(2,1)S(1)} %get-tuple-element.46), channel_id=1, source_target_pairs={{4,8},{12,16},{20,24},{28,32},{36,40},{44,48},{52,56},{60,64},{68,... | collective-permute-start | bytes 122888 | tf_op jit(solution)/shard_map/ppermute | solution.py:24
  28.9 1.7 %collective-permute-done.7 = bf16[1,10,16,128]{3,2,1,0:T(8,128)(2,1)S(1)} collective-permute-done((bf16[1,10,16,128]{3,2,1,0:T(8,128)(2,1)S(1)}, bf16[1,10,16,128]{3,2,1,0:T(8,128)(2,1)S(1)}, u32[]{:S(2)}, u32[]{:S(2)}) %collective-permute-start.7) | collective-permute-done | bytes 40992 | tf_op jit(solution)/shard_map/ppermute | solution.py:24
  33.0 4.7 %collective-permute-start.9 = (bf16[2,1,16,128]{3,2,1,0:T(8,128)(2,1)S(1)}, bf16[2,1,16,128]{3,2,1,0:T(8,128)(2,1)S(1)}, u32[]{:S(2)}, u32[]{:S(2)}) collective-permute-start(bf16[2,1,16,128]{3,2,1,0:T(8,128)(2,1)S(1)} %get-tuple-element.50), channel_id=1, source_target_pairs={{0,1},{2,3},{1,0},{3,2},{4,5},{6,7},{5,4},{7,6},{8,9},{10,11},{9,8... | collective-permute-start | bytes 24584 | tf_op jit(solution)/shard_map/ppermute | solution.py:23
  37.7 1.0 %collective-permute-done.9 = bf16[2,1,16,128]{3,2,1,0:T(8,128)(2,1)S(1)} collective-permute-done((bf16[2,1,16,128]{3,2,1,0:T(8,128)(2,1)S(1)}, bf16[2,1,16,128]{3,2,1,0:T(8,128)(2,1)S(1)}, u32[]{:S(2)}, u32[]{:S(2)}) %collective-permute-start.9) | collective-permute-done | bytes 8224 | tf_op jit(solution)/shard_map/ppermute | solution.py:23
  38.9 4.8 %collective-permute-start.11 = (bf16[1,10,16,128]{3,2,1,0:T(8,128)(2,1)S(1)}, bf16[1,10,16,128]{3,2,1,0:T(8,128)(2,1)S(1)}, u32[]{:S(2)}, u32[]{:S(2)}) collective-permute-start(bf16[1,10,16,128]{3,2,1,0:T(8,128)(2,1)S(1)} %get-tuple-element.40), channel_id=1, source_target_pairs={{4,8},{12,16},{20,24},{28,32},{36,40},{44,48},{52,56},{60,64},{68,... | collective-permute-start | bytes 122888 | tf_op jit(solution)/shard_map/ppermute | solution.py:24
  43.7 1.7 %collective-permute-done.11 = bf16[1,10,16,128]{3,2,1,0:T(8,128)(2,1)S(1)} collective-permute-done((bf16[1,10,16,128]{3,2,1,0:T(8,128)(2,1)S(1)}, bf16[1,10,16,128]{3,2,1,0:T(8,128)(2,1)S(1)}, u32[]{:S(2)}, u32[]{:S(2)}) %collective-permute-start.11) | collective-permute-done | bytes 40992 | tf_op jit(solution)/shard_map/ppermute | solution.py:24
  47.9 3.1 %collective-permute-start.13 = (bf16[2,1,16,128]{3,2,1,0:T(8,128)(2,1)S(1)}, bf16[2,1,16,128]{3,2,1,0:T(8,128)(2,1)S(1)}, u32[]{:S(2)}, u32[]{:S(2)}) collective-permute-start(bf16[2,1,16,128]{3,2,1,0:T(8,128)(2,1)S(1)} %get-tuple-element.48), channel_id=1, source_target_pairs={{0,1},{2,3},{1,0},{3,2},{4,5},{6,7},{5,4},{7,6},{8,9},{10,11},{9,8... | collective-permute-start | bytes 24584 | tf_op jit(solution)/shard_map/ppermute | solution.py:23
  50.9 1.0 %collective-permute-done.13 = bf16[2,1,16,128]{3,2,1,0:T(8,128)(2,1)S(1)} collective-permute-done((bf16[2,1,16,128]{3,2,1,0:T(8,128)(2,1)S(1)}, bf16[2,1,16,128]{3,2,1,0:T(8,128)(2,1)S(1)}, u32[]{:S(2)}, u32[]{:S(2)}) %collective-permute-start.13) | collective-permute-done | bytes 8224 | tf_op jit(solution)/shard_map/ppermute | solution.py:23
  52.1 4.6 %collective-permute-start.15 = (bf16[1,10,16,128]{3,2,1,0:T(8,128)(2,1)S(1)}, bf16[1,10,16,128]{3,2,1,0:T(8,128)(2,1)S(1)}, u32[]{:S(2)}, u32[]{:S(2)}) collective-permute-start(bf16[1,10,16,128]{3,2,1,0:T(8,128)(2,1)S(1)} %get-tuple-element.34), channel_id=1, source_target_pairs={{4,8},{12,16},{20,24},{28,32},{36,40},{44,48},{52,56},{60,64},{68,... | collective-permute-start | bytes 122888 | tf_op jit(solution)/shard_map/ppermute | solution.py:24
  57.0 1.4 %collective-permute-done.15 = bf16[1,10,16,128]{3,2,1,0:T(8,128)(2,1)S(1)} collective-permute-done((bf16[1,10,16,128]{3,2,1,0:T(8,128)(2,1)S(1)}, bf16[1,10,16,128]{3,2,1,0:T(8,128)(2,1)S(1)}, u32[]{:S(2)}, u32[]{:S(2)}) %collective-permute-start.15) | collective-permute-done | bytes 40992 | tf_op jit(solution)/shard_map/ppermute | solution.py:24
  60.2 1.3 %multiply_reduce_fusion = (f32[6,16]{1,0:T(8,128)S(1)}, f32[6,2,8,16,128]{4,3,2,1,0:T(8,128)}) fusion(f32[2,8,16,128]{3,2,1,0:T(8,128)S(1)} %multiply_subtract_fusion, f32[6]{0:T(128)S(1)} %get-tuple-element.5, f32[2,8,16,128]{3,2,1,0:T(8,128)S(1)} %get-tuple-element.12, f32[6]{0:T(128)S(1)} %get-tuple-element.6, f32[2,8,16,128]{3,2,1,0:T(8,128)S(1)} %get-tuple-element.16, ...), kind=kLoop, calls=%fused_computation | loop fusion | flops 2162592 | bytes 1442296 | tf_op jit(solution)/shard_map/reduce_sum | solution.py:105
  61.6 25.8 %all_to_all.5 = f32[128,1,128]{2,1,0:T(1,128)S(1)} all-to-all(f32[128,1,128]{2,1,0:T(1,128)S(1)} %broadcast_in_dim.912), channel_id=1, replica_groups=mesh['gx_0'=4,'gx_1'=4,'gx_2'=2,'gy'=4] {'gx_0','gx_1','gx_2','gy'}, dimensions={0} | all-to-all | bytes 131072 | tf_op jit(solution)/shard_map/all_to_all | solution.py:34
  (101 shorter events, 11.3 us)
Async XLA Ops:
  0.6 19.6 %copy-start = (bf16[2,8,4,128,128]{4,3,2,1,0:T(8,128)(2,1)S(1)}, bf16[2,8,4,128,128]{4,3,2,1,0:T(8,128)(2,1)}, u32[]{:S(2)}) copy-start(bf16[2,8,4,128,128]{4,3,2,1,0:T(8,128)(2,1)} %param.9) | copy-start | bytes 6291460
  3.3 8.9 %collective-permute-start = (bf16[2,1,17,128]{3,2,1,0:T(8,128)(2,1)S(1)}, bf16[2,1,17,128]{3,2,1,0:T(8,128)(2,1)S(1)}, u32[]{:S(2)}, u32[]{:S(2)}) collective-permute-start(bf16[2,1,17,128]{3,2,1,0:T(8,128)(2,1)S(1)} %get-tuple-element.27), channel_id=1, source_target_pairs={{1,2},{2,1},{5,6},{6,5},{9,10},{10,9},{13,14},{14,13},{17,18},{18,... | collective-permute-start | bytes 26120 | tf_op jit(solution)/shard_map/ppermute | solution.py:24
  4.0 8.2 %collective-permute-start.1 = (bf16[2,1,17,128]{3,2,1,0:T(8,128)(2,1)S(1)}, bf16[2,1,17,128]{3,2,1,0:T(8,128)(2,1)S(1)}, u32[]{:S(2)}, u32[]{:S(2)}) collective-permute-start(bf16[2,1,17,128]{3,2,1,0:T(8,128)(2,1)S(1)} %get-tuple-element.28), channel_id=1, source_target_pairs={{0,1},{2,3},{1,0},{3,2},{4,5},{6,7},{5,4},{7,6},{8,9},{10,11},{9,8... | collective-permute-start | bytes 26120 | tf_op jit(solution)/shard_map/ppermute | solution.py:23
  12.3 5.2 %collective-permute-start.2 = (bf16[1,10,17,128]{3,2,1,0:T(8,128)(2,1)S(1)}, bf16[1,10,17,128]{3,2,1,0:T(8,128)(2,1)S(1)}, u32[]{:S(2)}, u32[]{:S(2)}) collective-permute-start(bf16[1,10,17,128]{3,2,1,0:T(8,128)(2,1)S(1)} %get-tuple-element.25), channel_id=1, source_target_pairs={{0,4},{8,12},{16,20},{24,28},{32,36},{40,44},{48,52},{56,60},{64,6... | collective-permute-start | bytes 130568 | tf_op jit(solution)/shard_map/ppermute | solution.py:23
  13.6 5.5 %collective-permute-start.3 = (bf16[1,10,17,128]{3,2,1,0:T(8,128)(2,1)S(1)}, bf16[1,10,17,128]{3,2,1,0:T(8,128)(2,1)S(1)}, u32[]{:S(2)}, u32[]{:S(2)}) collective-permute-start(bf16[1,10,17,128]{3,2,1,0:T(8,128)(2,1)S(1)} %get-tuple-element.26), channel_id=1, source_target_pairs={{4,8},{12,16},{20,24},{28,32},{36,40},{44,48},{52,56},{60,64},{68,... | collective-permute-start | bytes 130568 | tf_op jit(solution)/shard_map/ppermute | solution.py:24
  20.0 1.0 %copy-start.1 = (f32[2,8,16,128]{3,2,1,0:T(8,128)S(1)}, f32[2,8,16,128]{3,2,1,0:T(8,128)}, u32[]{:S(2)}) copy-start(f32[2,8,16,128]{3,2,1,0:T(8,128)} %param.8) | copy-start | bytes 393220
  21.0 2.6 %collective-permute-start.4 = (bf16[2,1,16,128]{3,2,1,0:T(8,128)(2,1)S(1)}, bf16[2,1,16,128]{3,2,1,0:T(8,128)(2,1)S(1)}, u32[]{:S(2)}, u32[]{:S(2)}) collective-permute-start(bf16[2,1,16,128]{3,2,1,0:T(8,128)(2,1)S(1)} %get-tuple-element.51), channel_id=1, source_target_pairs={{1,2},{2,1},{5,6},{6,5},{9,10},{10,9},{13,14},{14,13},{17,18},{18,... | collective-permute-start | bytes 24584 | tf_op jit(solution)/shard_map/ppermute | solution.py:24
  21.7 3.0 %collective-permute-start.5 = (bf16[2,1,16,128]{3,2,1,0:T(8,128)(2,1)S(1)}, bf16[2,1,16,128]{3,2,1,0:T(8,128)(2,1)S(1)}, u32[]{:S(2)}, u32[]{:S(2)}) collective-permute-start(bf16[2,1,16,128]{3,2,1,0:T(8,128)(2,1)S(1)} %get-tuple-element.52), channel_id=1, source_target_pairs={{0,1},{2,3},{1,0},{3,2},{4,5},{6,7},{5,4},{7,6},{8,9},{10,11},{9,8... | collective-permute-start | bytes 24584 | tf_op jit(solution)/shard_map/ppermute | solution.py:23
  24.7 4.2 %collective-permute-start.6 = (bf16[1,10,16,128]{3,2,1,0:T(8,128)(2,1)S(1)}, bf16[1,10,16,128]{3,2,1,0:T(8,128)(2,1)S(1)}, u32[]{:S(2)}, u32[]{:S(2)}) collective-permute-start(bf16[1,10,16,128]{3,2,1,0:T(8,128)(2,1)S(1)} %get-tuple-element.45), channel_id=1, source_target_pairs={{0,4},{8,12},{16,20},{24,28},{32,36},{40,44},{48,52},{56,60},{64,6... | collective-permute-start | bytes 122888 | tf_op jit(solution)/shard_map/ppermute | solution.py:23
  24.8 5.8 %collective-permute-start.7 = (bf16[1,10,16,128]{3,2,1,0:T(8,128)(2,1)S(1)}, bf16[1,10,16,128]{3,2,1,0:T(8,128)(2,1)S(1)}, u32[]{:S(2)}, u32[]{:S(2)}) collective-permute-start(bf16[1,10,16,128]{3,2,1,0:T(8,128)(2,1)S(1)} %get-tuple-element.46), channel_id=1, source_target_pairs={{4,8},{12,16},{20,24},{28,32},{36,40},{44,48},{52,56},{60,64},{68,... | collective-permute-start | bytes 122888 | tf_op jit(solution)/shard_map/ppermute | solution.py:24
  32.4 5.4 %collective-permute-start.8 = (bf16[2,1,16,128]{3,2,1,0:T(8,128)(2,1)S(1)}, bf16[2,1,16,128]{3,2,1,0:T(8,128)(2,1)S(1)}, u32[]{:S(2)}, u32[]{:S(2)}) collective-permute-start(bf16[2,1,16,128]{3,2,1,0:T(8,128)(2,1)S(1)} %get-tuple-element.49), channel_id=1, source_target_pairs={{1,2},{2,1},{5,6},{6,5},{9,10},{10,9},{13,14},{14,13},{17,18},{18,... | collective-permute-start | bytes 24584 | tf_op jit(solution)/shard_map/ppermute | solution.py:24
  33.0 5.7 %collective-permute-start.9 = (bf16[2,1,16,128]{3,2,1,0:T(8,128)(2,1)S(1)}, bf16[2,1,16,128]{3,2,1,0:T(8,128)(2,1)S(1)}, u32[]{:S(2)}, u32[]{:S(2)}) collective-permute-start(bf16[2,1,16,128]{3,2,1,0:T(8,128)(2,1)S(1)} %get-tuple-element.50), channel_id=1, source_target_pairs={{0,1},{2,3},{1,0},{3,2},{4,5},{6,7},{5,4},{7,6},{8,9},{10,11},{9,8... | collective-permute-start | bytes 24584 | tf_op jit(solution)/shard_map/ppermute | solution.py:23
  38.8 4.9 %collective-permute-start.10 = (bf16[1,10,16,128]{3,2,1,0:T(8,128)(2,1)S(1)}, bf16[1,10,16,128]{3,2,1,0:T(8,128)(2,1)S(1)}, u32[]{:S(2)}, u32[]{:S(2)}) collective-permute-start(bf16[1,10,16,128]{3,2,1,0:T(8,128)(2,1)S(1)} %get-tuple-element.39), channel_id=1, source_target_pairs={{0,4},{8,12},{16,20},{24,28},{32,36},{40,44},{48,52},{56,60},{64,6... | collective-permute-start | bytes 122888 | tf_op jit(solution)/shard_map/ppermute | solution.py:23
  38.9 6.5 %collective-permute-start.11 = (bf16[1,10,16,128]{3,2,1,0:T(8,128)(2,1)S(1)}, bf16[1,10,16,128]{3,2,1,0:T(8,128)(2,1)S(1)}, u32[]{:S(2)}, u32[]{:S(2)}) collective-permute-start(bf16[1,10,16,128]{3,2,1,0:T(8,128)(2,1)S(1)} %get-tuple-element.40), channel_id=1, source_target_pairs={{4,8},{12,16},{20,24},{28,32},{36,40},{44,48},{52,56},{60,64},{68,... | collective-permute-start | bytes 122888 | tf_op jit(solution)/shard_map/ppermute | solution.py:24
  46.2 10.5 %copy-start.2 = (f32[6,5]{1,0:T(8,128)S(1)}, f32[6,5]{1,0:T(8,128)}, u32[]{:S(2)}) copy-start(f32[6,5]{1,0:T(8,128)} %param.14) | copy-start | bytes 364
  47.2 3.8 %collective-permute-start.12 = (bf16[2,1,16,128]{3,2,1,0:T(8,128)(2,1)S(1)}, bf16[2,1,16,128]{3,2,1,0:T(8,128)(2,1)S(1)}, u32[]{:S(2)}, u32[]{:S(2)}) collective-permute-start(bf16[2,1,16,128]{3,2,1,0:T(8,128)(2,1)S(1)} %get-tuple-element.47), channel_id=1, source_target_pairs={{1,2},{2,1},{5,6},{6,5},{9,10},{10,9},{13,14},{14,13},{17,18},{18,... | collective-permute-start | bytes 24584 | tf_op jit(solution)/shard_map/ppermute | solution.py:24
  47.9 4.1 %collective-permute-start.13 = (bf16[2,1,16,128]{3,2,1,0:T(8,128)(2,1)S(1)}, bf16[2,1,16,128]{3,2,1,0:T(8,128)(2,1)S(1)}, u32[]{:S(2)}, u32[]{:S(2)}) collective-permute-start(bf16[2,1,16,128]{3,2,1,0:T(8,128)(2,1)S(1)} %get-tuple-element.48), channel_id=1, source_target_pairs={{0,1},{2,3},{1,0},{3,2},{4,5},{6,7},{5,4},{7,6},{8,9},{10,11},{9,8... | collective-permute-start | bytes 24584 | tf_op jit(solution)/shard_map/ppermute | solution.py:23
  52.0 4.9 %collective-permute-start.14 = (bf16[1,10,16,128]{3,2,1,0:T(8,128)(2,1)S(1)}, bf16[1,10,16,128]{3,2,1,0:T(8,128)(2,1)S(1)}, u32[]{:S(2)}, u32[]{:S(2)}) collective-permute-start(bf16[1,10,16,128]{3,2,1,0:T(8,128)(2,1)S(1)} %get-tuple-element.33), channel_id=1, source_target_pairs={{0,4},{8,12},{16,20},{24,28},{32,36},{40,44},{48,52},{56,60},{64,6... | collective-permute-start | bytes 122888 | tf_op jit(solution)/shard_map/ppermute | solution.py:23
  52.1 6.3 %collective-permute-start.15 = (bf16[1,10,16,128]{3,2,1,0:T(8,128)(2,1)S(1)}, bf16[1,10,16,128]{3,2,1,0:T(8,128)(2,1)S(1)}, u32[]{:S(2)}, u32[]{:S(2)}) collective-permute-start(bf16[1,10,16,128]{3,2,1,0:T(8,128)(2,1)S(1)} %get-tuple-element.34), channel_id=1, source_target_pairs={{4,8},{12,16},{20,24},{28,32},{36,40},{44,48},{52,56},{60,64},{68,... | collective-permute-start | bytes 122888 | tf_op jit(solution)/shard_map/ppermute | solution.py:24

commit v2 on v0

v2 whole, which is shorter than its diff:
```python
import jax
import jax.numpy as jnp
from jax import lax
from jax.experimental import pallas as pl
from jax.experimental.pallas import tpu as pltpu
from jax.sharding import Mesh
from jax.sharding import PartitionSpec as P

GX_GY = ("gx_0", "gx_1", "gx_2", "gy")
GX = ("gx_0", "gx_1", "gx_2")
F32 = jnp.float32
BF16 = jnp.bfloat16
EDGE = 32
ROWS, COLS = 2, 8
WIDE = COLS + 4
SPOTS = (ROWS + 4) * WIDE
ZERO = 2 * SPOTS
SLOTS = 4
HI, INFO, PACK, LONG = 128, 144, 160, 176
LIVE, BOUND, DIR, BOUND2, BOUND3, BOUND4 = 0, 1, 2, 6, 7, 8
VMEM = pl.BlockSpec(memory_space=pltpu.VMEM)
SMEM = pl.BlockSpec(memory_space=pltpu.SMEM)
ANY = pl.BlockSpec(memory_space=pl.ANY)


def params(mib):
    return pltpu.CompilerParams(vmem_limit_bytes=mib * 1024 * 1024)


def cost(flops):
    return pl.CostEstimate(flops=flops, bytes_accessed=1 << 20, transcendentals=0)


def spot(row, col):
    return (row + 2) * WIDE + (col + 2)


def lanes():
    return lax.broadcasted_iota(jnp.int32, (16, 128), 1)


def below(count):
    return (lanes() < count).astype(F32)


def split(value):
    high = value.astype(BF16)
    return high, value - high.astype(F32)


def info_of(rows):
    index = lax.broadcasted_iota(jnp.int32, (16, 128), 0)
    info = jnp.zeros((16, 128), F32)
    for row, value in rows.items():
        info = jnp.where(index == row, value, info)
    return info.astype(BF16)


def odd_z():
    return lax.axis_index("gy") % 2


def odd_core():
    return lax.axis_index("gx_2")


def merge(parts):
    lane = lanes()
    merged = parts[0]
    for index, part in enumerate(parts[1:], 1):
        merged = jnp.where(lane < EDGE * index, merged, pltpu.roll(part, EDGE * index, 1))
    return jnp.where(lane < EDGE * len(parts), merged, 0.0)


def piece(pack, index):
    moved = pltpu.roll(pack, 128 - EDGE * index, 1) if index else pack
    return jnp.where(lanes() < EDGE, moved, 0.0)


def block_message(out, at, refs, row, col, row2, col2):
    signals, dirs, masks, live, bound = refs
    value = signals[row, col] * below(live[row, col])
    high, low = split(value)
    second = signals[row2, col2] * below(bound[row2, col2])
    rows = {LIVE: below(live[row, col]), BOUND: below(bound[row, col]), BOUND2: below(bound[row2, col2])}
    for slot in range(SLOTS):
        used = jnp.where(masks[row, col, slot] == 1, dirs[row, col, slot], 9)
        rows[DIR + slot] = jnp.full((16, 128), used.astype(F32))
    out[at, HI:INFO] = high
    out[at, INFO:PACK] = info_of(rows)
    out[at, PACK:LONG] = merge([low, second]).astype(BF16)


def pack_z(tiles, signals, dirs, masks, live, bound, out_a, out_b, sem):
    refs = (signals, dirs, masks, live, bound)
    odd = odd_z()
    copies = []
    for which, out in enumerate((out_a, out_b)):
        right = odd == which
        col = jnp.where(right, COLS - 1, 0)
        for slot in range(SLOTS):
            copies.append(
                pltpu.make_async_copy(
                    tiles.at[:, col, slot, 0:EDGE, :], out.at[:, EDGE * slot : EDGE * (slot + 1), :], sem.at[which, slot]
                )
            )
            copies[-1].start()
    for which, out in enumerate((out_a, out_b)):
        right = odd == which
        col, col2 = jnp.where(right, COLS - 1, 0), jnp.where(right, COLS - 2, 1)
        for row in range(ROWS):
            block_message(out, row, refs, row, col, row, col2)
    for copy in copies:
        copy.wait()


def pack_x(tiles, signals, dirs, masks, live, bound, out_s, out_b, sem):
    refs = (signals, dirs, masks, live, bound)
    core = odd_core()
    copies = []
    for which, out in enumerate((out_s, out_b)):
        row = jnp.where(core == which, 1, 0)
        for slot in range(SLOTS):
            copies.append(
                pltpu.make_async_copy(
                    tiles.at[row, :, slot, 0:EDGE, :],
                    out.at[1 : 1 + COLS, EDGE * slot : EDGE * (slot + 1), :],
                    sem.at[which, slot],
                )
            )
            copies[-1].start()
    for which, out in enumerate((out_s, out_b)):
        row = jnp.where(core == which, 1, 0)
        for col in range(COLS):
            block_message(out, 1 + col, refs, row, col, 1 - row, col)
        for at in (0, COLS + 1):
            out[at] = jnp.zeros((LONG, 128), BF16)
    for copy in copies:
        copy.wait()


def corners_1(from_a, from_b, in_s, in_b, out_s, out_b, room, sem):
    del in_s, in_b
    odd, core = odd_z(), odd_core()
    copies = []
    for side, halo in enumerate((from_a, from_b)):
        at = jnp.where(odd == side, COLS + 1, 0)
        for which, out in enumerate((out_s, out_b)):
            row = jnp.where(core == which, 1, 0)
            first, other = halo[row].astype(F32), halo[1 - row].astype(F32)
            info, info2 = first[INFO:PACK], other[INFO:PACK]
            index = lax.broadcasted_iota(jnp.int32, (16, 128), 0)
            for place, source in (
                (BOUND2, info2[BOUND : BOUND + 1]),
                (BOUND3, info[BOUND2 : BOUND2 + 1]),
                (BOUND4, info2[BOUND2 : BOUND2 + 1]),
            ):
                info = jnp.where(index == place, source, info)
            own2 = other[HI:INFO] * info2[BOUND : BOUND + 1]
            pack = merge([first[PACK:LONG], own2, piece(first[PACK:LONG], 1), piece(other[PACK:LONG], 1)])
            room[which, side, 0:INFO] = halo[row, 0:INFO]
            room[which, side, INFO:PACK] = info.astype(BF16)
            room[which, side, PACK:LONG] = pack.astype(BF16)
            copies.append(pltpu.make_async_copy(room.at[which, side], out.at[at], sem.at[which, side]))
    for copy in copies:
        copy.start()
    for copy in copies:
        copy.wait()


def corners_2(bounds_a, bounds_b, from_a, from_b, in_s, in_b, out_s, out_b, room, sem):
    del in_s, in_b
    odd, core = odd_z(), odd_core()
    copies = []
    for side, (halo, bounds) in enumerate(((from_a, bounds_a), (from_b, bounds_b))):
        at = jnp.where(odd == side, COLS + 1, 0)
        for which, out in enumerate((out_s, out_b)):
            row = jnp.where(core == which, 1, 0)
            first, other = halo[row].astype(F32), halo[1 - row].astype(F32)
            info2 = bounds[1 - row, INFO:PACK].astype(F32)
            own2 = other[0:16] * info2[BOUND : BOUND + 1]
            pack = merge([first[16:32], own2, piece(first[16:32], 1), piece(other[16:32], 1)])
            room[which, side, 0:16] = halo[row, 0:16]
            room[which, side, 16:32] = pack.astype(BF16)
            copies.append(pltpu.make_async_copy(room.at[which, side], out.at[at], sem.at[which, side]))
    for copy in copies:
        copy.start()
    for copy in copies:
        copy.wait()


def product(inputs, weights):
    total = None
    for first in range(0, SLOTS, 2):
        term = lax.dot_general(
            jnp.concatenate(inputs[first : first + 2], axis=1),
            jnp.concatenate(weights[first : first + 2], axis=1),
            (((1,), (1,)), ((), ())),
            preferred_element_type=F32,
        )
        total = term if total is None else total + term
    return total


def ghost_blocks(from_a, from_b, from_s, from_x):
    odd, core = odd_z(), odd_core()
    found = []
    for side, halo in enumerate((from_a, from_b)):
        col = jnp.where(odd == side, COLS, -1)
        found += [(halo, row, row, col) for row in range(ROWS)]
    for which, halo in enumerate((from_s, from_x)):
        row = jnp.where(core == which, ROWS, -1)
        found += [(halo, at, row, at - 1) for at in range(COLS + 2)]
    return found


def wide(value):
    return jnp.concatenate([value, jnp.zeros((value.shape[0], 128 - value.shape[1]), value.dtype)], axis=1)


def ghost_product(halo, at, place, room, height):
    info = halo[at, INFO:PACK].astype(F32)
    offsets = [(d // 3 - 1) * WIDE + d % 3 - 1 for d in range(9)]
    inputs = []
    near = [room[place + offsets[d] + (SPOTS if d == 4 else 0)] for d in range(9)]
    for slot in range(SLOTS):
        turn = jnp.broadcast_to(info[DIR + slot : DIR + slot + 1], (16, 128)).astype(BF16)
        halves = []
        for half in range(0, height, 16):
            chosen = jnp.zeros((16, 128), BF16)
            for d in range(9):
                chosen = jnp.where(turn == d, near[d][half : half + 16], chosen)
            halves.append(chosen)
        inputs.append(halves[0] if height == 16 else jnp.concatenate(halves, axis=0))
    weights = [halo[at, EDGE * slot : EDGE * (slot + 1)] for slot in range(SLOTS)]
    return wide(product(inputs, weights))


def own_product(tiles, index, row, col, room):
    inputs = [room[index[row, col, slot]] for slot in range(SLOTS)]
    return product(inputs, [tiles[row, col, slot] for slot in range(SLOTS)])


def place_own(room, row, col, value, bound):
    at = spot(row, col)
    room[SPOTS + at, 0:16] = value.astype(BF16)
    room[at, 0:16] = (value * below(bound[row, col])).astype(BF16)


def message_2(out, at, value, bound, row, col, row2, col2):
    high, low = split(value[row, col])
    second = value[row2, col2] * below(bound[row2, col2])
    out[at, 0:16] = high
    out[at, 16:32] = merge([low, second]).astype(BF16)


def steps_12(
    tiles, signals, index, live, bound, spectral, from_a, from_b, from_s, from_x,
    degree, first_out, second_out, ghost_degree, ghost_first, out_a, out_b, out_s, out_x, room, room2,
):
    factor = 2.0 / jnp.full((16, 128), spectral[0])
    odd, core = odd_z(), odd_core()
    lane = lanes()
    head = lax.broadcasted_iota(jnp.int32, (16, 128), 0) == 0
    room[ZERO] = jnp.zeros((32, 128), BF16)
    room2[ZERO] = jnp.zeros((16, 128), BF16)

    def put_own(at, high, info):
        room[SPOTS + at, 0:16] = high
        room[SPOTS + at, 16:32] = info
        inside = info[BOUND : BOUND + 1].astype(F32)
        room[at, 0:16] = (high.astype(F32) * inside).astype(BF16)
        room[at, 16:32] = (info.astype(F32) * inside).astype(BF16)

    def put_far(at, pack, place, inside):
        room[at, 0:16] = piece(pack, place).astype(BF16)
        room[at, 16:32] = jnp.where(head, inside, 0.0).astype(BF16)

    for row in range(ROWS):
        for col in range(COLS):
            at = spot(row, col)
            alive, inside = below(live[row, col]), below(bound[row, col])
            value = signals[row, col] * alive
            place_own(room, row, col, value, bound)
            room[SPOTS + at, 16:32] = jnp.where(head, alive, 0.0).astype(BF16)
            room[at, 16:32] = jnp.where(head, inside, 0.0).astype(BF16)
    for side, halo in enumerate((from_a, from_b)):
        right = odd == side
        col, far = jnp.where(right, COLS, -1), jnp.where(right, COLS + 1, -2)
        for row in range(ROWS):
            info = halo[row, INFO:PACK]
            put_own(spot(row, col), halo[row, HI:INFO], info)
            pack = halo[row, PACK:LONG].astype(F32)
            put_far(spot(row, far), pack, 1, info[BOUND2 : BOUND2 + 1].astype(F32))
    for which, halo in enumerate((from_s, from_x)):
        down = core == which
        row, far = jnp.where(down, ROWS, -1), jnp.where(down, ROWS + 1, -2)
        for k in range(COLS + 2):
            info = halo[k, INFO:PACK]
            put_own(spot(row, k - 1), halo[k, HI:INFO], info)
            info = info.astype(F32)
            pack = halo[k, PACK:LONG].astype(F32)
            put_far(spot(far, k - 1), pack, 1, info[BOUND2 : BOUND2 + 1])
            if k in (0, COLS + 1):
                col = -2 if k == 0 else COLS + 1
                put_far(spot(row, col), pack, 2, info[BOUND3 : BOUND3 + 1])
                put_far(spot(far, col), pack, 3, info[BOUND4 : BOUND4 + 1])

    for number, (halo, at, row, col) in enumerate(ghost_blocks(from_a, from_b, from_s, from_x)):
        place = spot(row, col)
        sums = ghost_product(halo, at, place, room, 32)
        value = halo[at, HI:INFO].astype(F32) + piece(halo[at, PACK:LONG].astype(F32), 0)
        around = jnp.broadcast_to(sums[16:17], (16, 128))
        result = factor * (around * value - sums[0:16]) - value
        ghost_degree[number] = around
        ghost_first[number] = result
        inside = halo[at, INFO:PACK].astype(F32)[BOUND : BOUND + 1]
        room2[place] = jnp.where(lane < EDGE, result * inside, 0.0).astype(BF16)

    for row in range(ROWS):
        for col in range(COLS):
            sums = own_product(tiles, index, row, col, room)
            alive = below(live[row, col])
            value = signals[row, col] * alive
            around = jnp.broadcast_to(sums[16:17], (16, 128)) * alive
            result = factor * (around * value - sums[0:16] * alive) - value
            degree[row, col] = around
            first_out[row, col] = result
            place_own(room2, row, col, result, bound)

    for row in range(ROWS):
        for col in range(COLS):
            sums = own_product(tiles, index, row, col, room2)
            alive = below(live[row, col])
            value = first_out[row, col]
            result = 2.0 * (factor * (degree[row, col] * value - sums * alive) - value)
            second_out[row, col] = result - signals[row, col] * alive

    for side, out in enumerate((out_a, out_b)):
        right = odd == side
        col, col2 = jnp.where(right, COLS - 1, 0), jnp.where(right, COLS - 2, 1)
        for row in range(ROWS):
            message_2(out, row, second_out, bound, row, col, row, col2)
    for which, out in enumerate((out_s, out_x)):
        row = jnp.where(core == which, 1, 0)
        for col in range(COLS):
            message_2(out, 1 + col, second_out, bound, row, col, 1 - row, col)
        for at in (0, COLS + 1):
            out[at] = jnp.zeros((32, 128), BF16)


def steps_34(
    tiles, signals, index, live, bound, spectral, scales, from_a, from_b, from_s, from_x,
    degree, first, second, ghost_degree, ghost_first, new_a, new_b, new_s, new_x,
    coefficients, partial, room, room2, third,
):
    factor = 2.0 / jnp.full((16, 128), spectral[0])
    odd, core = odd_z(), odd_core()
    lane = lanes()
    room[ZERO] = jnp.zeros((16, 128), BF16)
    room2[ZERO] = jnp.zeros((16, 128), BF16)

    def put_own(at, high, info):
        room[SPOTS + at] = high
        room[at] = (high.astype(F32) * info.astype(F32)[BOUND : BOUND + 1]).astype(BF16)

    def put_far(at, pack, place):
        room[at] = piece(pack, place).astype(BF16)

    for row in range(ROWS):
        for col in range(COLS):
            place_own(room, row, col, second[row, col], bound)
    for side, (halo, old) in enumerate(((new_a, from_a), (new_b, from_b))):
        right = odd == side
        col, far = jnp.where(right, COLS, -1), jnp.where(right, COLS + 1, -2)
        for row in range(ROWS):
            put_own(spot(row, col), halo[row, 0:16], old[row, INFO:PACK])
            put_far(spot(row, far), halo[row, 16:32].astype(F32), 1)
    for which, (halo, old) in enumerate(((new_s, from_s), (new_x, from_x))):
        down = core == which
        row, far = jnp.where(down, ROWS, -1), jnp.where(down, ROWS + 1, -2)
        for k in range(COLS + 2):
            put_own(spot(row, k - 1), halo[k, 0:16], old[k, INFO:PACK])
            pack = halo[k, 16:32].astype(F32)
            put_far(spot(far, k - 1), pack, 1)
            if k in (0, COLS + 1):
                col = -2 if k == 0 else COLS + 1
                put_far(spot(row, col), pack, 2)
                put_far(spot(far, col), pack, 3)

    values = ghost_blocks(new_a, new_b, new_s, new_x)
    for number, (halo, at, row, col) in enumerate(ghost_blocks(from_a, from_b, from_s, from_x)):
        place = spot(row, col)
        sums = ghost_product(halo, at, place, room, 16)
        fresh = values[number][0]
        value = fresh[at, 0:16].astype(F32) + piece(fresh[at, 16:32].astype(F32), 0)
        result = 2.0 * (factor * (ghost_degree[number] * value - sums) - value) - ghost_first[number]
        inside = halo[at, INFO:PACK].astype(F32)[BOUND : BOUND + 1]
        room2[place] = jnp.where(lane < EDGE, result * inside, 0.0).astype(BF16)

    for row in range(ROWS):
        for col in range(COLS):
            sums = own_product(tiles, index, row, col, room)
            alive = below(live[row, col])
            value = second[row, col]
            result = 2.0 * (factor * (degree[row, col] * value - sums * alive) - value) - first[row, col]
            third[row, col] = result
            place_own(room2, row, col, result, bound)

    count = scales.shape[0]
    squares = [jnp.zeros((16, 128), F32) for _ in range(count)]
    for row in range(ROWS):
        for col in range(COLS):
            sums = own_product(tiles, index, row, col, room2)
            alive = below(live[row, col])
            value = third[row, col]
            fourth = 2.0 * (factor * (degree[row, col] * value - sums * alive) - value) - second[row, col]
            terms = (signals[row, col] * alive, first[row, col], second[row, col], value, fourth)
            for scale in range(count):
                total = (0.5 * scales[scale, 0]) * terms[0]
                for order in range(1, len(terms)):
                    total = total + scales[scale, order] * terms[order]
                coefficients[scale, row, col] = total
                squares[scale] = squares[scale] + total * total
    block = jnp.concatenate(squares + [jnp.zeros((128 - 16 * count, 128), F32)], axis=0)
    line = jnp.sum(jnp.transpose(block), axis=0, keepdims=True)
    partial[...] = jnp.broadcast_to(line[None], partial.shape)


def neighbour_pairs(devices, first):
    pairs = [(i, i + 1) for i in range(first, devices - 1, 2)]
    return pairs + [(j, i) for i, j in pairs]


def shape(dims, kind=BF16):
    return jax.ShapeDtypeStruct(dims, kind)


def shards(signals, tiles, tile_dir, tile_mask, live_rows, bound_rows, scale_coeffs, spectral_bound):
    devices_x, devices_z = lax.axis_size(GX), lax.axis_size("gy")
    devices = devices_x * devices_z
    scales, channels = scale_coeffs.shape[0], signals.shape[2]
    nodes = ROWS * COLS * 128 * devices

    def swap_z(a, b):
        return (
            lax.ppermute(a, "gy", neighbour_pairs(devices_z, 0)),
            lax.ppermute(b, "gy", neighbour_pairs(devices_z, 1)),
        )

    def swap_x(s, x):
        far = lax.ppermute(x, GX, neighbour_pairs(devices_x, 1))
        return lax.ppermute(s, "gx_2", [(0, 1), (1, 0)]), far

    base = spot(
        lax.broadcasted_iota(jnp.int32, tile_dir.shape, 0), lax.broadcasted_iota(jnp.int32, tile_dir.shape, 1)
    )
    moved = base + (tile_dir // 3 - 1) * WIDE + tile_dir % 3 - 1
    index = jnp.where(tile_dir == 4, SPOTS + base, moved)
    index = jnp.where(tile_mask == 1, index, ZERO)

    local = (tiles, signals, tile_dir, tile_mask, live_rows, bound_rows)
    local_specs = [ANY, VMEM] + [SMEM] * 4
    message_z, message_x = shape((ROWS, LONG, 128)), shape((COLS + 2, LONG, 128))
    a, b = pl.pallas_call(
        pack_z,
        out_shape=[message_z] * 2,
        in_specs=local_specs,
        out_specs=[VMEM] * 2,
        scratch_shapes=[pltpu.SemaphoreType.DMA((2, SLOTS))],
        compiler_params=params(8),
        cost_estimate=cost(1000),
        name="pack_z",
    )(*local)
    s, x = pl.pallas_call(
        pack_x,
        out_shape=[message_x] * 2,
        in_specs=local_specs,
        out_specs=[VMEM] * 2,
        scratch_shapes=[pltpu.SemaphoreType.DMA((2, SLOTS))],
        compiler_params=params(8),
        cost_estimate=cost(2000000),
        name="pack_x",
    )(*local)
    a, b = swap_z(a, b)
    s, x = pl.pallas_call(
        corners_1,
        out_shape=[message_x] * 2,
        in_specs=[VMEM] * 2 + [ANY] * 2,
        out_specs=[ANY] * 2,
        scratch_shapes=[pltpu.VMEM((2, 2, LONG, 128), BF16), pltpu.SemaphoreType.DMA((2, 2))],
        input_output_aliases={2: 0, 3: 1},
        compiler_params=params(8),
        cost_estimate=cost(1000),
        name="corners_1",
    )(a, b, s, x)
    s, x = swap_x(s, x)

    ghosts = 2 * ROWS + 2 * (COLS + 2)
    field = shape((ROWS, COLS, channels, 128), F32)
    extra = shape((ghosts, channels, 128), F32)
    short_z, short_x = shape((ROWS, 32, 128)), shape((COLS + 2, 32, 128))
    state = pl.pallas_call(
        steps_12,
        out_shape=[field] * 3 + [extra] * 2 + [short_z] * 2 + [short_x] * 2,
        in_specs=[VMEM] * 2 + [SMEM] * 4 + [VMEM] * 4,
        out_specs=[VMEM] * 9,
        scratch_shapes=[pltpu.VMEM((ZERO + 1, 32, 128), BF16), pltpu.VMEM((ZERO + 1, 16, 128), BF16)],
        compiler_params=params(24),
        cost_estimate=cost(1 << 27),
        name="steps_12",
    )(tiles, signals, index, live_rows, bound_rows, spectral_bound, a, b, s, x)
    degree, first, second, ghost_degree, ghost_first, a2, b2, s2, x2 = state
    a2, b2 = swap_z(a2, b2)
    s2, x2 = pl.pallas_call(
        corners_2,
        out_shape=[short_x] * 2,
        in_specs=[VMEM] * 4 + [ANY] * 2,
        out_specs=[ANY] * 2,
        scratch_shapes=[pltpu.VMEM((2, 2, 32, 128), BF16), pltpu.SemaphoreType.DMA((2, 2))],
        input_output_aliases={4: 0, 5: 1},
        compiler_params=params(8),
        cost_estimate=cost(1000),
        name="corners_2",
    )(a, b, a2, b2, s2, x2)
    s2, x2 = swap_x(s2, x2)
    totals, partial = pl.pallas_call(
        steps_34,
        out_shape=[shape((scales, ROWS, COLS, channels, 128), F32), shape((devices, 1, 128), F32)],
        in_specs=[VMEM] * 2 + [SMEM] * 5 + [VMEM] * 13,
        out_specs=[VMEM] * 2,
        scratch_shapes=[
            pltpu.VMEM((ZERO + 1, 16, 128), BF16),
            pltpu.VMEM((ZERO + 1, 16, 128), BF16),
            pltpu.VMEM((ROWS, COLS, channels, 128), F32),
        ],
        compiler_params=params(24),
        cost_estimate=cost(1 << 27),
        name="steps_34",
    )(
        tiles, signals, index, live_rows, bound_rows, spectral_bound, scale_coeffs, a, b, s, x,
        degree, first, second, ghost_degree, ghost_first, a2, b2, s2, x2,
    )
    gathered = lax.all_to_all(partial, GX_GY, 0, 0)
    energy = jnp.sum(gathered, axis=(0, 1))[: scales * channels].reshape(scales, channels) / nodes
    return (totals, energy)


def solution(mesh):
    torus = Mesh(mesh.devices.reshape(4, 4, 2, mesh.shape["gy"]), ("gx_0", "gx_1", "gx_2", "gy"))
    placed = (
        P(GX, "gy", None, None),
        P(GX, "gy", None, None, None),
        P(GX, "gy", None),
        P(GX, "gy", None),
        P(GX, "gy"),
        P(GX, "gy"),
        P(),
        P(),
    )
    return jax.shard_map(
        shards,
        mesh=torus,
        in_specs=placed,
        out_specs=(P(None, GX, "gy", None, None), P()),
        check_vma=False,
    )
```

time: 115 us -> 68.8 us (0.60); the launches traced: 113 us -> 68.5 us
  starting transfers between devices: 44.7 us -> 17.4 us
  blocking collectives: 39 us -> 25 us
  other arithmetic: 11.6 us -> 0.24 us
  Pallas kernels: 0 us -> 9.39 us
  local copies, waits for them, and re-layouts: 0.2 us -> 6.09 us
  waiting for transfers between devices: 13.1 us -> 8.85 us
  matrix products: 2.6 us -> 0 us
    psum x4 -> x0, blocking collectives: 39 us -> none  [over_axes(): array = lax.psum(array, axis)]
    ppermute x16 -> x8, starting transfers between devices: 44.7 us -> 17.4 us  [the longest x2 7.94 us: swap_z(): lax.ppermute(a, 'gy', neighbour_pairs(devices_z, 0))]
    all_to_all x0 -> x1, blocking collectives: none -> 25 us  [shards(): gathered = lax.all_to_all(partial, GX_GY, 0, 0)]
    pallas_call x0 -> x6, Pallas kernels: none -> 9.39 us  [the longest x1 3.44 us: shards(): pl.pallas_call(steps_34, out_shape=[shape((scales, ROWS, COLS, channels,...]
    unnamed x27 -> x20, local copies, waits for them, and re-layouts: 0.16 us -> 5.42 us
    ppermute x16 -> x8, waiting for transfers between devices: 13.1 us -> 8.85 us  [the longest x2 7.94 us: swap_x(): far = lax.ppermute(x, GX, neighbour_pairs(devices_x, 1))]
    select_n x16 -> x1, other arithmetic: 3.91 us -> 0.08 us  [shards(): index = jnp.where(tile_mask == 1, index, ZERO)]
    dot_general x4 -> x0, matrix products: 2.6 us -> none  [adjacency(): lax.dot_general(flat_inputs, flat_tiles, (((1, 3), (1, 3)), ((0,), (0,)))...]
  transfers between devices with their start and end apart: 16 -> 8, of which waited for: 8 -> 4; matrix products, arithmetic and copies ran while one was open for 3% -> 0% of each run, Pallas kernels for 0% -> 2%
where the time goes in v2:
time: 68.8 us; the launch traced here: 68.5 us
  blocking collectives  25 us (36%)
  starting transfers between devices  17.4 us (25%)
  Pallas kernels  9.39 us (14%)
  waiting for transfers between devices  8.85 us (13%)
  local copies, waits for them, and re-layouts  6.09 us (9%)
  between operations  1.44 us (2%)
    all_to_all x1, blocking collectives, shards(): gathered = lax.all_to_all(partial, GX_GY, 0, 0)  25 us
    ppermute x2, waiting for transfers between devices, swap_x(): far = lax.ppermute(x, GX, neighbour_pairs(devices_x, 1))  7.94 us
    ppermute x2, starting transfers between devices, swap_z(): lax.ppermute(a, 'gy', neighbour_pairs(devices_z, 0))  7.94 us
    ppermute x2, starting transfers between devices, swap_x(): far = lax.ppermute(x, GX, neighbour_pairs(devices_x, 1))  6.79 us
    unnamed x20, local copies, waits for them, and re-layouts  5.42 us
    pallas_call x1, Pallas kernels, shards(): pl.pallas_call(steps_34, out_shape=[shape((scales, ROWS, COLS, channels,...  3.44 us
    pallas_call x1, Pallas kernels, shards(): pl.pallas_call(steps_12, out_shape=[field] * 3 + [extra] * 2 + [short_z]...  2.95 us
    ppermute x2, starting transfers between devices, swap_x(): return (lax.ppermute(s, 'gx_2', [(0, 1), (1, 0)]), far)  1.42 us
  transfers between devices with their start and end apart: 8, of which 4 were waited for; matrix products, arithmetic and copies ran while one was open for 0% of the time, Pallas kernels for 2%

profile of v2, /device:TPU:1, one launch (start us, length us, event | category | flops | bytes accessed | tf_op | source)
XLA Modules:
  0.0 68.5 jit_solution(14091245758776238795)
XLA Ops:
  0.6 0.8 %copy.15.dirs = s32[2,8,4]{2,1,0:T(8,128)S(1)} copy(s32[2,8,4]{1,2,0:T(4,128)} %param.10) | data formatting | bytes 512 | tf_op args[2]
  1.4 0.8 %copy.14.masks = s32[2,8,4]{2,1,0:T(8,128)S(1)} copy(s32[2,8,4]{1,2,0:T(4,128)} %param.11) | data formatting | bytes 512 | tf_op args[3]
  2.2 1.6 %copy-done = bf16[2,8,4,128,128]{4,3,2,1,0:T(8,128)(2,1)S(1)} copy-done((bf16[2,8,4,128,128]{4,3,2,1,0:T(8,128)(2,1)S(1)}, bf16[2,8,4,128,128]{4,3,2,1,0:T(8,128)(2,1)}, u32[]{:S(2)}) %copy-start) | copy-done | bytes 2097176
  3.8 0.9 %copy-done.2 = f32[2,8,16,128]{3,2,1,0:T(8,128)S(1)} copy-done((f32[2,8,16,128]{3,2,1,0:T(8,128)S(1)}, f32[2,8,16,128]{3,2,1,0:T(8,128)}, u32[]{:S(2)}) %copy-start.2) | copy-done | bytes 131096
  4.7 0.7 copy-done.4
  5.3 0.7 copy-done.6
  6.0 1.1 %pack_z.1 = (bf16[2,176,128]{2,1,0:T(8,128)(2,1)S(1)}, bf16[2,176,128]{2,1,0:T(8,128)(2,1)S(1)}) custom-call(bf16[2,8,4,128,128]{4,3,2,1,0:T(8,128)(2,1)S(1)} %copy-done, f32[2,8,16,128]{3,2,1,0:T(8,128)S(1)} %copy-done.2, s32[2,8,4]{2,1,0:T(8,128)S(1)} %copy.15.dirs, s32[2,8,4]{2,1,0:T(8,128)S(1)} %copy.14.masks, s32[2,8]{1,0:T(2,128)S(1)} %copy-done.4, ...), custom_call_target="tpu_custom_call" | custom-call | flops 1000 | bytes 1048576 | tf_op jit(solution)/shard_map/pack_z/pallas_call | solution.py:465
  7.2 2.5 %collective-permute-start = (bf16[2,176,128]{2,1,0:T(8,128)(2,1)S(1)}, bf16[2,176,128]{2,1,0:T(8,128)(2,1)S(1)}, u32[]{:S(2)}, u32[]{:S(2)}) collective-permute-start(bf16[2,176,128]{2,1,0:T(8,128)(2,1)S(1)} %get-tuple-element.21), channel_id=1, source_target_pairs={{0,1},{2,3},{1,0},{3,2},{4,5},{6,7},{5,4},{7,6},{8,9},{10,11},{9,8... | collective-permute-start | bytes 270344 | tf_op jit(solution)/shard_map/ppermute | solution.py:447
  9.7 0.7 collective-permute-start.1
  10.4 1.2 %pack_x.1 = (bf16[10,176,128]{2,1,0:T(8,128)(2,1)S(1)}, bf16[10,176,128]{2,1,0:T(8,128)(2,1)S(1)}) custom-call(bf16[2,8,4,128,128]{4,3,2,1,0:T(8,128)(2,1)S(1)} %copy-done, f32[2,8,16,128]{3,2,1,0:T(8,128)S(1)} %copy-done.2, s32[2,8,4]{2,1,0:T(8,128)S(1)} %copy.15.dirs, s32[2,8,4]{2,1,0:T(8,128)S(1)} %copy.14.masks, s32[2,8]{1,0:T(2,128)S(1)} %copy-done.4, ...), custom_call_target="tpu_custom_call" | custom-call | flops 2000000 | bytes 1048576 | tf_op jit(solution)/shard_map/pack_x/pallas_call | solution.py:475
  11.6 0.4 collective-permute-done.from_a.bounds_a
  12.1 0.4 corners_1.1
  12.5 1.3 %collective-permute-start.2 = (bf16[10,176,128]{2,1,0:T(8,128)(2,1)S(1)}, bf16[10,176,128]{2,1,0:T(8,128)(2,1)S(1)}, u32[]{:S(2)}, u32[]{:S(2)}) collective-permute-start(bf16[10,176,128]{2,1,0:T(8,128)(2,1)S(1)} %get-tuple-element.25), channel_id=1, source_target_pairs={{0,4},{4,0},{1,5},{5,1},{2,6},{6,2},{3,7},{7,3},{8,12},{12,8},{9,1... | collective-permute-start | bytes 1351688 | tf_op jit(solution)/shard_map/ppermute | solution.py:453
  13.8 3.1 %collective-permute-start.3 = (bf16[10,176,128]{2,1,0:T(8,128)(2,1)S(1)}, bf16[10,176,128]{2,1,0:T(8,128)(2,1)S(1)}, u32[]{:S(2)}, u32[]{:S(2)}) collective-permute-start(bf16[10,176,128]{2,1,0:T(8,128)(2,1)S(1)} %get-tuple-element.26), channel_id=1, source_target_pairs={{4,8},{12,16},{20,24},{28,32},{36,40},{44,48},{52,56},{60,64},{68,... | collective-permute-start | bytes 1351688 | tf_op jit(solution)/shard_map/ppermute | solution.py:452
  17.7 5.8 %collective-permute-done.3.from_x = bf16[10,176,128]{2,1,0:T(8,128)(2,1)S(1)} collective-permute-done((bf16[10,176,128]{2,1,0:T(8,128)(2,1)S(1)}, bf16[10,176,128]{2,1,0:T(8,128)(2,1)S(1)}, u32[]{:S(2)}, u32[]{:S(2)}) %collective-permute-start.3) | collective-permute-done | bytes 450592 | tf_op jit(solution)/shard_map/ppermute | solution.py:452
  23.6 2.9 %steps_12.1 = (f32[2,8,16,128]{3,2,1,0:T(8,128)S(1)}, f32[2,8,16,128]{3,2,1,0:T(8,128)S(1)}, f32[2,8,16,128]{3,2,1,0:T(8,128)S(1)}, f32[24,16,128]{2,1,0:T(8,128...) custom-call(bf16[2,8,4,128,128]{4,3,2,1,0:T(8,128)(2,1)S(1)} %copy-d, ...), custom_call_target="tpu_custom_call" | custom-call | flops 134217728 | bytes 1048576 | tf_op jit(solution)/shard_map/steps_12/pallas_call | solution.py:503
  26.5 5.4 %collective-permute-start.4 = (bf16[2,32,128]{2,1,0:T(8,128)(2,1)S(1)}, bf16[2,32,128]{2,1,0:T(8,128)(2,1)S(1)}, u32[]{:S(2)}, u32[]{:S(2)}) collective-permute-start(bf16[2,32,128]{2,1,0:T(8,128)(2,1)S(1)} %get-tuple-element.32), channel_id=1, source_target_pairs={{0,1},{2,3},{1,0},{3,2},{4,5},{6,7},{5,4},{7,6},{8,9},{10,11},{9,8... | collective-permute-start | bytes 49160 | tf_op jit(solution)/shard_map/ppermute | solution.py:447
  31.9 0.7 collective-permute-start.5
  32.6 0.5 collective-permute-done.4.from_a.new_a
  33.4 3.7 %collective-permute-start.7 = (bf16[10,32,128]{2,1,0:T(8,128)(2,1)S(1)}, bf16[10,32,128]{2,1,0:T(8,128)(2,1)S(1)}, u32[]{:S(2)}, u32[]{:S(2)}) collective-permute-start(bf16[10,32,128]{2,1,0:T(8,128)(2,1)S(1)} %get-tuple-element.37), channel_id=1, source_target_pairs={{4,8},{12,16},{20,24},{28,32},{36,40},{44,48},{52,56},{60,64},{68,... | collective-permute-start | bytes 245768 | tf_op jit(solution)/shard_map/ppermute | solution.py:452
  37.1 2.1 %collective-permute-done.7.new_x = bf16[10,32,128]{2,1,0:T(8,128)(2,1)S(1)} collective-permute-done((bf16[10,32,128]{2,1,0:T(8,128)(2,1)S(1)}, bf16[10,32,128]{2,1,0:T(8,128)(2,1)S(1)}, u32[]{:S(2)}, u32[]{:S(2)}) %collective-permute-start.7) | collective-permute-done | bytes 81952 | tf_op jit(solution)/shard_map/ppermute | solution.py:452
  39.2 3.4 %steps_34.1 = (f32[6,2,8,16,128]{4,3,2,1,0:T(8,128)}, f32[128,1,128]{2,1,0:T(1,128)S(1)}) custom-call(bf16[2,8,4,128,128]{4,3,2,1,0:T(8,128)(2,1)S(1)} %copy-done.1, f32[2,8,16,128]{3,2,1,0:T(8,128)S(1)} %copy-done.3, s32[2,8,4]{2,1,0:T(8,128)S(1)} %fusion.1.index, s32[2,8]{1,0:T(2,128)S(1)} %copy-done.5, s32[2,8]{1,0:T(2,128)S(1)} %copy-done.7, ...), custom_call_target="tpu_custom_call" | custom-call | flops 134217728 | bytes 1048576 | tf_op jit(solution)/shard_map/steps_34/pallas_call | solution.py:527
  42.6 25.0 %all_to_all.5 = f32[128,1,128]{2,1,0:T(1,128)S(1)} all-to-all(f32[128,1,128]{2,1,0:T(1,128)S(1)} %get-tuple-element.39), channel_id=1, replica_groups=mesh['gx_0'=4,'gx_1'=4,'gx_2'=2,'gy'=4] {'gx_0','gx_1','gx_2','gy'}, dimensions={0} | all-to-all | bytes 131072 | tf_op jit(solution)/shard_map/all_to_all | solution.py:544
  67.8 0.7 div.17
  (25 shorter events, 0.6 us)
Async XLA Ops:
  2.2 1.6 %copy-start = (bf16[2,8,4,128,128]{4,3,2,1,0:T(8,128)(2,1)S(1)}, bf16[2,8,4,128,128]{4,3,2,1,0:T(8,128)(2,1)}, u32[]{:S(2)}) copy-start(bf16[2,8,4,128,128]{4,3,2,1,0:T(8,128)(2,1)} %tiles.7) | copy-start | bytes 6291460
  3.8 0.9 %copy-start.2 = (f32[2,8,16,128]{3,2,1,0:T(8,128)S(1)}, f32[2,8,16,128]{3,2,1,0:T(8,128)}, u32[]{:S(2)}) copy-start(f32[2,8,16,128]{3,2,1,0:T(8,128)} %signals.7) | copy-start | bytes 393220
  4.7 0.7 copy-start.4
  5.3 0.7 copy-start.6
  7.2 16.4 %copy-start.1 = (bf16[2,8,4,128,128]{4,3,2,1,0:T(8,128)(2,1)S(1)}, bf16[2,8,4,128,128]{4,3,2,1,0:T(8,128)(2,1)}, u32[]{:S(2)}) copy-start(bf16[2,8,4,128,128]{4,3,2,1,0:T(8,128)(2,1)} %tiles.7) | copy-start | bytes 6291460
  7.2 16.4 %copy-start.3 = (f32[2,8,16,128]{3,2,1,0:T(8,128)S(1)}, f32[2,8,16,128]{3,2,1,0:T(8,128)}, u32[]{:S(2)}) copy-start(f32[2,8,16,128]{3,2,1,0:T(8,128)} %signals.7) | copy-start | bytes 393220
  7.2 16.4 %copy-start.5 = (s32[2,8]{1,0:T(2,128)S(1)}, s32[2,8]{1,0:T(2,128)}, u32[]{:S(2)}) copy-start(s32[2,8]{1,0:T(2,128)} %live.7) | copy-start | bytes 196
  7.2 16.4 %copy-start.7 = (s32[2,8]{1,0:T(2,128)S(1)}, s32[2,8]{1,0:T(2,128)}, u32[]{:S(2)}) copy-start(s32[2,8]{1,0:T(2,128)} %bound.7) | copy-start | bytes 196
  7.2 4.9 %collective-permute-start = (bf16[2,176,128]{2,1,0:T(8,128)(2,1)S(1)}, bf16[2,176,128]{2,1,0:T(8,128)(2,1)S(1)}, u32[]{:S(2)}, u32[]{:S(2)}) collective-permute-start(bf16[2,176,128]{2,1,0:T(8,128)(2,1)S(1)} %get-tuple-element.21), channel_id=1, source_target_pairs={{0,1},{2,3},{1,0},{3,2},{4,5},{6,7},{5,4},{7,6},{8,9},{10,11},{9,8... | collective-permute-start | bytes 270344 | tf_op jit(solution)/shard_map/ppermute | solution.py:447
  9.7 2.3 %collective-permute-start.1 = (bf16[2,176,128]{2,1,0:T(8,128)(2,1)S(1)}, bf16[2,176,128]{2,1,0:T(8,128)(2,1)S(1)}, u32[]{:S(2)}, u32[]{:S(2)}) collective-permute-start(bf16[2,176,128]{2,1,0:T(8,128)(2,1)S(1)} %get-tuple-element.22), channel_id=1, source_target_pairs={{1,2},{2,1},{5,6},{6,5},{9,10},{10,9},{13,14},{14,13},{17,18},{18,... | collective-permute-start | bytes 270344 | tf_op jit(solution)/shard_map/ppermute | solution.py:448
  12.5 26.7 %copy-start.8 = (f32[6,5]{1,0:T(8,128)S(1)}, f32[6,5]{1,0:T(8,128)}, u32[]{:S(2)}) copy-start(f32[6,5]{1,0:T(8,128)} %scales.1) | copy-start | bytes 364
  12.5 5.2 %collective-permute-start.2 = (bf16[10,176,128]{2,1,0:T(8,128)(2,1)S(1)}, bf16[10,176,128]{2,1,0:T(8,128)(2,1)S(1)}, u32[]{:S(2)}, u32[]{:S(2)}) collective-permute-start(bf16[10,176,128]{2,1,0:T(8,128)(2,1)S(1)} %get-tuple-element.25), channel_id=1, source_target_pairs={{0,4},{4,0},{1,5},{5,1},{2,6},{6,2},{3,7},{7,3},{8,12},{12,8},{9,1... | collective-permute-start | bytes 1351688 | tf_op jit(solution)/shard_map/ppermute | solution.py:453
  13.8 9.7 %collective-permute-start.3 = (bf16[10,176,128]{2,1,0:T(8,128)(2,1)S(1)}, bf16[10,176,128]{2,1,0:T(8,128)(2,1)S(1)}, u32[]{:S(2)}, u32[]{:S(2)}) collective-permute-start(bf16[10,176,128]{2,1,0:T(8,128)(2,1)S(1)} %get-tuple-element.26), channel_id=1, source_target_pairs={{4,8},{12,16},{20,24},{28,32},{36,40},{44,48},{52,56},{60,64},{68,... | collective-permute-start | bytes 1351688 | tf_op jit(solution)/shard_map/ppermute | solution.py:452
  26.5 6.5 %collective-permute-start.4 = (bf16[2,32,128]{2,1,0:T(8,128)(2,1)S(1)}, bf16[2,32,128]{2,1,0:T(8,128)(2,1)S(1)}, u32[]{:S(2)}, u32[]{:S(2)}) collective-permute-start(bf16[2,32,128]{2,1,0:T(8,128)(2,1)S(1)} %get-tuple-element.32), channel_id=1, source_target_pairs={{0,1},{2,3},{1,0},{3,2},{4,5},{6,7},{5,4},{7,6},{8,9},{10,11},{9,8... | collective-permute-start | bytes 49160 | tf_op jit(solution)/shard_map/ppermute | solution.py:447
  31.9 1.1 %collective-permute-start.5 = (bf16[2,32,128]{2,1,0:T(8,128)(2,1)S(1)}, bf16[2,32,128]{2,1,0:T(8,128)(2,1)S(1)}, u32[]{:S(2)}, u32[]{:S(2)}) collective-permute-start(bf16[2,32,128]{2,1,0:T(8,128)(2,1)S(1)} %get-tuple-element.33), channel_id=1, source_target_pairs={{1,2},{2,1},{5,6},{6,5},{9,10},{10,9},{13,14},{14,13},{17,18},{18,... | collective-permute-start | bytes 49160 | tf_op jit(solution)/shard_map/ppermute | solution.py:448
  33.3 3.8 %collective-permute-start.6 = (bf16[10,32,128]{2,1,0:T(8,128)(2,1)S(1)}, bf16[10,32,128]{2,1,0:T(8,128)(2,1)S(1)}, u32[]{:S(2)}, u32[]{:S(2)}) collective-permute-start(bf16[10,32,128]{2,1,0:T(8,128)(2,1)S(1)} %get-tuple-element.36), channel_id=1, source_target_pairs={{0,4},{4,0},{1,5},{5,1},{2,6},{6,2},{3,7},{7,3},{8,12},{12,8},{9,1... | collective-permute-start | bytes 245768 | tf_op jit(solution)/shard_map/ppermute | solution.py:453
  33.4 5.8 %collective-permute-start.7 = (bf16[10,32,128]{2,1,0:T(8,128)(2,1)S(1)}, bf16[10,32,128]{2,1,0:T(8,128)(2,1)S(1)}, u32[]{:S(2)}, u32[]{:S(2)}) collective-permute-start(bf16[10,32,128]{2,1,0:T(8,128)(2,1)S(1)} %get-tuple-element.37), channel_id=1, source_target_pairs={{4,8},{12,16},{20,24},{28,32},{36,40},{44,48},{52,56},{60,64},{68,... | collective-permute-start | bytes 245768 | tf_op jit(solution)/shard_map/ppermute | solution.py:452

commit v3 on v2

v3 whole, which is shorter than its diff:
```python
import jax
import jax.numpy as jnp
from jax import lax
from jax.experimental import pallas as pl
from jax.experimental.pallas import tpu as pltpu
from jax.sharding import Mesh
from jax.sharding import PartitionSpec as P

GX_GY = ("gx_0", "gx_1", "gx_2", "gy")
GX = ("gx_0", "gx_1", "gx_2")
F32 = jnp.float32
BF16 = jnp.bfloat16
EDGE = 32
ROWS, COLS = 2, 8
WIDE = COLS + 4
SPOTS = (ROWS + 4) * WIDE
ZERO = 2 * SPOTS
SLOTS = 4
HI, INFO, PACK, LONG = 128, 144, 160, 176
LIVE, BOUND, DIR, BOUND2, BOUND3, BOUND4 = 0, 1, 2, 6, 7, 8
VMEM = pl.BlockSpec(memory_space=pltpu.VMEM)
SMEM = pl.BlockSpec(memory_space=pltpu.SMEM)
ANY = pl.BlockSpec(memory_space=pl.ANY)
HBM = pl.BlockSpec(memory_space=pltpu.MemorySpace.HBM)


def params(mib):
    return pltpu.CompilerParams(vmem_limit_bytes=mib * 1024 * 1024)


def cost(flops):
    return pl.CostEstimate(flops=flops, bytes_accessed=1 << 20, transcendentals=0)


def lanes():
    return lax.broadcasted_iota(jnp.int32, (16, 128), 1)


def below(count):
    return (lanes() < count).astype(F32)


def split(value):
    high = value.astype(BF16)
    return high, value - high.astype(F32)


def info_of(rows):
    index = lax.broadcasted_iota(jnp.int32, (16, 128), 0)
    info = jnp.zeros((16, 128), F32)
    for row, value in rows.items():
        info = jnp.where(index == row, value, info)
    return info.astype(BF16)


def odd_z():
    return lax.axis_index("gy") % 2


def odd_core():
    return lax.axis_index("gx_2")


def merge(parts):
    lane = lanes()
    merged = parts[0]
    for index, part in enumerate(parts[1:], 1):
        merged = jnp.where(lane < EDGE * index, merged, pltpu.roll(part, EDGE * index, 1))
    return jnp.where(lane < EDGE * len(parts), merged, 0.0)


def piece(pack, index):
    moved = pltpu.roll(pack, 128 - EDGE * index, 1) if index else pack
    return jnp.where(lanes() < EDGE, moved, 0.0)


def block_message(out, at, refs, row, col, row2, col2):
    signals, dirs, masks, live, bound = refs
    value = signals[row, col] * below(live[row, col])
    high, low = split(value)
    second = signals[row2, col2] * below(bound[row2, col2])
    rows = {LIVE: below(live[row, col]), BOUND: below(bound[row, col]), BOUND2: below(bound[row2, col2])}
    for slot in range(SLOTS):
        used = jnp.where(masks[row, slot, col] == 1, dirs[row, slot, col], 9)
        rows[DIR + slot] = jnp.full((16, 128), used.astype(F32))
    out[at, HI:INFO] = high
    out[at, INFO:PACK] = info_of(rows)
    out[at, PACK:LONG] = merge([low, second]).astype(BF16)


def fetch(refs, rooms, sems):
    copies = [pltpu.make_async_copy(ref, room, sems.at[i]) for i, (ref, room) in enumerate(zip(refs, rooms))]
    for copy in copies:
        copy.start()
    return copies


def pack_z(tiles, signals, dirs, masks, live, bound, out_a, out_b, signals_v, dirs_s, masks_s, live_s, bound_s, sem, sem2):
    refs = (signals_v, dirs_s, masks_s, live_s, bound_s)
    copies = fetch((signals, dirs, masks, live, bound), refs, sem2)
    odd = odd_z()
    later = []
    for which, out in enumerate((out_a, out_b)):
        right = odd == which
        col = jnp.where(right, COLS - 1, 0)
        for slot in range(SLOTS):
            later.append(
                pltpu.make_async_copy(
                    tiles.at[:, col, slot, 0:EDGE, :], out.at[:, EDGE * slot : EDGE * (slot + 1), :], sem.at[which, slot]
                )
            )
            later[-1].start()
    for copy in copies:
        copy.wait()
    for which, out in enumerate((out_a, out_b)):
        right = odd == which
        col, col2 = jnp.where(right, COLS - 1, 0), jnp.where(right, COLS - 2, 1)
        for row in range(ROWS):
            block_message(out, row, refs, row, col, row, col2)
    for copy in later:
        copy.wait()


def pack_x(tiles, signals, dirs, masks, live, bound, out_s, out_b, table, signals_v, dirs_s, masks_s, live_s, bound_s, sem, sem2):
    refs = (signals_v, dirs_s, masks_s, live_s, bound_s)
    copies = fetch((signals, dirs, masks, live, bound), refs, sem2)
    core = odd_core()
    later = []
    for which, out in enumerate((out_s, out_b)):
        row = jnp.where(core == which, 1, 0)
        for slot in range(SLOTS):
            later.append(
                pltpu.make_async_copy(
                    tiles.at[row, :, slot, 0:EDGE, :],
                    out.at[1 : 1 + COLS, EDGE * slot : EDGE * (slot + 1), :],
                    sem.at[which, slot],
                )
            )
            later[-1].start()
    for copy in copies:
        copy.wait()
    for which, out in enumerate((out_s, out_b)):
        row = jnp.where(core == which, 1, 0)
        for col in range(COLS):
            block_message(out, 1 + col, refs, row, col, 1 - row, col)
    odd = odd_z()
    down, right = (2 * core - 1) * WIDE, 1 - 2 * odd
    for row in range(ROWS):
        for col in range(COLS):
            base = place(jnp.where(core == row, 3, 2), jnp.where(odd == 1, COLS - 1 - col, col))
            for slot in range(SLOTS):
                side = dirs_s[row, slot, col]
                step = jnp.where(side > 5, 1, jnp.where(side > 2, 0, -1))
                index = base + step * down + (side - 3 * step - 4) * right
                index = jnp.where(side == 4, SPOTS + base, index)
                table[row, slot, col] = jnp.where(masks_s[row, slot, col] == 1, index, ZERO)
            table[row, SLOTS, col] = live_s[row, col]
            table[row, SLOTS + 1, col] = bound_s[row, col]
        for at in (0, COLS + 1):
            out[at] = jnp.zeros((LONG, 128), BF16)
    for copy in later:
        copy.wait()


def corners_1(from_a, from_b, in_s, in_b, out_s, out_b, room, sem):
    del in_s, in_b
    odd, core = odd_z(), odd_core()
    copies = []
    for side, halo in enumerate((from_a, from_b)):
        at = jnp.where(odd == side, COLS + 1, 0)
        for which, out in enumerate((out_s, out_b)):
            row = jnp.where(core == which, 1, 0)
            first, other = halo[row].astype(F32), halo[1 - row].astype(F32)
            info, info2 = first[INFO:PACK], other[INFO:PACK]
            index = lax.broadcasted_iota(jnp.int32, (16, 128), 0)
            for place, source in (
                (BOUND2, info2[BOUND : BOUND + 1]),
                (BOUND3, info[BOUND2 : BOUND2 + 1]),
                (BOUND4, info2[BOUND2 : BOUND2 + 1]),
            ):
                info = jnp.where(index == place, source, info)
            own2 = other[HI:INFO] * info2[BOUND : BOUND + 1]
            pack = merge([first[PACK:LONG], own2, piece(first[PACK:LONG], 1), piece(other[PACK:LONG], 1)])
            room[which, side, 0:INFO] = halo[row, 0:INFO]
            room[which, side, INFO:PACK] = info.astype(BF16)
            room[which, side, PACK:LONG] = pack.astype(BF16)
            copies.append(pltpu.make_async_copy(room.at[which, side], out.at[at], sem.at[which, side]))
    for copy in copies:
        copy.start()
    for copy in copies:
        copy.wait()


def corners_2(bounds_a, bounds_b, from_a, from_b, in_s, in_b, out_s, out_b, room, sem):
    del in_s, in_b
    odd, core = odd_z(), odd_core()
    copies = []
    for side, (halo, bounds) in enumerate(((from_a, bounds_a), (from_b, bounds_b))):
        at = jnp.where(odd == side, COLS + 1, 0)
        for which, out in enumerate((out_s, out_b)):
            row = jnp.where(core == which, 1, 0)
            first, other = halo[row].astype(F32), halo[1 - row].astype(F32)
            info2 = bounds[1 - row, INFO:PACK].astype(F32)
            own2 = other[0:16] * info2[BOUND : BOUND + 1]
            pack = merge([first[16:32], own2, piece(first[16:32], 1), piece(other[16:32], 1)])
            room[which, side, 0:16] = halo[row, 0:16]
            room[which, side, 16:32] = pack.astype(BF16)
            copies.append(pltpu.make_async_copy(room.at[which, side], out.at[at], sem.at[which, side]))
    for copy in copies:
        copy.start()
    for copy in copies:
        copy.wait()


def place(u, v):
    return u * WIDE + v + 2


class Frame:
    def __init__(self):
        self.odd, self.core = odd_z(), odd_core()
        self.up = 2 * self.core - 1
        self.right = 1 - 2 * self.odd

    def row(self, u):
        return 1 - self.core if u == 2 else self.core

    def col(self, v):
        return jnp.where(self.odd == 1, COLS - 1 - v, v)


def product(inputs, weights):
    total = None
    for first in range(0, SLOTS, 2):
        term = lax.dot_general(
            jnp.concatenate(inputs[first : first + 2], axis=1),
            jnp.concatenate(weights[first : first + 2], axis=1),
            (((1,), (1,)), ((), ())),
            preferred_element_type=F32,
        )
        total = term if total is None else total + term
    return total


def ghost_blocks(frame, u, halo_a, halo_b, halo_x):
    row = frame.row(u)
    found = [(halo_a, row, u, COLS), (halo_b, row, u, -1)]
    return found + [(halo_x, frame.col(v) + 1, 1 if u == 2 else 4, v) for v in range(-1, COLS + 1)]


def wide(value):
    return jnp.concatenate([value, jnp.zeros((value.shape[0], 128 - value.shape[1]), value.dtype)], axis=1)


def ghost_product(frame, halo, at, spot_at, room, height):
    info = halo[at, INFO:PACK].astype(F32)
    step = jnp.where(info > 5.5, 1.0, jnp.where(info > 2.5, 0.0, -1.0))
    turned = 3.0 * (frame.up.astype(F32) * step) + frame.right.astype(F32) * (info - 3.0 * step - 4.0) + 4.0
    turned = jnp.where(info > 8.5, 9.0, turned)
    offsets = [(d // 3 - 1) * WIDE + d % 3 - 1 for d in range(9)]
    near = [room[spot_at + offsets[d] + (SPOTS if d == 4 else 0)] for d in range(9)]
    inputs = []
    for slot in range(SLOTS):
        turn = jnp.broadcast_to(turned[DIR + slot : DIR + slot + 1], (16, 128)).astype(BF16)
        halves = []
        for half in range(0, height, 16):
            chosen = jnp.zeros((16, 128), BF16)
            for d in range(9):
                chosen = jnp.where(turn == d, near[d][half : half + 16], chosen)
            halves.append(chosen)
        inputs.append(halves[0] if height == 16 else jnp.concatenate(halves, axis=0))
    weights = [halo[at, EDGE * slot : EDGE * (slot + 1)] for slot in range(SLOTS)]
    return wide(product(inputs, weights))


def own_product(tiles, table, row, col, room):
    inputs = [room[table[row, slot, col]] for slot in range(SLOTS)]
    return jnp.dot(jnp.concatenate(inputs, axis=1), tiles[row, col], preferred_element_type=F32)


def alive_of(table, row, col):
    return below(table[row, SLOTS, col])


def inside_of(table, row, col):
    return below(table[row, SLOTS + 1, col])


def place_own(room, table, row, col, at, value):
    room[SPOTS + at, 0:16] = value.astype(BF16)
    room[at, 0:16] = (value * inside_of(table, row, col)).astype(BF16)


def bound_row(halo, at):
    return halo[at, INFO:PACK].astype(F32)[BOUND : BOUND + 1]


def message_2(out, at, value, table, col, u, v, u2, v2, col2, row2):
    high, low = split(value[u - 2, v])
    second = value[u2 - 2, v2] * inside_of(table, row2, col2)
    out[at, 0:16] = high
    out[at, 16:32] = merge([low, second]).astype(BF16)


def turn_tiles(tiles, out):
    def one(block, carry):
        row, col = block // COLS, block % COLS
        for slot in range(SLOTS):
            out[row, col, 128 * slot : 128 * (slot + 1)] = jnp.transpose(tiles[row, col, slot])
        return carry

    lax.fori_loop(0, ROWS * COLS, one, 0)


def heads():
    return lax.broadcasted_iota(jnp.int32, (16, 128), 0) == 0


def fill_1(room, halo, at, near, far, corner):
    high, info = halo[at, HI:INFO], halo[at, INFO:PACK]
    rows, pack = info.astype(F32), halo[at, PACK:LONG].astype(F32)
    inside = rows[BOUND : BOUND + 1]
    room[SPOTS + near, 0:16] = high
    room[SPOTS + near, 16:32] = info
    room[near, 0:16] = (high.astype(F32) * inside).astype(BF16)
    room[near, 16:32] = (rows * inside).astype(BF16)
    for index, (spot_at, line) in enumerate(zip((far,) + corner, (BOUND2, BOUND3, BOUND4)), 1):
        room[spot_at, 0:16] = piece(pack, index).astype(BF16)
        room[spot_at, 16:32] = jnp.where(heads(), rows[line : line + 1], 0.0).astype(BF16)


def fill_2(room, halo, old, at, near, far, corner):
    high, pack = halo[at, 0:16], halo[at, 16:32].astype(F32)
    room[SPOTS + near] = high
    room[near] = (high.astype(F32) * bound_row(old, at)).astype(BF16)
    for index, spot_at in enumerate((far,) + corner, 1):
        room[spot_at] = piece(pack, index).astype(BF16)


def fill_z(fill, frame, room, halos):
    for halo, near, far in ((halos[0], COLS, COLS + 1), (halos[1], -1, -2)):
        for u in (2, 3):
            fill(room, *halo, frame.row(u), place(u, near), place(u, far), ())


def fill_x(fill, frame, room, halo, near, far):
    for v in range(-1, COLS + 1):
        beyond = {-1: -2, COLS: COLS + 1}.get(v)
        corner = () if beyond is None else (place(near, beyond), place(far, beyond))
        fill(room, *halo, frame.col(v) + 1, place(near, v), place(far, v), corner)


def half_1(frame, u, tiles, signals, table, factor, halos, room, room2, degree, first, ghost_degree, ghost_first):
    lane = lanes()
    for number, (halo, at, gu, gv) in enumerate(ghost_blocks(frame, u, *halos)):
        sums = ghost_product(frame, halo, at, place(gu, gv), room, 32)
        value = halo[at, HI:INFO].astype(F32) + piece(halo[at, PACK:LONG].astype(F32), 0)
        around = jnp.broadcast_to(sums[16:17], (16, 128))
        result = factor * (around * value - sums[0:16]) - value
        ghost_degree[number] = around
        ghost_first[number] = result
        room2[place(gu, gv)] = jnp.where(lane < EDGE, result * bound_row(halo, at), 0.0).astype(BF16)
    row = frame.row(u)
    for v in range(COLS):
        col = frame.col(v)
        sums = own_product(tiles, table, row, col, room)
        alive = alive_of(table, row, col)
        value = signals[row, col] * alive
        around = jnp.broadcast_to(sums[16:17], (16, 128)) * alive
        result = factor * (around * value - sums[0:16] * alive) - value
        degree[v] = around
        first[v] = result
        place_own(room2, table, row, col, place(u, v), result)


def half_3(frame, u, tiles, table, factor, halos, fresh, room, room2, degree, first, second, third, ghost_degree, ghost_first):
    lane = lanes()
    values = ghost_blocks(frame, u, *fresh)
    for number, (halo, at, gu, gv) in enumerate(ghost_blocks(frame, u, *halos)):
        sums = ghost_product(frame, halo, at, place(gu, gv), room, 16)
        new = values[number][0]
        value = new[at, 0:16].astype(F32) + piece(new[at, 16:32].astype(F32), 0)
        result = 2.0 * (factor * (ghost_degree[number] * value - sums) - value) - ghost_first[number]
        room2[place(gu, gv)] = jnp.where(lane < EDGE, result * bound_row(halo, at), 0.0).astype(BF16)
    row = frame.row(u)
    for v in range(COLS):
        col = frame.col(v)
        sums = own_product(tiles, table, row, col, room)
        value = second[u - 2, v]
        result = 2.0 * (factor * (degree[v] * value - sums * alive_of(table, row, col)) - value) - first[v]
        third[v] = result
        place_own(room2, table, row, col, place(u, v), result)


def carry_rooms(room, room_in, room2, room2_in):
    for u in (2, 3):
        for v in range(-2, COLS + 2):
            room[place(u, v)] = room_in[place(u, v)]
            room[SPOTS + place(u, v)] = room_in[SPOTS + place(u, v)]
    for v in range(-1, COLS + 1):
        room2[place(1, v)] = room2_in[place(1, v)]
        room2[place(2, v)] = room2_in[place(2, v)]
        if 0 <= v < COLS:
            room2[SPOTS + place(2, v)] = room2_in[SPOTS + place(2, v)]


def step_1a(
    tiles, signals, table, spectral, from_a, from_b, from_s, room, room2, degree, first, ghost_degree, ghost_first
):
    frame = Frame()
    factor = 2.0 / jnp.full((16, 128), spectral[0])
    room[ZERO] = jnp.zeros((32, 128), BF16)
    for u in (2, 3):
        row = frame.row(u)
        for v in range(COLS):
            col, at = frame.col(v), place(u, v)
            alive = alive_of(table, row, col)
            place_own(room, table, row, col, at, signals[row, col] * alive)
            room[SPOTS + at, 16:32] = jnp.where(heads(), alive, 0.0).astype(BF16)
            room[at, 16:32] = jnp.where(heads(), inside_of(table, row, col), 0.0).astype(BF16)
    fill_z(fill_1, frame, room, ((from_a,), (from_b,)))
    fill_x(fill_1, frame, room, (from_s,), 1, 0)
    halos = (from_a, from_b, from_s)
    half_1(frame, 2, tiles, signals, table, factor, halos, room, room2, degree, first, ghost_degree, ghost_first)


def step_1b(
    tiles, signals, table, spectral, from_a, from_b, from_x, room_in, room2_in, degree_a, first_a,
    degree, first, ghost_degree, ghost_first, second, out_a, out_b, room, room2,
):
    frame = Frame()
    factor = 2.0 / jnp.full((16, 128), spectral[0])
    room[ZERO] = jnp.zeros((32, 128), BF16)
    room2[ZERO] = jnp.zeros((16, 128), BF16)
    carry_rooms(room, room_in, room2, room2_in)
    fill_x(fill_1, frame, room, (from_x,), 4, 5)
    halos = (from_a, from_b, from_x)
    half_1(frame, 3, tiles, signals, table, factor, halos, room, room2, degree, first, ghost_degree, ghost_first)
    for u, degrees, firsts in ((2, degree_a, first_a), (3, degree, first)):
        row = frame.row(u)
        for v in range(COLS):
            col = frame.col(v)
            sums = own_product(tiles, table, row, col, room2)
            alive = alive_of(table, row, col)
            value = firsts[v]
            result = 2.0 * (factor * (degrees[v] * value - sums * alive) - value)
            second[u - 2, v] = result - signals[row, col] * alive
    for out, v, v2 in ((out_a, COLS - 1, COLS - 2), (out_b, 0, 1)):
        for u in (2, 3):
            row = frame.row(u)
            message_2(out, row, second, table, frame.col(v), u, v, u, v2, frame.col(v2), row)


def pack_x2(second, table, out_s, out_x):
    frame = Frame()
    for out, u in ((out_s, 2), (out_x, 3)):
        row = frame.row(u)
        for v in range(COLS):
            col = frame.col(v)
            message_2(out, col + 1, second, table, col, u, v, 5 - u, v, col, 1 - row)
        for at in (0, COLS + 1):
            out[at] = jnp.zeros((32, 128), BF16)


def step_3a(
    tiles, table, spectral, from_a, from_b, from_s, new_a, new_b, new_s,
    degree, first, second, ghost_degree, ghost_first, room, room2, third,
):
    frame = Frame()
    factor = 2.0 / jnp.full((16, 128), spectral[0])
    room[ZERO] = jnp.zeros((16, 128), BF16)
    for u in (2, 3):
        row = frame.row(u)
        for v in range(COLS):
            place_own(room, table, row, frame.col(v), place(u, v), second[u - 2, v])
    fill_z(fill_2, frame, room, ((new_a, from_a), (new_b, from_b)))
    fill_x(fill_2, frame, room, (new_s, from_s), 1, 0)
    half_3(
        frame, 2, tiles, table, factor, (from_a, from_b, from_s), (new_a, new_b, new_s), room, room2,
        degree, first, second, third, ghost_degree, ghost_first,
    )


def step_3b(
    tiles, signals, table, spectral, scales, from_a, from_b, from_x, new_a, new_b, new_x, room_in, room2_in,
    degree_a, degree, first_a, first, second, ghost_degree, ghost_first, third_a,
    coefficients, partial, room, room2, third,
):
    frame = Frame()
    factor = 2.0 / jnp.full((16, 128), spectral[0])
    room[ZERO] = jnp.zeros((16, 128), BF16)
    room2[ZERO] = jnp.zeros((16, 128), BF16)
    carry_rooms(room, room_in, room2, room2_in)
    fill_x(fill_2, frame, room, (new_x, from_x), 4, 5)
    half_3(
        frame, 3, tiles, table, factor, (from_a, from_b, from_x), (new_a, new_b, new_x), room, room2,
        degree, first, second, third, ghost_degree, ghost_first,
    )
    count = scales.shape[0]
    squares = [jnp.zeros((16, 128), F32) for _ in range(count)]
    for u, degrees, firsts, thirds in ((2, degree_a, first_a, third_a), (3, degree, first, third)):
        row = frame.row(u)
        for v in range(COLS):
            col = frame.col(v)
            sums = own_product(tiles, table, row, col, room2)
            alive = alive_of(table, row, col)
            value = thirds[v]
            fourth = 2.0 * (factor * (degrees[v] * value - sums * alive) - value) - second[u - 2, v]
            terms = (signals[row, col] * alive, firsts[v], second[u - 2, v], value, fourth)
            for scale in range(count):
                total = (0.5 * scales[scale, 0]) * terms[0]
                for order in range(1, len(terms)):
                    total = total + scales[scale, order] * terms[order]
                coefficients[scale, row, col] = total
                squares[scale] = squares[scale] + total * total
    block = jnp.concatenate(squares + [jnp.zeros((128 - 16 * count, 128), F32)], axis=0)
    line = jnp.sum(jnp.transpose(block), axis=0, keepdims=True)
    partial[...] = jnp.broadcast_to(line[None], partial.shape)


def in_hbm(*arrays):
    return tuple(pltpu.with_memory_space_constraint(array, pltpu.MemorySpace.HBM) for array in arrays)


def in_vmem(*arrays):
    return tuple(pltpu.with_memory_space_constraint(array, pltpu.MemorySpace.VMEM) for array in arrays)


def neighbour_pairs(devices, first):
    pairs = [(i, i + 1) for i in range(first, devices - 1, 2)]
    return pairs + [(j, i) for i, j in pairs]


def shape(dims, kind=BF16):
    return jax.ShapeDtypeStruct(dims, kind)


def shards(signals, tiles, tile_dir, tile_mask, live_rows, bound_rows, scale_coeffs, spectral_bound):
    devices_x, devices_z = lax.axis_size(GX), lax.axis_size("gy")
    devices = devices_x * devices_z
    scales, channels = scale_coeffs.shape[0], signals.shape[2]
    nodes = ROWS * COLS * 128 * devices

    def swap_z(a, b):
        return (
            lax.ppermute(a, "gy", neighbour_pairs(devices_z, 0)),
            lax.ppermute(b, "gy", neighbour_pairs(devices_z, 1)),
        )

    def swap_x(s, x):
        far = lax.ppermute(x, GX, neighbour_pairs(devices_x, 1))
        return lax.ppermute(s, "gx_2", [(0, 1), (1, 0)]), far

    def call(body, outs, in_specs, out_specs, scratch=(), aliases=None, flops=1000, mib=16):
        return pl.pallas_call(
            body,
            out_shape=outs,
            in_specs=in_specs,
            out_specs=out_specs,
            scratch_shapes=list(scratch),
            input_output_aliases=aliases or {},
            compiler_params=params(mib),
            cost_estimate=cost(flops),
        )

    tile_dir, tile_mask = jnp.swapaxes(tile_dir, 1, 2), jnp.swapaxes(tile_mask, 1, 2)
    local = (tiles, signals, tile_dir, tile_mask, live_rows, bound_rows)
    rooms = [
        pltpu.VMEM(signals.shape, F32),
        pltpu.SMEM(tile_dir.shape, jnp.int32),
        pltpu.SMEM(tile_dir.shape, jnp.int32),
        pltpu.SMEM(live_rows.shape, jnp.int32),
        pltpu.SMEM(live_rows.shape, jnp.int32),
        pltpu.SemaphoreType.DMA((2, SLOTS)),
        pltpu.SemaphoreType.DMA((5,)),
    ]
    message_z, message_x = pltpu.VMEM((ROWS, LONG, 128), BF16), pltpu.VMEM((COLS + 2, LONG, 128), BF16)
    a, b = call(pack_z, [message_z] * 2, [HBM] * 6, [VMEM] * 2, rooms)(*in_hbm(*local))
    table_shape = shape((ROWS, SLOTS + 2, COLS), jnp.int32)
    s, x, table = call(
        pack_x, [message_x] * 2 + [table_shape], [HBM] * 6, [VMEM] * 2 + [SMEM], rooms, flops=1 << 21
    )(*in_hbm(*local))
    a, b = swap_z(a, b)
    corner_room = [pltpu.VMEM((2, 2, LONG, 128), BF16), pltpu.SemaphoreType.DMA((2, 2))]
    s, x = call(
        corners_1, [message_x] * 2, [VMEM] * 2 + [ANY] * 2, [ANY] * 2, corner_room, {2: 0, 3: 1}
    )(a, b, *in_vmem(s, x))
    s, x = swap_x(s, x)

    turned = call(
        turn_tiles, [shape((ROWS, COLS, SLOTS * 128, 128))], [VMEM], [VMEM], flops=1 << 24
    )(tiles)[0]
    half = shape((COLS, channels, 128), F32)
    extra = shape((COLS + 4, channels, 128), F32)
    wide_room, room = shape((ZERO + 1, 32, 128)), shape((ZERO + 1, 16, 128))
    wide_scratch, scratch = pltpu.VMEM((ZERO + 1, 32, 128), BF16), pltpu.VMEM((ZERO + 1, 16, 128), BF16)
    short_z, short_x = pltpu.VMEM((ROWS, 32, 128), BF16), pltpu.VMEM((COLS + 2, 32, 128), BF16)
    room_1, room_2, degree_a, first_a, ghost_degree_a, ghost_first_a = call(
        step_1a, [wide_room, room, half, half, extra, extra], [VMEM] * 2 + [SMEM] * 2 + [VMEM] * 3, [VMEM] * 6, flops=1 << 25
    )(turned, signals, table, spectral_bound, a, b, s)
    degree_b, first_b, ghost_degree_b, ghost_first_b, second, a2, b2 = call(
        step_1b,
        [half, half, extra, extra, shape((ROWS, COLS, channels, 128), F32), short_z, short_z],
        [VMEM] * 2 + [SMEM] * 2 + [VMEM] * 7,
        [VMEM] * 7,
        [wide_scratch, scratch],
        flops=1 << 26,
    )(turned, signals, table, spectral_bound, a, b, x, room_1, room_2, degree_a, first_a)
    s2, x2 = call(pack_x2, [short_x] * 2, [VMEM, SMEM], [VMEM] * 2, flops=1 << 20)(second, table)
    a2, b2 = swap_z(a2, b2)
    corner_room = [pltpu.VMEM((2, 2, 32, 128), BF16), pltpu.SemaphoreType.DMA((2, 2))]
    s2, x2 = call(
        corners_2, [short_x] * 2, [VMEM] * 4 + [ANY] * 2, [ANY] * 2, corner_room, {4: 0, 5: 1}
    )(a, b, a2, b2, *in_vmem(s2, x2))
    s2, x2 = swap_x(s2, x2)
    room_1, room_2, third_a = call(
        step_3a, [room, room, half], [VMEM, SMEM, SMEM] + [VMEM] * 11, [VMEM] * 3, flops=1 << 25
    )(
        turned, table, spectral_bound, a, b, s, a2, b2, s2, degree_a, first_a, second, ghost_degree_a, ghost_first_a
    )
    totals, partial = call(
        step_3b,
        [shape((scales, ROWS, COLS, channels, 128), F32), shape((devices, 1, 128), F32)],
        [VMEM] * 2 + [SMEM] * 3 + [VMEM] * 16,
        [VMEM] * 2,
        [scratch, scratch, pltpu.VMEM((COLS, channels, 128), F32)],
        flops=1 << 26,
    )(
        turned, signals, table, spectral_bound, scale_coeffs, a, b, x, a2, b2, x2, room_1, room_2,
        degree_a, degree_b, first_a, first_b, second, ghost_degree_b, ghost_first_b, third_a,
    )
    gathered = lax.all_to_all(partial, GX_GY, 0, 0)
    energy = jnp.sum(gathered, axis=(0, 1))[: scales * channels].reshape(scales, channels) / nodes
    return (totals, energy)


def solution(mesh):
    torus = Mesh(mesh.devices.reshape(4, 4, 2, mesh.shape["gy"]), ("gx_0", "gx_1", "gx_2", "gy"))
    placed = (
        P(GX, "gy", None, None),
        P(GX, "gy", None, None, None),
        P(GX, "gy", None),
        P(GX, "gy", None),
        P(GX, "gy"),
        P(GX, "gy"),
        P(),
        P(),
    )
    return jax.shard_map(
        shards,
        mesh=torus,
        in_specs=placed,
        out_specs=(P(None, GX, "gy", None, None), P()),
        check_vma=False,
    )
```

time: 68.8 us -> 61.4 us (0.89)
  local copies, waits for them, and re-layouts: 6.09 us -> 0.69 us
  waiting for transfers between devices: 8.85 us -> 3.95 us
  Pallas kernels: 9.39 us -> 13.6 us
  starting transfers between devices: 17.4 us -> 16.4 us
    unnamed x20 -> x6, local copies, waits for them, and re-layouts: 5.42 us -> 0.02 us
    pallas_call x6 -> x10, Pallas kernels: 9.39 us -> 13.6 us  [the longest x1 2.71 us: shards(): call(step_3b, [shape((scales, ROWS, COLS, channels, 128), F32), shape((de...]
    ppermute x2, waiting for transfers between devices: 7.94 us -> 3.94 us  [swap_x(): far = lax.ppermute(x, GX, neighbour_pairs(devices_x, 1))]
    ppermute x2, waiting for transfers between devices: 0.9 us -> 0.01 us  [swap_z(): lax.ppermute(a, 'gy', neighbour_pairs(devices_z, 0))]
    ppermute x2, starting transfers between devices: 7.94 us -> 7.2 us  [swap_z(): lax.ppermute(a, 'gy', neighbour_pairs(devices_z, 0))]
  transfers between devices with their start and end apart: 8 -> 8, of which waited for: 4 -> 2; matrix products, arithmetic and copies ran while one was open for 0% -> 0% of each run, Pallas kernels for 2% -> 12%
where the time goes in v3:
time: 61.4 us; the launch traced here: 61.2 us
  blocking collectives  25 us (41%)
  starting transfers between devices  16.4 us (27%)
  Pallas kernels  13.6 us (22%)
  waiting for transfers between devices  3.95 us (6%)
  between operations  1.45 us (2%)
  local copies, waits for them, and re-layouts  0.69 us (1%)
    all_to_all x1, blocking collectives, shards(): gathered = lax.all_to_all(partial, GX_GY, 0, 0)  25 us
    ppermute x2, starting transfers between devices, swap_z(): lax.ppermute(a, 'gy', neighbour_pairs(devices_z, 0))  7.2 us
    ppermute x2, starting transfers between devices, swap_x(): far = lax.ppermute(x, GX, neighbour_pairs(devices_x, 1))  6.73 us
    ppermute x2, waiting for transfers between devices, swap_x(): far = lax.ppermute(x, GX, neighbour_pairs(devices_x, 1))  3.94 us
    pallas_call x1, Pallas kernels, shards(): call(step_3b, [shape((scales, ROWS, COLS, channels, 128), F32), shape((de...  2.71 us
    pallas_call x1, Pallas kernels, shards(): call(pack_x, [message_x] * 2 + [table_shape], [HBM] * 6, [VMEM] * 2 + [SM...  2.34 us
    pallas_call x1, Pallas kernels, shards(): call(step_1b, [half, half, extra, extra, shape((ROWS, COLS, channels, 128...  1.78 us
    pallas_call x1, Pallas kernels, shards(): call(turn_tiles, [shape((ROWS, COLS, SLOTS * 128, 128))], [VMEM], [VMEM],...  1.48 us
  transfers between devices with their start and end apart: 8, of which 2 were waited for; matrix products, arithmetic and copies ran while one was open for 0% of the time, Pallas kernels for 12%

profile of v3, /device:TPU:1, one launch (start us, length us, event | category | flops | bytes accessed | tf_op | source)
XLA Modules:
  0.0 61.2 jit_solution(4454836656001249174)
XLA Ops:
  0.6 1.2 %shard_map.97 = (bf16[2,176,128]{2,1,0:T(8,128)(2,1)S(1)}, bf16[2,176,128]{2,1,0:T(8,128)(2,1)S(1)}) custom-call(bf16[2,8,4,128,128]{4,3,2,1,0:T(8,128)(2,1)} %tiles.5, f32[2,8,16,128]{3,2,1,0:T(8,128)} %signals.9, s32[2,4,8]{2,1,0:T(4,128)} %bitcast.2, s32[2,4,8]{2,1,0:T(4,128)} %bitcast.4, s32[2,8]{1,0:T(2,128)} %live.3, s32[2,8]{1,0:T(2,128)} %bound.3), custom_call_target="tpu_custom_call" | custom-call | flops 1000 | bytes 1048576 | tf_op jit(solution)/shard_map/pallas_call | solution.py:578
  1.9 0.0 copy-start
  1.9 2.5 %collective-permute-start = (bf16[2,176,128]{2,1,0:T(8,128)(2,1)S(1)}, bf16[2,176,128]{2,1,0:T(8,128)(2,1)S(1)}, u32[]{:S(2)}, u32[]{:S(2)}) collective-permute-start(bf16[2,176,128]{2,1,0:T(8,128)(2,1)S(1)} %get-tuple-element.32), channel_id=1, source_target_pairs={{0,1},{2,3},{1,0},{3,2},{4,5},{6,7},{5,4},{7,6},{8,9},{10,11},{9,8... | collective-permute-start | bytes 270344 | tf_op jit(solution)/shard_map/ppermute | solution.py:546
  4.4 0.7 %collective-permute-start.1 = (bf16[2,176,128]{2,1,0:T(8,128)(2,1)S(1)}, bf16[2,176,128]{2,1,0:T(8,128)(2,1)S(1)}, u32[]{:S(2)}, u32[]{:S(2)}) collective-permute-start(bf16[2,176,128]{2,1,0:T(8,128)(2,1)S(1)} %get-tuple-element.33), channel_id=1, source_target_pairs={{1,2},{2,1},{5,6},{6,5},{9,10},{10,9},{13,14},{14,13},{17,18},{18,... | collective-permute-start | bytes 270344 | tf_op jit(solution)/shard_map/ppermute | solution.py:547
  5.1 2.3 %shard_map.96 = (bf16[10,176,128]{2,1,0:T(8,128)(2,1)S(1)}, bf16[10,176,128]{2,1,0:T(8,128)(2,1)S(1)}, s32[2,6,8]{2,1,0:T(8,128)S(1)}) custom-call(bf16[2,8,4,128,128]{4,3,2,1,0:T(8,128)(2,1)} %tiles.5, f32[2,8,16,128]{3,2,1,0:T(8,128)} %signals.9, s32[2,4,8]{2,1,0:T(4,128)} %bitcast.3, s32[2,4,8]{2,1,0:T(4,128)} %bitcast.5, s32[2,8]{1,0:T(2,128)} %live.3, ...), custom_call_target="tpu_custom_call" | custom-call | flops 2097152 | bytes 1048576 | tf_op jit(solution)/shard_map/pallas_call | solution.py:580
  7.4 0.4 shard_map.98
  7.9 1.0 %collective-permute-start.3 = (bf16[10,176,128]{2,1,0:T(8,128)(2,1)S(1)}, bf16[10,176,128]{2,1,0:T(8,128)(2,1)S(1)}, u32[]{:S(2)}, u32[]{:S(2)}) collective-permute-start(bf16[10,176,128]{2,1,0:T(8,128)(2,1)S(1)} %get-tuple-element.37), channel_id=1, source_target_pairs={{0,4},{4,0},{1,5},{5,1},{2,6},{6,2},{3,7},{7,3},{8,12},{12,8},{9,1... | collective-permute-start | bytes 1351688 | tf_op jit(solution)/shard_map/ppermute | solution.py:552
  8.9 3.1 %collective-permute-start.2 = (bf16[10,176,128]{2,1,0:T(8,128)(2,1)S(1)}, bf16[10,176,128]{2,1,0:T(8,128)(2,1)S(1)}, u32[]{:S(2)}, u32[]{:S(2)}) collective-permute-start(bf16[10,176,128]{2,1,0:T(8,128)(2,1)S(1)} %get-tuple-element.36), channel_id=1, source_target_pairs={{4,8},{12,16},{20,24},{28,32},{36,40},{44,48},{52,56},{60,64},{68,... | collective-permute-start | bytes 1351688 | tf_op jit(solution)/shard_map/ppermute | solution.py:551
  12.7 1.5 %shard_map.95.tiles = bf16[2,8,512,128]{3,2,1,0:T(8,128)(2,1)S(1)} custom-call(bf16[2,8,4,128,128]{4,3,2,1,0:T(8,128)(2,1)S(1)} %copy-done), custom_call_target="tpu_custom_call" | custom-call | flops 16777216 | bytes 1048576 | tf_op jit(solution)/shard_map/pallas_call | solution.py:590
  14.2 1.4 %shard_map.99 = (bf16[145,32,128]{2,1,0:T(8,128)(2,1)S(1)}, bf16[145,16,128]{2,1,0:T(8,128)(2,1)S(1)}, f32[8,16,128]{2,1,0:T(8,128)S(1)}, f32[8,16,128]{2,1,0:T(...) custom-call(bf16[2,8,512,128]{3,2,1,0:T(8,128)(2,1)S(1)} %shard_map.95.tiles, ...), custom_call_target="tpu_custom_call" | custom-call | flops 33554432 | bytes 1048576 | tf_op jit(solution)/shard_map/pallas_call | solution.py:598
  15.6 3.0 %collective-permute-done.2.from_x = bf16[10,176,128]{2,1,0:T(8,128)(2,1)S(1)} collective-permute-done((bf16[10,176,128]{2,1,0:T(8,128)(2,1)S(1)}, bf16[10,176,128]{2,1,0:T(8,128)(2,1)S(1)}, u32[]{:S(2)}, u32[]{:S(2)}) %collective-permute-start.2) | collective-permute-done | bytes 450592 | tf_op jit(solution)/shard_map/ppermute | solution.py:551
  18.6 1.8 %shard_map.100 = (f32[8,16,128]{2,1,0:T(8,128)S(1)}, f32[8,16,128]{2,1,0:T(8,128)S(1)}, f32[12,16,128]{2,1,0:T(8,128)S(1)}, f32[12,16,128]{2,1,0:T(8,128)S(1)}, ...) custom-call(bf16[2,8,512,128]{3,2,1,0:T(8,128)(2,1)S(1)} %shard_map.95.tiles, ...), custom_call_target="tpu_custom_call" | custom-call | flops 67108864 | bytes 1048576 | tf_op jit(solution)/shard_map/pallas_call | solution.py:601
  20.4 4.7 %collective-permute-start.4 = (bf16[2,32,128]{2,1,0:T(8,128)(2,1)S(1)}, bf16[2,32,128]{2,1,0:T(8,128)(2,1)S(1)}, u32[]{:S(2)}, u32[]{:S(2)}) collective-permute-start(bf16[2,32,128]{2,1,0:T(8,128)(2,1)S(1)} %get-tuple-element.42), channel_id=1, source_target_pairs={{0,1},{2,3},{1,0},{3,2},{4,5},{6,7},{5,4},{7,6},{8,9},{10,11},{9,8... | collective-permute-start | bytes 49160 | tf_op jit(solution)/shard_map/ppermute | solution.py:546
  25.1 0.7 %collective-permute-start.5 = (bf16[2,32,128]{2,1,0:T(8,128)(2,1)S(1)}, bf16[2,32,128]{2,1,0:T(8,128)(2,1)S(1)}, u32[]{:S(2)}, u32[]{:S(2)}) collective-permute-start(bf16[2,32,128]{2,1,0:T(8,128)(2,1)S(1)} %get-tuple-element.43), channel_id=1, source_target_pairs={{1,2},{2,1},{5,6},{6,5},{9,10},{10,9},{13,14},{14,13},{17,18},{18,... | collective-permute-start | bytes 49160 | tf_op jit(solution)/shard_map/ppermute | solution.py:547
  25.7 0.8 %shard_map.101 = (bf16[10,32,128]{2,1,0:T(8,128)(2,1)S(1)}, bf16[10,32,128]{2,1,0:T(8,128)(2,1)S(1)}) custom-call(f32[2,8,16,128]{3,2,1,0:T(8,128)S(1)} %get-tuple-element.44.second, s32[2,6,8]{2,1,0:T(8,128)S(1)} %get-tuple-element.31.table), custom_call_target="tpu_custom_call" | custom-call | flops 1048576 | bytes 1048576 | tf_op jit(solution)/shard_map/pallas_call | solution.py:609
  26.5 0.2 shard_map.102
  26.8 0.1 collective-permute-start.7
  26.9 3.6 %collective-permute-start.6 = (bf16[10,32,128]{2,1,0:T(8,128)(2,1)S(1)}, bf16[10,32,128]{2,1,0:T(8,128)(2,1)S(1)}, u32[]{:S(2)}, u32[]{:S(2)}) collective-permute-start(bf16[10,32,128]{2,1,0:T(8,128)(2,1)S(1)} %get-tuple-element.47), channel_id=1, source_target_pairs={{4,8},{12,16},{20,24},{28,32},{36,40},{44,48},{52,56},{60,64},{68,... | collective-permute-start | bytes 245768 | tf_op jit(solution)/shard_map/ppermute | solution.py:551
  30.5 1.2 %shard_map.103 = (bf16[145,16,128]{2,1,0:T(8,128)(2,1)S(1)}, bf16[145,16,128]{2,1,0:T(8,128)(2,1)S(1)}, f32[8,16,128]{2,1,0:T(8,128)S(1)}) custom-call(bf16[2,8,512,128]{3,2,1,0:T(8,128)(2,1)S(1)} %shard_map.95.tiles, s32[2,6,8]{2,1,0:T(8,128)S(1)} %get-tuple-element.31.table, f32[1]{0:T(128)S(6)} %copy.18.spectral, ...), custom_call_target="tpu_custom_call" | custom-call | flops 33554432 | bytes 1048576 | tf_op jit(solution)/shard_map/pallas_call | solution.py:616
  31.8 0.9 %collective-permute-done.6.new_x = bf16[10,32,128]{2,1,0:T(8,128)(2,1)S(1)} collective-permute-done((bf16[10,32,128]{2,1,0:T(8,128)(2,1)S(1)}, bf16[10,32,128]{2,1,0:T(8,128)(2,1)S(1)}, u32[]{:S(2)}, u32[]{:S(2)}) %collective-permute-start.6) | collective-permute-done | bytes 81952 | tf_op jit(solution)/shard_map/ppermute | solution.py:551
  32.6 2.7 %shard_map.104 = (f32[6,2,8,16,128]{4,3,2,1,0:T(8,128)}, f32[128,1,128]{2,1,0:T(1,128)S(1)}) custom-call(bf16[2,8,512,128]{3,2,1,0:T(8,128)(2,1)S(1)} %shard_map.95.tiles, f32[2,8,16,128]{3,2,1,0:T(8,128)S(1)} %copy-done.1, s32[2,6,8]{2,1,0:T(8,128)S(1)} %get-tuple-element.31.table, f32[1]{0:T(128)S(6)} %copy.18.spectral, f32[6,5]{1,0:T(8,128)S(1)} %copy-done.2, ...), custom_call_target="tpu_custom_call" | custom-call | flops 67108864 | bytes 1048576 | tf_op jit(solution)/shard_map/pallas_call | solution.py:621
  35.4 25.0 %all_to_all.5 = f32[128,1,128]{2,1,0:T(1,128)S(1)} all-to-all(f32[128,1,128]{2,1,0:T(1,128)S(1)} %get-tuple-element.59), channel_id=1, replica_groups=mesh['gx_0'=4,'gx_1'=4,'gx_2'=2,'gy'=4] {'gx_0','gx_1','gx_2','gy'}, dimensions={0} | all-to-all | bytes 131072 | tf_op jit(solution)/shard_map/all_to_all | solution.py:632
  60.3 0.2 reduce_sum.9
  60.5 0.7 %div.10 = f32[6,16]{1,0:T(8,128)} reshape(f32[96]{0:T(128)S(1)} %slice_multiply_fusion) | data formatting | bytes 768 | tf_op jit(solution)/shard_map/div | solution.py:633
  (12 shorter events, 0.0 us)
Async XLA Ops:
  1.9 10.8 %copy-start = (bf16[2,8,4,128,128]{4,3,2,1,0:T(8,128)(2,1)S(1)}, bf16[2,8,4,128,128]{4,3,2,1,0:T(8,128)(2,1)}, u32[]{:S(2)}) copy-start(bf16[2,8,4,128,128]{4,3,2,1,0:T(8,128)(2,1)} %tiles.5) | copy-start | bytes 6291460
  1.9 5.5 %collective-permute-start = (bf16[2,176,128]{2,1,0:T(8,128)(2,1)S(1)}, bf16[2,176,128]{2,1,0:T(8,128)(2,1)S(1)}, u32[]{:S(2)}, u32[]{:S(2)}) collective-permute-start(bf16[2,176,128]{2,1,0:T(8,128)(2,1)S(1)} %get-tuple-element.32), channel_id=1, source_target_pairs={{0,1},{2,3},{1,0},{3,2},{4,5},{6,7},{5,4},{7,6},{8,9},{10,11},{9,8... | collective-permute-start | bytes 270344 | tf_op jit(solution)/shard_map/ppermute | solution.py:546
  4.4 3.0 %collective-permute-start.1 = (bf16[2,176,128]{2,1,0:T(8,128)(2,1)S(1)}, bf16[2,176,128]{2,1,0:T(8,128)(2,1)S(1)}, u32[]{:S(2)}, u32[]{:S(2)}) collective-permute-start(bf16[2,176,128]{2,1,0:T(8,128)(2,1)S(1)} %get-tuple-element.33), channel_id=1, source_target_pairs={{1,2},{2,1},{5,6},{6,5},{9,10},{10,9},{13,14},{14,13},{17,18},{18,... | collective-permute-start | bytes 270344 | tf_op jit(solution)/shard_map/ppermute | solution.py:547
  7.9 6.3 %collective-permute-start.3 = (bf16[10,176,128]{2,1,0:T(8,128)(2,1)S(1)}, bf16[10,176,128]{2,1,0:T(8,128)(2,1)S(1)}, u32[]{:S(2)}, u32[]{:S(2)}) collective-permute-start(bf16[10,176,128]{2,1,0:T(8,128)(2,1)S(1)} %get-tuple-element.37), channel_id=1, source_target_pairs={{0,4},{4,0},{1,5},{5,1},{2,6},{6,2},{3,7},{7,3},{8,12},{12,8},{9,1... | collective-permute-start | bytes 1351688 | tf_op jit(solution)/shard_map/ppermute | solution.py:552
  8.9 9.7 %collective-permute-start.2 = (bf16[10,176,128]{2,1,0:T(8,128)(2,1)S(1)}, bf16[10,176,128]{2,1,0:T(8,128)(2,1)S(1)}, u32[]{:S(2)}, u32[]{:S(2)}) collective-permute-start(bf16[10,176,128]{2,1,0:T(8,128)(2,1)S(1)} %get-tuple-element.36), channel_id=1, source_target_pairs={{4,8},{12,16},{20,24},{28,32},{36,40},{44,48},{52,56},{60,64},{68,... | collective-permute-start | bytes 1351688 | tf_op jit(solution)/shard_map/ppermute | solution.py:551
  12.7 1.5 %copy-start.1 = (f32[2,8,16,128]{3,2,1,0:T(8,128)S(1)}, f32[2,8,16,128]{3,2,1,0:T(8,128)}, u32[]{:S(2)}) copy-start(f32[2,8,16,128]{3,2,1,0:T(8,128)} %signals.9) | copy-start | bytes 393220
  20.4 12.2 %copy-start.2 = (f32[6,5]{1,0:T(8,128)S(1)}, f32[6,5]{1,0:T(8,128)}, u32[]{:S(2)}) copy-start(f32[6,5]{1,0:T(8,128)} %scales.1) | copy-start | bytes 364
  20.4 6.1 %collective-permute-start.4 = (bf16[2,32,128]{2,1,0:T(8,128)(2,1)S(1)}, bf16[2,32,128]{2,1,0:T(8,128)(2,1)S(1)}, u32[]{:S(2)}, u32[]{:S(2)}) collective-permute-start(bf16[2,32,128]{2,1,0:T(8,128)(2,1)S(1)} %get-tuple-element.42), channel_id=1, source_target_pairs={{0,1},{2,3},{1,0},{3,2},{4,5},{6,7},{5,4},{7,6},{8,9},{10,11},{9,8... | collective-permute-start | bytes 49160 | tf_op jit(solution)/shard_map/ppermute | solution.py:546
  25.1 1.5 %collective-permute-start.5 = (bf16[2,32,128]{2,1,0:T(8,128)(2,1)S(1)}, bf16[2,32,128]{2,1,0:T(8,128)(2,1)S(1)}, u32[]{:S(2)}, u32[]{:S(2)}) collective-permute-start(bf16[2,32,128]{2,1,0:T(8,128)(2,1)S(1)} %get-tuple-element.43), channel_id=1, source_target_pairs={{1,2},{2,1},{5,6},{6,5},{9,10},{10,9},{13,14},{14,13},{17,18},{18,... | collective-permute-start | bytes 49160 | tf_op jit(solution)/shard_map/ppermute | solution.py:547
  26.8 3.7 %collective-permute-start.7 = (bf16[10,32,128]{2,1,0:T(8,128)(2,1)S(1)}, bf16[10,32,128]{2,1,0:T(8,128)(2,1)S(1)}, u32[]{:S(2)}, u32[]{:S(2)}) collective-permute-start(bf16[10,32,128]{2,1,0:T(8,128)(2,1)S(1)} %get-tuple-element.48), channel_id=1, source_target_pairs={{0,4},{4,0},{1,5},{5,1},{2,6},{6,2},{3,7},{7,3},{8,12},{12,8},{9,1... | collective-permute-start | bytes 245768 | tf_op jit(solution)/shard_map/ppermute | solution.py:552
  26.9 5.8 %collective-permute-start.6 = (bf16[10,32,128]{2,1,0:T(8,128)(2,1)S(1)}, bf16[10,32,128]{2,1,0:T(8,128)(2,1)S(1)}, u32[]{:S(2)}, u32[]{:S(2)}) collective-permute-start(bf16[10,32,128]{2,1,0:T(8,128)(2,1)S(1)} %get-tuple-element.47), channel_id=1, source_target_pairs={{4,8},{12,16},{20,24},{28,32},{36,40},{44,48},{52,56},{60,64},{68,... | collective-permute-start | bytes 245768 | tf_op jit(solution)/shard_map/ppermute | solution.py:551

commit v4 on v3

v4 whole, which is shorter than its diff:
```python
import jax
import jax.numpy as jnp
from jax import lax
from jax.experimental import pallas as pl
from jax.experimental.pallas import tpu as pltpu
from jax.sharding import Mesh
from jax.sharding import PartitionSpec as P

GX_GY = ("gx_0", "gx_1", "gx_2", "gy")
GX = ("gx_0", "gx_1", "gx_2")
F32 = jnp.float32
BF16 = jnp.bfloat16
EDGE = 32
ROWS, COLS = 2, 8
WIDE = COLS + 4
SPOTS = (ROWS + 4) * WIDE
ZERO = SPOTS
SLOTS = 4
NEAR, INFO, FAR, LONG = 32, 48, 64, 80
HIGH, LOW, OWN_HIGH, OWN_LOW = 0, 1, 2, 3
DIRS, BOUND, DEGREE, BOUND2, BOUND3, BOUND4 = 0, 1, 2, 3, 4, 5
VMEM = pl.BlockSpec(memory_space=pltpu.VMEM)
SMEM = pl.BlockSpec(memory_space=pltpu.SMEM)
ANY = pl.BlockSpec(memory_space=pl.ANY)
HBM = pl.BlockSpec(memory_space=pltpu.MemorySpace.HBM)


def params(mib):
    return pltpu.CompilerParams(vmem_limit_bytes=mib * 1024 * 1024)


def cost(flops):
    return pl.CostEstimate(flops=flops, bytes_accessed=1 << 20, transcendentals=0)


def lanes():
    return lax.broadcasted_iota(jnp.int32, (16, 128), 1)


def below(count):
    return (lanes() < count).astype(F32)


def split(value):
    high = value.astype(BF16)
    return high, value - high.astype(F32)


def info_of(rows):
    index = lax.broadcasted_iota(jnp.int32, (16, 128), 0)
    info = jnp.zeros((16, 128), F32)
    for row, value in rows.items():
        info = jnp.where(index == row, value, info)
    return info.astype(BF16)


def odd_z():
    return lax.axis_index("gy") % 2


def odd_core():
    return lax.axis_index("gx_2")


def merge(parts):
    lane = lax.broadcasted_iota(jnp.int32, parts[0].shape, 1)
    merged = parts[0]
    for index, part in enumerate(parts[1:], 1):
        merged = jnp.where(lane < EDGE * index, merged, pltpu.roll(part, EDGE * index, 1))
    return merged if len(parts) == 4 else jnp.where(lane < EDGE * len(parts), merged, 0.0)


def piece(pack, index):
    moved = pltpu.roll(pack, 128 - EDGE * index, 1) if index else pack
    return jnp.where(lanes() < EDGE, moved, 0.0)


def repeat(value):
    value = value + pltpu.roll(value, EDGE, 1)
    return value + pltpu.roll(value, 2 * EDGE, 1)


def wide(value):
    return jnp.concatenate([value, jnp.zeros((value.shape[0], 128 - value.shape[1]), value.dtype)], axis=1)


def with_head(value, line):
    return jnp.concatenate([value.astype(BF16), jnp.where(heads(), line, 0.0).astype(BF16)], axis=0)


def heads():
    return lax.broadcasted_iota(jnp.int32, (16, 128), 0) == 0


def block_message(out, at, refs, raw, row, col, row2, col2):
    signals, dirs, masks, live, bound = refs
    alive, inside = below(live[row, col]), below(bound[row, col])
    value = signals[row, col] * alive
    full = with_head(value, alive).astype(F32)
    inputs, sides = [], []
    for slot in range(SLOTS):
        side, used = dirs[row, slot, col], masks[row, slot, col] == 1
        own = jnp.where(side == 4, jnp.where(used, 1.0, 0.0), 0.0)
        inputs.append((full * own).astype(BF16))
        sides.append(jnp.full((16, 128), jnp.where(used, side, 9).astype(F32)))
    product = lax.dot_general(
        jnp.concatenate(inputs, axis=1),
        jnp.concatenate([raw[slot] for slot in range(SLOTS)], axis=1),
        (((1,), (1,)), ((), ())),
        preferred_element_type=F32,
    )
    product = wide(product)
    value = value * inside
    high, low = split(value)
    own_high, own_low = split(product[0:16])
    own_high = own_high.astype(F32)
    degree_high, degree_low = split(product[16:17])
    out[at, 0:NEAR] = merge([raw[slot].astype(F32) for slot in range(SLOTS)]).astype(BF16)
    out[at, NEAR:INFO] = merge([high.astype(F32), low, own_high, own_low]).astype(BF16)
    inside2 = below(bound[row2, col2])
    lane = lanes()
    rows = {
        DIRS: jnp.where(
            lane < EDGE, sides[0], jnp.where(lane < 2 * EDGE, sides[1], jnp.where(lane < 3 * EDGE, sides[2], sides[3]))
        ),
        BOUND: repeat(inside),
        DEGREE: jnp.broadcast_to(degree_high.astype(F32) + pltpu.roll(degree_low, EDGE, 1), (16, 128)),
        BOUND2: repeat(inside2),
    }
    out[at, INFO:FAR] = info_of(rows)
    out[at, FAR:LONG] = (signals[row2, col2] * inside2).astype(BF16)


def fetch(refs, rooms, sems):
    copies = [pltpu.make_async_copy(ref, room, sems.at[i]) for i, (ref, room) in enumerate(zip(refs, rooms))]
    for copy in copies:
        copy.start()
    return copies


def pack_z(tiles, signals, dirs, masks, live, bound, out_a, out_b, raw, signals_v, dirs_s, masks_s, live_s, bound_s, sem, sem2):
    refs = (signals_v, dirs_s, masks_s, live_s, bound_s)
    copies = fetch((signals, dirs, masks, live, bound), refs, sem2)
    odd = odd_z()
    for which in range(2):
        col = jnp.where(odd == which, COLS - 1, 0)
        copies.append(pltpu.make_async_copy(tiles.at[:, col, :, 0:EDGE, :], raw.at[which], sem.at[which]))
        copies[-1].start()
    for copy in copies:
        copy.wait()
    for which, out in enumerate((out_a, out_b)):
        right = odd == which
        col, col2 = jnp.where(right, COLS - 1, 0), jnp.where(right, COLS - 2, 1)
        for row in range(ROWS):
            block_message(out, row, refs, raw[which, row], row, col, row, col2)


def pack_x(tiles, signals, dirs, masks, live, bound, out_s, out_b, raw, signals_v, dirs_s, masks_s, live_s, bound_s, sem, sem2):
    refs = (signals_v, dirs_s, masks_s, live_s, bound_s)
    copies = fetch((signals, dirs, masks, live, bound), refs, sem2)
    core = odd_core()
    for which in range(2):
        row = jnp.where(core == which, 1, 0)
        copies.append(pltpu.make_async_copy(tiles.at[row, :, :, 0:EDGE, :], raw.at[which], sem.at[which]))
        copies[-1].start()
    for copy in copies:
        copy.wait()
    for which, out in enumerate((out_s, out_b)):
        row = jnp.where(core == which, 1, 0)
        for col in range(COLS):
            block_message(out, 1 + col, refs, raw[which, col], row, col, 1 - row, col)


def place_corners(from_a, from_b, out_s, out_b, room, sem, far, info_at):
    odd, core = odd_z(), odd_core()
    copies = []
    for side, halo in enumerate((from_a, from_b)):
        at = jnp.where(odd == side, COLS + 1, 0)
        for which, out in enumerate((out_s, out_b)):
            row = jnp.where(core == which, 1, 0)
            near = far - 16 if info_at is None else info_at - 16
            first, other = halo[row, far : far + 16].astype(F32), halo[1 - row, far : far + 16].astype(F32)
            pack = merge([halo[1 - row, near : near + 16].astype(F32), first, other])
            room[which, side, 0:far] = halo[row, 0:far]
            room[which, side, far : far + 16] = pack.astype(BF16)
            if info_at is not None:
                info = halo[row, info_at : info_at + 16].astype(F32)
                info2 = halo[1 - row, info_at : info_at + 16].astype(F32)
                index = lax.broadcasted_iota(jnp.int32, (16, 128), 0)
                for place_at, source in (
                    (BOUND2, info2[BOUND : BOUND + 1]),
                    (BOUND3, info[BOUND2 : BOUND2 + 1]),
                    (BOUND4, info2[BOUND2 : BOUND2 + 1]),
                ):
                    info = jnp.where(index == place_at, source, info)
                room[which, side, info_at : info_at + 16] = info.astype(BF16)
            copies.append(pltpu.make_async_copy(room.at[which, side], out.at[at], sem.at[which, side]))
    for copy in copies:
        copy.start()
    for copy in copies:
        copy.wait()


def corners_1(from_a, from_b, in_s, in_b, out_s, out_b, room, sem):
    del in_s, in_b
    place_corners(from_a, from_b, out_s, out_b, room, sem, FAR, INFO)


def corners_2(from_a, from_b, in_s, in_b, out_s, out_b, room, sem):
    del in_s, in_b
    place_corners(from_a, from_b, out_s, out_b, room, sem, 16, None)


def place(u, v):
    return u * WIDE + v + 2


class Frame:
    def __init__(self):
        self.odd, self.core = odd_z(), odd_core()
        self.up = 2 * self.core - 1
        self.right = 1 - 2 * self.odd

    def row(self, u):
        return 1 - self.core if u == 2 else self.core

    def col(self, v):
        return jnp.where(self.odd == 1, COLS - 1 - v, v)


def ghost_blocks(frame, u, halo_a, halo_b, halo_x):
    row = frame.row(u)
    found = [(halo_a, row, u, COLS), (halo_b, row, u, -1)]
    return found + [(halo_x, frame.col(v) + 1, 1 if u == 2 else 4, v) for v in range(-1, COLS + 1)]


def ghost_product(frame, halo, at, spot_at, room, height):
    info = halo[at, INFO:FAR].astype(F32)
    step = jnp.where(info > 5.5, 1.0, jnp.where(info > 2.5, 0.0, -1.0))
    turned = 3.0 * (frame.up.astype(F32) * step) + frame.right.astype(F32) * (info - 3.0 * step - 4.0) + 4.0
    turned = jnp.where(info > 8.5, 9.0, turned)
    turn = jnp.broadcast_to(turned[DIRS : DIRS + 1], (16, 128)).astype(BF16)
    halves = [jnp.zeros((16, 128), BF16) for _ in range(height // 16)]
    for d in (0, 1, 2, 3, 5, 6, 7, 8):
        near = room[spot_at + (d // 3 - 1) * WIDE + d % 3 - 1]
        chosen = turn == d
        halves = [jnp.where(chosen, near[16 * h : 16 * h + 16], half) for h, half in enumerate(halves)]
    inputs = halves[0] if height == 16 else jnp.concatenate(halves, axis=0)
    product = lax.dot_general(inputs, halo[at, 0:NEAR], (((1,), (1,)), ((), ())), preferred_element_type=F32)
    return wide(product)


def slot_lanes():
    return (lanes() // EDGE).astype(F32).astype(BF16)


def near_input(table, row, col, room, height):
    group = slot_lanes()
    blocks = [room[table[row, slot, col]] for slot in range(SLOTS)]
    halves = []
    for half in range(0, height, 16):
        chosen = blocks[0][half : half + 16]
        for slot in range(1, SLOTS):
            chosen = jnp.where(group == slot, blocks[slot][half : half + 16], chosen)
        halves.append(chosen)
    return halves[0] if height == 16 else jnp.concatenate(halves, axis=0)


def own_product(weights, table, row, col, room, own):
    near = near_input(table, row, col, room, own.shape[0])
    return jnp.dot(jnp.concatenate([own, own, near], axis=1), weights[row, col], preferred_element_type=F32)


def alive_of(table, row, col):
    return below(table[row, SLOTS, col])


def inside_of(table, row, col):
    return below(table[row, SLOTS + 1, col])


def place_edge(room, at, value):
    room[at, 0:16] = repeat(value).astype(BF16)


def bound_row(halo, at):
    return halo[at, INFO:FAR].astype(F32)[BOUND : BOUND + 1]


def message_2(out, at, second, weights, table, u, v, u2, v2, frame):
    row, col = frame.row(u), frame.col(v)
    value = second[u - 2, v]
    own = value.astype(BF16)
    product = jnp.dot(jnp.concatenate([own, own], axis=1), weights[row, col, 0:256], preferred_element_type=F32)
    high, low = split(value * inside_of(table, row, col))
    own_high, own_low = split(product)
    out[at, 0:16] = merge([high.astype(F32), low, own_high.astype(F32), own_low]).astype(BF16)
    out[at, 16:32] = (second[u2 - 2, v2] * inside_of(table, frame.row(u2), frame.col(v2))).astype(BF16)
    return product


def turn_tiles(
    tiles, dirs, masks, live, bound, scales, out, table, scales_out, dirs_s, masks_s, live_s, bound_s, sem
):
    refs = (dirs_s, masks_s, live_s, bound_s, scales_out)
    for copy in fetch((dirs, masks, live, bound, scales), refs, sem):
        copy.wait()

    def one(block, carry):
        row, col = block // COLS, block % COLS
        total = jnp.zeros((128, 128), F32)
        for slot in range(SLOTS):
            own = jnp.where(dirs_s[row, slot, col] == 4, jnp.where(masks_s[row, slot, col] == 1, 1.0, 0.0), 0.0)
            tile = tiles[row, col, slot]
            total = total + tile.astype(F32) * own
            out[row, col, 256 + EDGE * slot : 256 + EDGE * (slot + 1)] = jnp.transpose(tile)[0:EDGE]
        high = total.astype(BF16)
        out[row, col, 0:128] = jnp.transpose(high)
        out[row, col, 128:256] = jnp.transpose((total - high.astype(F32)).astype(BF16))
        return carry

    lax.fori_loop(0, ROWS * COLS, one, 0)
    core, odd = odd_core(), odd_z()
    down, right = (2 * core - 1) * WIDE, 1 - 2 * odd
    for row in range(ROWS):
        for col in range(COLS):
            base = place(jnp.where(core == row, 3, 2), jnp.where(odd == 1, COLS - 1 - col, col))
            for slot in range(SLOTS):
                side = dirs_s[row, slot, col]
                step = jnp.where(side > 5, 1, jnp.where(side > 2, 0, -1))
                index = base + step * down + (side - 3 * step - 4) * right
                index = jnp.where(side == 4, ZERO, index)
                table[row, slot, col] = jnp.where(masks_s[row, slot, col] == 1, index, ZERO)
            table[row, SLOTS, col] = live_s[row, col]
            table[row, SLOTS + 1, col] = bound_s[row, col]


def fill(room, halo, near, info, far, at, near_at, far_at, corner):
    place_edge(room, near_at, piece(halo[at, near : near + 16].astype(F32), HIGH))
    beyond = halo[at, far : far + 16].astype(F32)
    places = (far_at,) + corner
    for index, spot_at in enumerate(places):
        place_edge(room, spot_at, piece(beyond, index))
    if info is not None:
        lines = halo[at, info : info + 16].astype(F32)
        for spot_at, line in zip((near_at,) + places, (BOUND, BOUND2, BOUND3, BOUND4)):
            room[spot_at, 16:32] = jnp.where(heads(), lines[line : line + 1], 0.0).astype(BF16)


FIRST, SECOND = (NEAR, INFO, FAR), (0, None, 16)


def fill_z(frame, room, rows, halo_a, halo_b):
    for halo, near, far in ((halo_a, COLS, COLS + 1), (halo_b, -1, -2)):
        for u in (2, 3):
            fill(room, halo, *rows, frame.row(u), place(u, near), place(u, far), ())


def fill_x(frame, room, rows, halo, near, far):
    for v in range(-1, COLS + 1):
        beyond = {-1: -2, COLS: COLS + 1}.get(v)
        corner = () if beyond is None else (place(near, beyond), place(far, beyond))
        fill(room, halo, *rows, frame.col(v) + 1, place(near, v), place(far, v), corner)


def half_1(frame, u, weights, signals, table, factor, halos, room, room2, degree, first, ghost_degree, ghost_first):
    for number, (halo, at, gu, gv) in enumerate(ghost_blocks(frame, u, *halos)):
        pack = halo[at, NEAR:INFO].astype(F32)
        value = piece(pack, HIGH) + piece(pack, LOW)
        near = ghost_product(frame, halo, at, place(gu, gv), room, 32)
        sums = near[0:16] + (piece(pack, OWN_HIGH) + piece(pack, OWN_LOW))
        line = jnp.broadcast_to(halo[at, INFO:FAR].astype(F32)[DEGREE : DEGREE + 1], (16, 128))
        around = jnp.broadcast_to(near[16:17], (16, 128)) + (piece(line, 0) + piece(line, 1))
        result = factor * (around * value - sums) - value
        ghost_degree[number] = around
        ghost_first[number] = result
        place_edge(room2, place(gu, gv), jnp.where(lanes() < EDGE, result * bound_row(halo, at), 0.0))
    row = frame.row(u)
    for v in range(COLS):
        col = frame.col(v)
        alive = alive_of(table, row, col)
        value = signals[row, col] * alive
        sums = own_product(weights, table, row, col, room, with_head(value, alive))
        around = jnp.broadcast_to(sums[16:17], (16, 128)) * alive
        result = factor * (around * value - sums[0:16] * alive) - value
        degree[v] = around
        first[v] = result
        place_edge(room2, place(u, v), result * inside_of(table, row, col))


def half_3(frame, u, weights, table, factor, halos, fresh, room, room2, degree, first, second, products, third, ghost_degree, ghost_first):
    values = ghost_blocks(frame, u, *fresh)
    for number, (halo, at, gu, gv) in enumerate(ghost_blocks(frame, u, *halos)):
        pack = values[number][0][at, 0:16].astype(F32)
        value = piece(pack, HIGH) + piece(pack, LOW)
        sums = ghost_product(frame, halo, at, place(gu, gv), room, 16) + (piece(pack, OWN_HIGH) + piece(pack, OWN_LOW))
        result = 2.0 * (factor * (ghost_degree[number] * value - sums) - value) - ghost_first[number]
        place_edge(room2, place(gu, gv), jnp.where(lanes() < EDGE, result * bound_row(halo, at), 0.0))
    row = frame.row(u)
    for v in range(COLS):
        col = frame.col(v)
        near = near_input(table, row, col, room, 16)
        sums = products[u - 2, v] + jnp.dot(near, weights[row, col, 256:384], preferred_element_type=F32)
        value = second[u - 2, v]
        result = 2.0 * (factor * (degree[v] * value - sums * alive_of(table, row, col)) - value) - first[v]
        third[v] = result
        place_edge(room2, place(u, v), result * inside_of(table, row, col))


def carry_rooms(room, room_in, room2, room2_in):
    for v in range(-2, COLS + 2):
        for u in (2, 3):
            room[place(u, v)] = room_in[place(u, v)]
    for v in range(-1, COLS + 1):
        for u in (1, 2):
            room2[place(u, v)] = room2_in[place(u, v)]


def step_1a(
    weights, signals, table, spectral, from_a, from_b, from_s, room, room2, degree, first, ghost_degree, ghost_first
):
    frame = Frame()
    factor = 2.0 / jnp.full((16, 128), spectral[0])
    room[ZERO] = jnp.zeros((32, 128), BF16)
    for u in (2, 3):
        row = frame.row(u)
        for v in range(COLS):
            col, at = frame.col(v), place(u, v)
            inside = inside_of(table, row, col)
            place_edge(room, at, signals[row, col] * inside)
            room[at, 16:32] = jnp.where(heads(), repeat(inside), 0.0).astype(BF16)
    fill_z(frame, room, FIRST, from_a, from_b)
    fill_x(frame, room, FIRST, from_s, 1, 0)
    halos = (from_a, from_b, from_s)
    half_1(frame, 2, weights, signals, table, factor, halos, room, room2, degree, first, ghost_degree, ghost_first)


def step_1b(
    weights, signals, table, spectral, from_a, from_b, from_x, room_in, room2_in, degree_a, first_a,
    degree, first, ghost_degree, ghost_first, second, out_a, out_b, room, room2,
):
    frame = Frame()
    factor = 2.0 / jnp.full((16, 128), spectral[0])
    room[ZERO] = jnp.zeros((32, 128), BF16)
    room2[ZERO] = jnp.zeros((16, 128), BF16)
    carry_rooms(room, room_in, room2, room2_in)
    fill_x(frame, room, FIRST, from_x, 4, 5)
    halos = (from_a, from_b, from_x)
    half_1(frame, 3, weights, signals, table, factor, halos, room, room2, degree, first, ghost_degree, ghost_first)
    for u, degrees, firsts in ((2, degree_a, first_a), (3, degree, first)):
        row = frame.row(u)
        for v in range(COLS):
            col = frame.col(v)
            value = firsts[v]
            sums = own_product(weights, table, row, col, room2, value.astype(BF16))
            alive = alive_of(table, row, col)
            result = 2.0 * (factor * (degrees[v] * value - sums * alive) - value)
            second[u - 2, v] = result - signals[row, col] * alive
    for out, v, v2 in ((out_a, COLS - 1, COLS - 2), (out_b, 0, 1)):
        for u in (2, 3):
            message_2(out, frame.row(u), second, weights, table, u, v, u, v2, frame)


def pack_x2(second, weights, table, out_s, out_x, products):
    frame = Frame()
    for out, u in ((out_s, 2), (out_x, 3)):
        for v in range(COLS):
            products[u - 2, v] = message_2(out, frame.col(v) + 1, second, weights, table, u, v, 5 - u, v, frame)


def step_3a(
    weights, table, spectral, from_a, from_b, from_s, new_a, new_b, new_s,
    degree, first, second, products, ghost_degree, ghost_first, room, room2, third,
):
    frame = Frame()
    factor = 2.0 / jnp.full((16, 128), spectral[0])
    room[ZERO] = jnp.zeros((16, 128), BF16)
    for u in (2, 3):
        for v in range(COLS):
            place_edge(room, place(u, v), second[u - 2, v] * inside_of(table, frame.row(u), frame.col(v)))
    fill_z(frame, room, SECOND, new_a, new_b)
    fill_x(frame, room, SECOND, new_s, 1, 0)
    half_3(
        frame, 2, weights, table, factor, (from_a, from_b, from_s), (new_a, new_b, new_s), room, room2,
        degree, first, second, products, third, ghost_degree, ghost_first,
    )


def step_3b(
    weights, signals, table, spectral, scales, from_a, from_b, from_x, new_a, new_b, new_x, room_in, room2_in,
    degree_a, degree, first_a, first, second, products, ghost_degree, ghost_first, third_a,
    partial, third, fourths, room, room2,
):
    frame = Frame()
    factor = 2.0 / jnp.full((16, 128), spectral[0])
    room[ZERO] = jnp.zeros((16, 128), BF16)
    room2[ZERO] = jnp.zeros((16, 128), BF16)
    carry_rooms(room, room_in, room2, room2_in)
    fill_x(frame, room, SECOND, new_x, 4, 5)
    half_3(
        frame, 3, weights, table, factor, (from_a, from_b, from_x), (new_a, new_b, new_x), room, room2,
        degree, first, second, products, third, ghost_degree, ghost_first,
    )
    count = scales.shape[0]
    squares = [jnp.zeros((16, 128), F32) for _ in range(count)]
    for u, degrees, firsts, thirds in ((2, degree_a, first_a, third_a), (3, degree, first, third)):
        row = frame.row(u)
        for v in range(COLS):
            col = frame.col(v)
            value = thirds[v]
            sums = own_product(weights, table, row, col, room2, value.astype(BF16))
            alive = alive_of(table, row, col)
            fourth = 2.0 * (factor * (degrees[v] * value - sums * alive) - value) - second[u - 2, v]
            fourths[u - 2, v] = fourth
            terms = (signals[row, col] * alive, firsts[v], second[u - 2, v], value, fourth)
            for scale, total in enumerate(weighted(scales, terms)):
                squares[scale] = squares[scale] + total * total
    block = jnp.concatenate(squares + [jnp.zeros((128 - 16 * count, 128), F32)], axis=0)
    line = jnp.sum(jnp.transpose(block), axis=0, keepdims=True)
    partial[...] = jnp.broadcast_to(line[None], partial.shape)


def weighted(scales, terms):
    for scale in range(scales.shape[0]):
        total = (0.5 * scales[scale, 0]) * terms[0]
        for order in range(1, len(terms)):
            total = total + scales[scale, order] * terms[order]
        yield total


def combine(signals, table, scales, first_a, first_b, second, third_a, third_b, fourths, coefficients):
    frame = Frame()
    for u, firsts, thirds in ((2, first_a, third_a), (3, first_b, third_b)):
        row = frame.row(u)
        for v in range(COLS):
            col = frame.col(v)
            terms = (signals[row, col] * alive_of(table, row, col), firsts[v], second[u - 2, v], thirds[v], fourths[u - 2, v])
            for scale, total in enumerate(weighted(scales, terms)):
                coefficients[scale, row, col] = total


def in_hbm(*arrays):
    return tuple(pltpu.with_memory_space_constraint(array, pltpu.MemorySpace.HBM) for array in arrays)


def in_vmem(*arrays):
    return tuple(pltpu.with_memory_space_constraint(array, pltpu.MemorySpace.VMEM) for array in arrays)


def in_smem(*arrays):
    return tuple(pltpu.with_memory_space_constraint(array, pltpu.MemorySpace.SMEM) for array in arrays)


def neighbour_pairs(devices, first):
    pairs = [(i, i + 1) for i in range(first, devices - 1, 2)]
    return pairs + [(j, i) for i, j in pairs]


def shape(dims, kind=BF16):
    return jax.ShapeDtypeStruct(dims, kind)


def shards(signals, tiles, tile_dir, tile_mask, live_rows, bound_rows, scale_coeffs, spectral_bound):
    devices_x, devices_z = lax.axis_size(GX), lax.axis_size("gy")
    devices = devices_x * devices_z
    scales, channels = scale_coeffs.shape[0], signals.shape[2]
    nodes = ROWS * COLS * 128 * devices

    def swap_z(a, b):
        return (
            lax.ppermute(a, "gy", neighbour_pairs(devices_z, 0)),
            lax.ppermute(b, "gy", neighbour_pairs(devices_z, 1)),
        )

    def swap_x(s, x):
        far = lax.ppermute(x, GX, neighbour_pairs(devices_x, 1))
        return lax.ppermute(s, "gx_2", [(0, 1), (1, 0)]), far

    def call(body, outs, in_specs, out_specs, scratch=(), aliases=None, flops=1000, mib=16):
        return pl.pallas_call(
            body,
            out_shape=outs,
            in_specs=in_specs,
            out_specs=out_specs,
            scratch_shapes=list(scratch),
            input_output_aliases=aliases or {},
            compiler_params=params(mib),
            cost_estimate=cost(flops),
        )

    tile_dir, tile_mask = jnp.swapaxes(tile_dir, 1, 2), jnp.swapaxes(tile_mask, 1, 2)
    local = (tiles, signals, tile_dir, tile_mask, live_rows, bound_rows)
    rooms = [
        pltpu.VMEM((2, ROWS, SLOTS, EDGE, 128), BF16),
        pltpu.VMEM(signals.shape, F32),
        pltpu.SMEM(tile_dir.shape, jnp.int32),
        pltpu.SMEM(tile_dir.shape, jnp.int32),
        pltpu.SMEM(live_rows.shape, jnp.int32),
        pltpu.SMEM(live_rows.shape, jnp.int32),
        pltpu.SemaphoreType.DMA((2,)),
        pltpu.SemaphoreType.DMA((5,)),
    ]
    wide_rooms = [pltpu.VMEM((2, COLS, SLOTS, EDGE, 128), BF16)] + rooms[1:]
    message_z, message_x = pltpu.VMEM((ROWS, LONG, 128), BF16), pltpu.VMEM((COLS + 2, LONG, 128), BF16)
    a, b = call(pack_z, [message_z] * 2, [HBM] * 6, [VMEM] * 2, rooms)(*in_hbm(*local))
    s, x = call(pack_x, [message_x] * 2, [HBM] * 6, [VMEM] * 2, wide_rooms, flops=1 << 21)(*in_hbm(*local))
    a, b = swap_z(a, b)
    corner_room = [pltpu.VMEM((2, 2, LONG, 128), BF16), pltpu.SemaphoreType.DMA((2, 2))]
    s, x = call(
        corners_1, [message_x] * 2, [VMEM] * 2 + [ANY] * 2, [ANY] * 2, corner_room, {2: 0, 3: 1}
    )(a, b, *in_vmem(s, x))
    s, x = swap_x(s, x)

    weights, table, scale_table = call(
        turn_tiles,
        [
            shape((ROWS, COLS, 384, 128)),
            pltpu.SMEM((ROWS, SLOTS + 2, COLS), jnp.int32),
            pltpu.SMEM(scale_coeffs.shape, F32),
        ],
        [VMEM] + [HBM] * 5,
        [VMEM, SMEM, SMEM],
        rooms[2:6] + [pltpu.SemaphoreType.DMA((5,))],
        flops=1 << 24,
    )(tiles, *in_hbm(*local[2:], scale_coeffs))
    table, scale_table = in_smem(table, scale_table)
    half = shape((COLS, channels, 128), F32)
    extra = shape((COLS + 4, channels, 128), F32)
    wide_room, room = shape((ZERO + 1, 32, 128)), shape((ZERO + 1, 16, 128))
    wide_scratch, scratch = pltpu.VMEM((ZERO + 1, 32, 128), BF16), pltpu.VMEM((ZERO + 1, 16, 128), BF16)
    short_z, short_x = pltpu.VMEM((ROWS, 32, 128), BF16), pltpu.VMEM((COLS + 2, 32, 128), BF16)
    full = shape((ROWS, COLS, channels, 128), F32)
    room_1, room_2, degree_a, first_a, ghost_degree_a, ghost_first_a = call(
        step_1a, [wide_room, room, half, half, extra, extra], [VMEM] * 2 + [SMEM] * 2 + [VMEM] * 3, [VMEM] * 6, flops=1 << 25
    )(weights, signals, table, spectral_bound, a, b, s)
    degree_b, first_b, ghost_degree_b, ghost_first_b, second, a2, b2 = call(
        step_1b,
        [half, half, extra, extra, full, short_z, short_z],
        [VMEM] * 2 + [SMEM] * 2 + [VMEM] * 7,
        [VMEM] * 7,
        [wide_scratch, scratch],
        flops=1 << 26,
    )(weights, signals, table, spectral_bound, a, b, x, room_1, room_2, degree_a, first_a)
    s2, x2, products = call(
        pack_x2, [short_x] * 2 + [full], [VMEM, VMEM, SMEM], [VMEM] * 3, flops=1 << 20
    )(second, weights, table)
    a2, b2 = swap_z(a2, b2)
    corner_room = [pltpu.VMEM((2, 2, 32, 128), BF16), pltpu.SemaphoreType.DMA((2, 2))]
    s2, x2 = call(
        corners_2, [short_x] * 2, [VMEM] * 2 + [ANY] * 2, [ANY] * 2, corner_room, {2: 0, 3: 1}
    )(a2, b2, *in_vmem(s2, x2))
    s2, x2 = swap_x(s2, x2)
    room_1, room_2, third_a = call(
        step_3a, [room, room, half], [VMEM, SMEM, SMEM] + [VMEM] * 12, [VMEM] * 3, flops=1 << 25
    )(
        weights, table, spectral_bound, a, b, s, a2, b2, s2, degree_a, first_a, second, products,
        ghost_degree_a, ghost_first_a,
    )
    partial, third_b, fourth = call(
        step_3b,
        [pltpu.VMEM((devices, 1, 128), F32), half, full],
        [VMEM] * 2 + [SMEM] * 3 + [VMEM] * 17,
        [VMEM] * 3,
        [scratch, scratch],
        flops=1 << 26,
    )(
        weights, signals, table, spectral_bound, scale_table, a, b, x, a2, b2, x2, room_1, room_2,
        degree_a, degree_b, first_a, first_b, second, products, ghost_degree_b, ghost_first_b, third_a,
    )
    totals = call(
        combine,
        [shape((scales, ROWS, COLS, channels, 128), F32)],
        [VMEM, SMEM, SMEM] + [VMEM] * 6,
        [VMEM],
        flops=1 << 24,
    )(signals, table, scale_table, first_a, first_b, second, third_a, third_b, fourth)[0]
    gathered = lax.all_to_all(partial, GX_GY, 0, 0)
    energy = jnp.sum(gathered, axis=(0, 1))[: scales * channels].reshape(scales, channels) / nodes
    return (totals, energy)


def solution(mesh):
    torus = Mesh(mesh.devices.reshape(4, 4, 2, mesh.shape["gy"]), ("gx_0", "gx_1", "gx_2", "gy"))
    placed = (
        P(GX, "gy", None, None),
        P(GX, "gy", None, None, None),
        P(GX, "gy", None),
        P(GX, "gy", None),
        P(GX, "gy"),
        P(GX, "gy"),
        P(),
        P(),
    )
    return jax.shard_map(
        shards,
        mesh=torus,
        in_specs=placed,
        out_specs=(P(None, GX, "gy", None, None), P()),
        check_vma=False,
    )
```

time: 61.4 us -> 57.4 us (0.935)
  blocking collectives: 25 us -> 0 us
  starting transfers between devices: 16.4 us -> 31.5 us
  waiting for transfers between devices: 3.95 us -> 10.1 us
    all_to_all x1 -> x0, blocking collectives: 25 us -> none  [shards(): gathered = lax.all_to_all(partial, GX_GY, 0, 0)]
    all_to_all x0 -> x1, starting transfers between devices: none -> 15.1 us  [shards(): gathered = lax.all_to_all(partial, GX_GY, 0, 0)]
    all_to_all x0 -> x1, waiting for transfers between devices: none -> 8.46 us  [shards(): gathered = lax.all_to_all(partial, GX_GY, 0, 0)]
    ppermute x2, waiting for transfers between devices: 3.94 us -> 1.49 us  [swap_x(): far = lax.ppermute(x, GX, neighbour_pairs(devices_x, 1))]
    pallas_call x7 -> x8, Pallas kernels: 10.6 us -> 10.8 us  [the longest x1 3.01 us: shards(): call(turn_tiles, [shape((ROWS, COLS, 384, 128)), pltpu.SMEM((ROWS, SLOTS...]
  transfers between devices with their start and end apart: 8 -> 9, of which waited for: 2 -> 3; matrix products, arithmetic and copies ran while one was open for 0% -> 0% of each run, Pallas kernels for 12% -> 14%
where the time goes in v4:
time: 57.4 us; the launch traced here: 57.1 us
  starting transfers between devices  31.5 us (55%)
  Pallas kernels  13.3 us (23%)
  waiting for transfers between devices  10.1 us (18%)
  between operations  1.43 us (2%)
  local copies, waits for them, and re-layouts  0.68 us (1%)
    all_to_all x1, starting transfers between devices, shards(): gathered = lax.all_to_all(partial, GX_GY, 0, 0)  15.1 us
    all_to_all x1, waiting for transfers between devices, shards(): gathered = lax.all_to_all(partial, GX_GY, 0, 0)  8.46 us
    ppermute x2, starting transfers between devices, swap_z(): lax.ppermute(a, 'gy', neighbour_pairs(devices_z, 0))  7.09 us
    ppermute x2, starting transfers between devices, swap_x(): far = lax.ppermute(x, GX, neighbour_pairs(devices_x, 1))  6.68 us
    pallas_call x1, Pallas kernels, shards(): call(turn_tiles, [shape((ROWS, COLS, 384, 128)), pltpu.SMEM((ROWS, SLOTS...  3.01 us
    pallas_call x1, Pallas kernels, shards(): call(pack_x, [message_x] * 2, [HBM] * 6, [VMEM] * 2, wide_rooms, flops=1...  2 us
    pallas_call x1, Pallas kernels, shards(): call(step_3b, [pltpu.VMEM((devices, 1, 128), F32), half, full], [VMEM] *...  1.99 us
    ppermute x2, waiting for transfers between devices, swap_x(): far = lax.ppermute(x, GX, neighbour_pairs(devices_x, 1))  1.49 us
  transfers between devices with their start and end apart: 9, of which 3 were waited for; matrix products, arithmetic and copies ran while one was open for 0% of the time, Pallas kernels for 14%

profile of v4, /device:TPU:1, one launch (start us, length us, event | category | flops | bytes accessed | tf_op | source)
XLA Modules:
  0.0 57.1 jit_solution(8251023663322905600)
XLA Ops:
  0.6 1.4 %shard_map.96 = (bf16[2,80,128]{2,1,0:T(8,128)(2,1)S(1)}, bf16[2,80,128]{2,1,0:T(8,128)(2,1)S(1)}) custom-call(bf16[2,8,4,128,128]{4,3,2,1,0:T(8,128)(2,1)} %tiles.5, f32[2,8,16,128]{3,2,1,0:T(8,128)} %signals.11, s32[2,4,8]{2,1,0:T(4,128)} %bitcast.2, s32[2,4,8]{2,1,0:T(4,128)} %bitcast.5, s32[2,8]{1,0:T(2,128)} %live.5, s32[2,8]{1,0:T(2,128)} %bound.5), custom_call_target="tpu_custom_call" | custom-call | flops 1000 | bytes 1048576 | tf_op jit(solution)/shard_map/pallas_call | solution.py:605
  2.1 2.5 %collective-permute-start = (bf16[2,80,128]{2,1,0:T(8,128)(2,1)S(1)}, bf16[2,80,128]{2,1,0:T(8,128)(2,1)S(1)}, u32[]{:S(2)}, u32[]{:S(2)}) collective-permute-start(bf16[2,80,128]{2,1,0:T(8,128)(2,1)S(1)} %get-tuple-element.38), channel_id=1, source_target_pairs={{0,1},{2,3},{1,0},{3,2},{4,5},{6,7},{5,4},{7,6},{8,9},{10,11},{9,8... | collective-permute-start | bytes 122888 | tf_op jit(solution)/shard_map/ppermute | solution.py:571
  4.6 0.8 %collective-permute-start.1 = (bf16[2,80,128]{2,1,0:T(8,128)(2,1)S(1)}, bf16[2,80,128]{2,1,0:T(8,128)(2,1)S(1)}, u32[]{:S(2)}, u32[]{:S(2)}) collective-permute-start(bf16[2,80,128]{2,1,0:T(8,128)(2,1)S(1)} %get-tuple-element.39), channel_id=1, source_target_pairs={{1,2},{2,1},{5,6},{6,5},{9,10},{10,9},{13,14},{14,13},{17,18},{18,... | collective-permute-start | bytes 122888 | tf_op jit(solution)/shard_map/ppermute | solution.py:572
  5.4 2.0 %shard_map.97 = (bf16[10,80,128]{2,1,0:T(8,128)(2,1)S(1)}, bf16[10,80,128]{2,1,0:T(8,128)(2,1)S(1)}) custom-call(bf16[2,8,4,128,128]{4,3,2,1,0:T(8,128)(2,1)} %tiles.5, f32[2,8,16,128]{3,2,1,0:T(8,128)} %signals.11, s32[2,4,8]{2,1,0:T(4,128)} %bitcast.3, s32[2,4,8]{2,1,0:T(4,128)} %bitcast.6, s32[2,8]{1,0:T(2,128)} %live.5, s32[2,8]{1,0:T(2,128)} %bound.5), custom_call_target="tpu_custom_call" | custom-call | flops 2097152 | bytes 1048576 | tf_op jit(solution)/shard_map/pallas_call | solution.py:606
  7.4 0.2 shard_map.98
  7.7 1.0 %collective-permute-start.2 = (bf16[10,80,128]{2,1,0:T(8,128)(2,1)S(1)}, bf16[10,80,128]{2,1,0:T(8,128)(2,1)S(1)}, u32[]{:S(2)}, u32[]{:S(2)}) collective-permute-start(bf16[10,80,128]{2,1,0:T(8,128)(2,1)S(1)} %get-tuple-element.42), channel_id=1, source_target_pairs={{0,4},{4,0},{1,5},{5,1},{2,6},{6,2},{3,7},{7,3},{8,12},{12,8},{9,1... | collective-permute-start | bytes 614408 | tf_op jit(solution)/shard_map/ppermute | solution.py:577
  8.7 3.1 %collective-permute-start.3 = (bf16[10,80,128]{2,1,0:T(8,128)(2,1)S(1)}, bf16[10,80,128]{2,1,0:T(8,128)(2,1)S(1)}, u32[]{:S(2)}, u32[]{:S(2)}) collective-permute-start(bf16[10,80,128]{2,1,0:T(8,128)(2,1)S(1)} %get-tuple-element.44), channel_id=1, source_target_pairs={{4,8},{12,16},{20,24},{28,32},{36,40},{44,48},{52,56},{60,64},{68,... | collective-permute-start | bytes 614408 | tf_op jit(solution)/shard_map/ppermute | solution.py:576
  12.5 3.0 %shard_map.95 = (bf16[2,8,384,128]{3,2,1,0:T(8,128)(2,1)S(1)}, s32[2,6,8]{2,1,0:T(8,128)S(4)}, f32[6,5]{1,0:T(8,128)S(4)}) custom-call(bf16[2,8,4,128,128]{4,3,2,1,0:T(8,128)(2,1)S(1)} %copy-done, s32[2,4,8]{2,1,0:T(4,128)} %bitcast.4, s32[2,4,8]{2,1,0:T(4,128)} %bitcast.7, s32[2,8]{1,0:T(2,128)} %live.5, s32[2,8]{1,0:T(2,128)} %bound.5, f32[6,5]{1,0:T(8,128)} %scales.1), custom_call_target="tpu_custom_call" | custom-call | flops 16777216 | bytes 1048576 | tf_op jit(solution)/shard_map/pallas_call | solution.py:614
  15.5 0.8 %shard_map.99 = (bf16[73,32,128]{2,1,0:T(8,128)(2,1)S(1)}, bf16[73,16,128]{2,1,0:T(8,128)(2,1)S(1)}, f32[8,16,128]{2,1,0:T(8,128)S(1)}, f32[8,16,128]{2,1,0:T(8,...) custom-call(bf16[2,8,384,128]{3,2,1,0:T(8,128)(2,1)S(1)} %get-tuple-element.37.weights, ...), custom_call_target="tpu_custom_call" | custom-call | flops 33554432 | bytes 1048576 | tf_op jit(solution)/shard_map/pallas_call | solution.py:633
  16.4 1.3 %shard_map.100 = (f32[8,16,128]{2,1,0:T(8,128)S(1)}, f32[8,16,128]{2,1,0:T(8,128)S(1)}, f32[12,16,128]{2,1,0:T(8,128)S(1)}, f32[12,16,128]{2,1,0:T(8,128)S(1)}, ...) custom-call(bf16[2,8,384,128]{3,2,1,0:T(8,128)(2,1)S(1)} %get-tuple-element.37.weight, ...), custom_call_target="tpu_custom_call" | custom-call | flops 67108864 | bytes 1048576 | tf_op jit(solution)/shard_map/pallas_call | solution.py:636
  17.7 4.5 %collective-permute-start.4 = (bf16[2,32,128]{2,1,0:T(8,128)(2,1)S(1)}, bf16[2,32,128]{2,1,0:T(8,128)(2,1)S(1)}, u32[]{:S(2)}, u32[]{:S(2)}) collective-permute-start(bf16[2,32,128]{2,1,0:T(8,128)(2,1)S(1)} %get-tuple-element.50), channel_id=1, source_target_pairs={{0,1},{2,3},{1,0},{3,2},{4,5},{6,7},{5,4},{7,6},{8,9},{10,11},{9,8... | collective-permute-start | bytes 49160 | tf_op jit(solution)/shard_map/ppermute | solution.py:571
  22.3 0.7 %collective-permute-start.5 = (bf16[2,32,128]{2,1,0:T(8,128)(2,1)S(1)}, bf16[2,32,128]{2,1,0:T(8,128)(2,1)S(1)}, u32[]{:S(2)}, u32[]{:S(2)}) collective-permute-start(bf16[2,32,128]{2,1,0:T(8,128)(2,1)S(1)} %get-tuple-element.51), channel_id=1, source_target_pairs={{1,2},{2,1},{5,6},{6,5},{9,10},{10,9},{13,14},{14,13},{17,18},{18,... | collective-permute-start | bytes 49160 | tf_op jit(solution)/shard_map/ppermute | solution.py:572
  22.9 0.4 shard_map.101
  23.3 0.1 collective-permute-done.4.from_a.new_a
  23.4 0.2 shard_map.102
  23.7 3.6 %collective-permute-start.7 = (bf16[10,32,128]{2,1,0:T(8,128)(2,1)S(1)}, bf16[10,32,128]{2,1,0:T(8,128)(2,1)S(1)}, u32[]{:S(2)}, u32[]{:S(2)}) collective-permute-start(bf16[10,32,128]{2,1,0:T(8,128)(2,1)S(1)} %get-tuple-element.59), channel_id=1, source_target_pairs={{4,8},{12,16},{20,24},{28,32},{36,40},{44,48},{52,56},{60,64},{68,... | collective-permute-start | bytes 245768 | tf_op jit(solution)/shard_map/ppermute | solution.py:576
  27.2 0.7 %shard_map.103 = (bf16[73,16,128]{2,1,0:T(8,128)(2,1)S(1)}, bf16[73,16,128]{2,1,0:T(8,128)(2,1)S(1)}, f32[8,16,128]{2,1,0:T(8,128)S(1)}) custom-call(bf16[2,8,384,128]{3,2,1,0:T(8,128)(2,1)S(1)} %get-tuple-element.37.weights, s32[2,6,8]{2,1,0:T(8,128)S(4)} %get-tuple-element.35.table, f32[1]{0:T(128)S(6)} %copy.18.spectral, ...), custom_call_target="tpu_custom_call" | custom-call | flops 33554432 | bytes 1048576 | tf_op jit(solution)/shard_map/pallas_call | solution.py:653
  27.9 1.5 %collective-permute-done.7.new_x = bf16[10,32,128]{2,1,0:T(8,128)(2,1)S(1)} collective-permute-done((bf16[10,32,128]{2,1,0:T(8,128)(2,1)S(1)}, bf16[10,32,128]{2,1,0:T(8,128)(2,1)S(1)}, u32[]{:S(2)}, u32[]{:S(2)}) %collective-permute-start.7) | collective-permute-done | bytes 81952 | tf_op jit(solution)/shard_map/ppermute | solution.py:576
  29.4 2.0 %shard_map.104 = (f32[128,1,128]{2,1,0:T(1,128)}, f32[8,16,128]{2,1,0:T(8,128)S(1)}, f32[2,8,16,128]{3,2,1,0:T(8,128)S(1)}) custom-call(bf16[2,8,384,128]{3,2,1,0:T(8,128)(2,1)S(1)} %get-tuple-element.37.weights, f32[2,8,16,128]{3,2,1,0:T(8,128)S(1)} %copy-done.1, s32[2,6,8]{2,1,0:T(8,128)S(4)} %get-tuple-element.35.table, f32[1]{0:T(128)S(6)} %copy.18.spectral, ...), custom_call_target="tpu_custom_call" | custom-call | flops 67108864 | bytes 1048576 | tf_op jit(solution)/shard_map/pallas_call | solution.py:659
  31.4 15.1 %all-to-all-start = ((f32[128,1,128]{2,1,0:T(1,128)}), f32[128,1,128]{2,1,0:T(1,128)S(1)}, u32[]{:S(2)}, u32[]{:S(2)}) async-start(f32[128,1,128]{2,1,0:T(1,128)} %get-tuple-element.67), calls=%async_computation | async-start | bytes 131072 | tf_op jit(solution)/shard_map/all_to_all | solution.py:677
  46.6 1.3 %shard_map.105 = f32[6,2,8,16,128]{4,3,2,1,0:T(8,128)} custom-call(f32[2,8,16,128]{3,2,1,0:T(8,128)S(1)} %copy-done.1, s32[2,6,8]{2,1,0:T(8,128)S(4)} %get-tuple-element.35.table, f32[6,5]{1,0:T(8,128)S(4)} %get-tuple-element.36.scales, f32[8,16,128]{2,1,0:T(8,128)S(1)} %get-tuple-element.43.first_a.first, ...), custom_call_target="tpu_custom_call" | custom-call | flops 16777216 | bytes 1048576 | tf_op jit(solution)/shard_map/pallas_call | solution.py:670
  47.8 8.5 %all-to-all-done = f32[128,1,128]{2,1,0:T(1,128)S(1)} async-done(((f32[128,1,128]{2,1,0:T(1,128)}), f32[128,1,128]{2,1,0:T(1,128)S(1)}, u32[]{:S(2)}, u32[]{:S(2)}) %all-to-all-start) | async-done | bytes 65568 | tf_op jit(solution)/shard_map/all_to_all | solution.py:677
  56.3 0.2 reduce_sum.9
  56.4 0.7 %div.10 = f32[6,16]{1,0:T(8,128)} reshape(f32[96]{0:T(128)S(1)} %slice_multiply_fusion) | data formatting | bytes 768 | tf_op jit(solution)/shard_map/div | solution.py:678
  (12 shorter events, 0.1 us)
Async XLA Ops:
  0.6 11.9 %copy-start = (bf16[2,8,4,128,128]{4,3,2,1,0:T(8,128)(2,1)S(1)}, bf16[2,8,4,128,128]{4,3,2,1,0:T(8,128)(2,1)}, u32[]{:S(2)}) copy-start(bf16[2,8,4,128,128]{4,3,2,1,0:T(8,128)(2,1)} %tiles.5) | copy-start | bytes 6291460
  2.1 5.3 %collective-permute-start = (bf16[2,80,128]{2,1,0:T(8,128)(2,1)S(1)}, bf16[2,80,128]{2,1,0:T(8,128)(2,1)S(1)}, u32[]{:S(2)}, u32[]{:S(2)}) collective-permute-start(bf16[2,80,128]{2,1,0:T(8,128)(2,1)S(1)} %get-tuple-element.38), channel_id=1, source_target_pairs={{0,1},{2,3},{1,0},{3,2},{4,5},{6,7},{5,4},{7,6},{8,9},{10,11},{9,8... | collective-permute-start | bytes 122888 | tf_op jit(solution)/shard_map/ppermute | solution.py:571
  4.6 10.9 %copy-start.1 = (f32[2,8,16,128]{3,2,1,0:T(8,128)S(1)}, f32[2,8,16,128]{3,2,1,0:T(8,128)}, u32[]{:S(2)}) copy-start(f32[2,8,16,128]{3,2,1,0:T(8,128)} %signals.11) | copy-start | bytes 393220
  4.6 2.8 %collective-permute-start.1 = (bf16[2,80,128]{2,1,0:T(8,128)(2,1)S(1)}, bf16[2,80,128]{2,1,0:T(8,128)(2,1)S(1)}, u32[]{:S(2)}, u32[]{:S(2)}) collective-permute-start(bf16[2,80,128]{2,1,0:T(8,128)(2,1)S(1)} %get-tuple-element.39), channel_id=1, source_target_pairs={{1,2},{2,1},{5,6},{6,5},{9,10},{10,9},{13,14},{14,13},{17,18},{18,... | collective-permute-start | bytes 122888 | tf_op jit(solution)/shard_map/ppermute | solution.py:572
  7.7 7.8 %collective-permute-start.2 = (bf16[10,80,128]{2,1,0:T(8,128)(2,1)S(1)}, bf16[10,80,128]{2,1,0:T(8,128)(2,1)S(1)}, u32[]{:S(2)}, u32[]{:S(2)}) collective-permute-start(bf16[10,80,128]{2,1,0:T(8,128)(2,1)S(1)} %get-tuple-element.42), channel_id=1, source_target_pairs={{0,4},{4,0},{1,5},{5,1},{2,6},{6,2},{3,7},{7,3},{8,12},{12,8},{9,1... | collective-permute-start | bytes 614408 | tf_op jit(solution)/shard_map/ppermute | solution.py:577
  8.7 7.6 %collective-permute-start.3 = (bf16[10,80,128]{2,1,0:T(8,128)(2,1)S(1)}, bf16[10,80,128]{2,1,0:T(8,128)(2,1)S(1)}, u32[]{:S(2)}, u32[]{:S(2)}) collective-permute-start(bf16[10,80,128]{2,1,0:T(8,128)(2,1)S(1)} %get-tuple-element.44), channel_id=1, source_target_pairs={{4,8},{12,16},{20,24},{28,32},{36,40},{44,48},{52,56},{60,64},{68,... | collective-permute-start | bytes 614408 | tf_op jit(solution)/shard_map/ppermute | solution.py:576
  17.7 5.7 %collective-permute-start.4 = (bf16[2,32,128]{2,1,0:T(8,128)(2,1)S(1)}, bf16[2,32,128]{2,1,0:T(8,128)(2,1)S(1)}, u32[]{:S(2)}, u32[]{:S(2)}) collective-permute-start(bf16[2,32,128]{2,1,0:T(8,128)(2,1)S(1)} %get-tuple-element.50), channel_id=1, source_target_pairs={{0,1},{2,3},{1,0},{3,2},{4,5},{6,7},{5,4},{7,6},{8,9},{10,11},{9,8... | collective-permute-start | bytes 49160 | tf_op jit(solution)/shard_map/ppermute | solution.py:571
  22.3 1.1 %collective-permute-start.5 = (bf16[2,32,128]{2,1,0:T(8,128)(2,1)S(1)}, bf16[2,32,128]{2,1,0:T(8,128)(2,1)S(1)}, u32[]{:S(2)}, u32[]{:S(2)}) collective-permute-start(bf16[2,32,128]{2,1,0:T(8,128)(2,1)S(1)} %get-tuple-element.51), channel_id=1, source_target_pairs={{1,2},{2,1},{5,6},{6,5},{9,10},{10,9},{13,14},{14,13},{17,18},{18,... | collective-permute-start | bytes 49160 | tf_op jit(solution)/shard_map/ppermute | solution.py:572
  23.6 3.7 %collective-permute-start.6 = (bf16[10,32,128]{2,1,0:T(8,128)(2,1)S(1)}, bf16[10,32,128]{2,1,0:T(8,128)(2,1)S(1)}, u32[]{:S(2)}, u32[]{:S(2)}) collective-permute-start(bf16[10,32,128]{2,1,0:T(8,128)(2,1)S(1)} %get-tuple-element.54), channel_id=1, source_target_pairs={{0,4},{4,0},{1,5},{5,1},{2,6},{6,2},{3,7},{7,3},{8,12},{12,8},{9,1... | collective-permute-start | bytes 245768 | tf_op jit(solution)/shard_map/ppermute | solution.py:577
  23.7 5.8 %collective-permute-start.7 = (bf16[10,32,128]{2,1,0:T(8,128)(2,1)S(1)}, bf16[10,32,128]{2,1,0:T(8,128)(2,1)S(1)}, u32[]{:S(2)}, u32[]{:S(2)}) collective-permute-start(bf16[10,32,128]{2,1,0:T(8,128)(2,1)S(1)} %get-tuple-element.59), channel_id=1, source_target_pairs={{4,8},{12,16},{20,24},{28,32},{36,40},{44,48},{52,56},{60,64},{68,... | collective-permute-start | bytes 245768 | tf_op jit(solution)/shard_map/ppermute | solution.py:576
  31.4 24.9 %all-to-all-start = ((f32[128,1,128]{2,1,0:T(1,128)}), f32[128,1,128]{2,1,0:T(1,128)S(1)}, u32[]{:S(2)}, u32[]{:S(2)}) async-start(f32[128,1,128]{2,1,0:T(1,128)} %get-tuple-element.67), calls=%async_computation | async-start | bytes 131072 | tf_op jit(solution)/shard_map/all_to_all | solution.py:677

commit v5 on v4

--- a/solution.py
+++ b/solution.py
@@ -1,3 +1,5 @@
+import functools
+
 import jax
 import jax.numpy as jnp
 from jax import lax
@@ -138,7 +140,9 @@
     return copies
 
 
-def pack_z(tiles, signals, dirs, masks, live, bound, out_a, out_b, raw, signals_v, dirs_s, masks_s, live_s, bound_s, sem, sem2):
+def pack_z(
+    tiles, signals, dirs, masks, live, bound, out_a, out_b, dirs_s, masks_s, live_s, bound_s, raw, signals_v, sem, sem2
+):
     refs = (signals_v, dirs_s, masks_s, live_s, bound_s)
     copies = fetch((signals, dirs, masks, live, bound), refs, sem2)
     odd = odd_z()
@@ -152,23 +156,17 @@
         right = odd == which
         col, col2 = jnp.where(right, COLS - 1, 0), jnp.where(right, COLS - 2, 1)
         for row in range(ROWS):
-            block_message(out, row, refs, raw[which, row], row, col, row, col2)
-
-
-def pack_x(tiles, signals, dirs, masks, live, bound, out_s, out_b, raw, signals_v, dirs_s, masks_s, live_s, bound_s, sem, sem2):
-    refs = (signals_v, dirs_s, masks_s, live_s, bound_s)
-    copies = fetch((signals, dirs, masks, live, bound), refs, sem2)
+            block_message(out, row, refs, [raw[which, row, slot] for slot in range(SLOTS)], row, col, row, col2)
+
+
+def pack_x(tiles, signals, dirs, masks, live, bound, out_s, out_b):
+    refs = (signals, dirs, masks, live, bound)
     core = odd_core()
-    for which in range(2):
-        row = jnp.where(core == which, 1, 0)
-        copies.append(pltpu.make_async_copy(tiles.at[row, :, :, 0:EDGE, :], raw.at[which], sem.at[which]))
-        copies[-1].start()
-    for copy in copies:
-        copy.wait()
     for which, out in enumerate((out_s, out_b)):
         row = jnp.where(core == which, 1, 0)
         for col in range(COLS):
-            block_message(out, 1 + col, refs, raw[which, col], row, col, 1 - row, col)
+            raw = [tiles[row, col, slot, 0:EDGE] for slot in range(SLOTS)]
+            block_message(out, 1 + col, refs, raw, row, col, 1 - row, col)
 
 
 def place_corners(from_a, from_b, out_s, out_b, room, sem, far, info_at):
@@ -268,7 +266,8 @@
 
 def own_product(weights, table, row, col, room, own):
     near = near_input(table, row, col, room, own.shape[0])
-    return jnp.dot(jnp.concatenate([own, own, near], axis=1), weights[row, col], preferred_element_type=F32)
+    product = jnp.dot(jnp.concatenate([own, own], axis=1), weights[0][row, col], preferred_element_type=F32)
+    return product + jnp.dot(near, weights[1][row, col], preferred_element_type=F32)
 
 
 def alive_of(table, row, col):
@@ -291,7 +290,7 @@
     row, col = frame.row(u), frame.col(v)
     value = second[u - 2, v]
     own = value.astype(BF16)
-    product = jnp.dot(jnp.concatenate([own, own], axis=1), weights[row, col, 0:256], preferred_element_type=F32)
+    product = jnp.dot(jnp.concatenate([own, own], axis=1), weights[0][row, col], preferred_element_type=F32)
     high, low = split(value * inside_of(table, row, col))
     own_high, own_low = split(product)
     out[at, 0:16] = merge([high.astype(F32), low, own_high.astype(F32), own_low]).astype(BF16)
@@ -299,27 +298,32 @@
     return product
 
 
-def turn_tiles(
-    tiles, dirs, masks, live, bound, scales, out, table, scales_out, dirs_s, masks_s, live_s, bound_s, sem
-):
-    refs = (dirs_s, masks_s, live_s, bound_s, scales_out)
-    for copy in fetch((dirs, masks, live, bound, scales), refs, sem):
-        copy.wait()
-
-    def one(block, carry):
-        row, col = block // COLS, block % COLS
-        total = jnp.zeros((128, 128), F32)
-        for slot in range(SLOTS):
-            own = jnp.where(dirs_s[row, slot, col] == 4, jnp.where(masks_s[row, slot, col] == 1, 1.0, 0.0), 0.0)
-            tile = tiles[row, col, slot]
-            total = total + tile.astype(F32) * own
-            out[row, col, 256 + EDGE * slot : 256 + EDGE * (slot + 1)] = jnp.transpose(tile)[0:EDGE]
-        high = total.astype(BF16)
-        out[row, col, 0:128] = jnp.transpose(high)
-        out[row, col, 128:256] = jnp.transpose((total - high.astype(F32)).astype(BF16))
-        return carry
-
-    lax.fori_loop(0, ROWS * COLS, one, 0)
+def turn_tiles(tiles, dirs_s, masks_s, live_s, bound_s, scales, corner_out, own_out, table, scales_out, sem):
+    copy = pltpu.make_async_copy(scales, scales_out, sem)
+    copy.start()
+    rows = lax.broadcasted_iota(jnp.int32, (128, 512), 0)
+    cols = lax.broadcasted_iota(jnp.int32, (128, 512), 1)
+    picked = jnp.where((rows // EDGE == cols // 128) & (rows % EDGE == cols % 128), 1.0, 0.0).astype(BF16)
+    same = jnp.where(rows[:, 0:128] == cols[:, 0:128], 1.0, 0.0)
+    for row in range(ROWS):
+        for col in range(COLS):
+            joined = jnp.concatenate([tiles[row, col, slot] for slot in range(SLOTS)], axis=1)
+            owned = []
+            for slot in range(SLOTS):
+                own = jnp.where(dirs_s[row, slot, col] == 4, jnp.where(masks_s[row, slot, col] == 1, 1.0, 0.0), 0.0)
+                owned.append((same * own).astype(BF16))
+            total = lax.dot_general(
+                jnp.concatenate(owned, axis=1), joined, (((1,), (1,)), ((), ())), preferred_element_type=F32
+            )
+            high, low = split(total)
+            own_out[row, col, 0:128] = high
+            own_out[row, col, 128:256] = low.astype(BF16)
+            if row == 0:
+                product = lax.dot_general(picked, joined, (((1,), (1,)), ((), ())), preferred_element_type=F32)
+                corner_out[row, col] = product.astype(BF16)
+            else:
+                for slot in range(SLOTS):
+                    corner_out[row, col, EDGE * slot : EDGE * (slot + 1)] = jnp.transpose(tiles[row, col, slot])[0:EDGE]
     core, odd = odd_core(), odd_z()
     down, right = (2 * core - 1) * WIDE, 1 - 2 * odd
     for row in range(ROWS):
@@ -333,6 +337,7 @@
                 table[row, slot, col] = jnp.where(masks_s[row, slot, col] == 1, index, ZERO)
             table[row, SLOTS, col] = live_s[row, col]
             table[row, SLOTS + 1, col] = bound_s[row, col]
+    copy.wait()
 
 
 def fill(room, halo, near, info, far, at, near_at, far_at, corner):
@@ -400,7 +405,7 @@
     for v in range(COLS):
         col = frame.col(v)
         near = near_input(table, row, col, room, 16)
-        sums = products[u - 2, v] + jnp.dot(near, weights[row, col, 256:384], preferred_element_type=F32)
+        sums = products[u - 2, v] + jnp.dot(near, weights[1][row, col], preferred_element_type=F32)
         value = second[u - 2, v]
         result = 2.0 * (factor * (degree[v] * value - sums * alive_of(table, row, col)) - value) - first[v]
         third[v] = result
@@ -417,9 +422,9 @@
 
 
 def step_1a(
-    weights, signals, table, spectral, from_a, from_b, from_s, room, room2, degree, first, ghost_degree, ghost_first
+    own_tiles, corner_tiles, signals, table, spectral, from_a, from_b, from_s, room, room2, degree, first, ghost_degree, ghost_first
 ):
-    frame = Frame()
+    frame, weights = Frame(), (own_tiles, corner_tiles)
     factor = 2.0 / jnp.full((16, 128), spectral[0])
     room[ZERO] = jnp.zeros((32, 128), BF16)
     for u in (2, 3):
@@ -436,10 +441,10 @@
 
 
 def step_1b(
-    weights, signals, table, spectral, from_a, from_b, from_x, room_in, room2_in, degree_a, first_a,
+    own_tiles, corner_tiles, signals, table, spectral, from_a, from_b, from_x, room_in, room2_in, degree_a, first_a,
     degree, first, ghost_degree, ghost_first, second, out_a, out_b, room, room2,
 ):
-    frame = Frame()
+    frame, weights = Frame(), (own_tiles, corner_tiles)
     factor = 2.0 / jnp.full((16, 128), spectral[0])
     room[ZERO] = jnp.zeros((32, 128), BF16)
     room2[ZERO] = jnp.zeros((16, 128), BF16)
@@ -461,18 +466,18 @@
             message_2(out, frame.row(u), second, weights, table, u, v, u, v2, frame)
 
 
-def pack_x2(second, weights, table, out_s, out_x, products):
-    frame = Frame()
+def pack_x2(second, own_tiles, table, out_s, out_x, products):
+    frame, weights = Frame(), (own_tiles,)
     for out, u in ((out_s, 2), (out_x, 3)):
         for v in range(COLS):
             products[u - 2, v] = message_2(out, frame.col(v) + 1, second, weights, table, u, v, 5 - u, v, frame)
 
 
 def step_3a(
-    weights, table, spectral, from_a, from_b, from_s, new_a, new_b, new_s,
+    own_tiles, corner_tiles, table, spectral, from_a, from_b, from_s, new_a, new_b, new_s,
     degree, first, second, products, ghost_degree, ghost_first, room, room2, third,
 ):
-    frame = Frame()
+    frame, weights = Frame(), (own_tiles, corner_tiles)
     factor = 2.0 / jnp.full((16, 128), spectral[0])
     room[ZERO] = jnp.zeros((16, 128), BF16)
     for u in (2, 3):
@@ -487,11 +492,11 @@
 
 
 def step_3b(
-    weights, signals, table, spectral, scales, from_a, from_b, from_x, new_a, new_b, new_x, room_in, room2_in,
+    own_tiles, corner_tiles, signals, table, spectral, scales, from_a, from_b, from_x, new_a, new_b, new_x, room_in, room2_in,
     degree_a, degree, first_a, first, second, products, ghost_degree, ghost_first, third_a,
     partial, third, fourths, room, room2,
 ):
-    frame = Frame()
+    frame, weights = Frame(), (own_tiles, corner_tiles)
     factor = 2.0 / jnp.full((16, 128), spectral[0])
     room[ZERO] = jnp.zeros((16, 128), BF16)
     room2[ZERO] = jnp.zeros((16, 128), BF16)
@@ -539,6 +544,13 @@
                 coefficients[scale, row, col] = total
 
 
+def finish(gathered, out, *, nodes):
+    total = jnp.sum(gathered[...], axis=0) * (1.0 / nodes)
+    scales, channels = out.shape
+    for scale in range(scales):
+        out[scale : scale + 1] = pltpu.roll(total, 128 - channels * scale, 1)[:, 0:channels] if scale else total[:, 0:channels]
+
+
 def in_hbm(*arrays):
     return tuple(pltpu.with_memory_space_constraint(array, pltpu.MemorySpace.HBM) for array in arrays)
 
@@ -567,10 +579,8 @@
     nodes = ROWS * COLS * 128 * devices
 
     def swap_z(a, b):
-        return (
-            lax.ppermute(a, "gy", neighbour_pairs(devices_z, 0)),
-            lax.ppermute(b, "gy", neighbour_pairs(devices_z, 1)),
-        )
+        b = lax.ppermute(b, "gy", neighbour_pairs(devices_z, 1))
+        return lax.ppermute(a, "gy", neighbour_pairs(devices_z, 0)), b
 
     def swap_x(s, x):
         far = lax.ppermute(x, GX, neighbour_pairs(devices_x, 1))
@@ -589,21 +599,22 @@
         )
 
     tile_dir, tile_mask = jnp.swapaxes(tile_dir, 1, 2), jnp.swapaxes(tile_mask, 1, 2)
-    local = (tiles, signals, tile_dir, tile_mask, live_rows, bound_rows)
-    rooms = [
-        pltpu.VMEM((2, ROWS, SLOTS, EDGE, 128), BF16),
-        pltpu.VMEM(signals.shape, F32),
-        pltpu.SMEM(tile_dir.shape, jnp.int32),
-        pltpu.SMEM(tile_dir.shape, jnp.int32),
-        pltpu.SMEM(live_rows.shape, jnp.int32),
-        pltpu.SMEM(live_rows.shape, jnp.int32),
-        pltpu.SemaphoreType.DMA((2,)),
-        pltpu.SemaphoreType.DMA((5,)),
-    ]
-    wide_rooms = [pltpu.VMEM((2, COLS, SLOTS, EDGE, 128), BF16)] + rooms[1:]
+    tables = (tile_dir, tile_mask, live_rows, bound_rows)
     message_z, message_x = pltpu.VMEM((ROWS, LONG, 128), BF16), pltpu.VMEM((COLS + 2, LONG, 128), BF16)
-    a, b = call(pack_z, [message_z] * 2, [HBM] * 6, [VMEM] * 2, rooms)(*in_hbm(*local))
-    s, x = call(pack_x, [message_x] * 2, [HBM] * 6, [VMEM] * 2, wide_rooms, flops=1 << 21)(*in_hbm(*local))
+    a, b, *tables = call(
+        pack_z,
+        [message_z] * 2 + [pltpu.SMEM(table.shape, jnp.int32) for table in tables],
+        [HBM] * 6,
+        [VMEM] * 2 + [SMEM] * 4,
+        [
+            pltpu.VMEM((2, ROWS, SLOTS, EDGE, 128), BF16),
+            pltpu.VMEM(signals.shape, F32),
+            pltpu.SemaphoreType.DMA((2,)),
+            pltpu.SemaphoreType.DMA((5,)),
+        ],
+    )(*in_hbm(tiles, signals, *tables))
+    tables = in_smem(*tables)
+    s, x = call(pack_x, [message_x] * 2, [VMEM] * 2 + [SMEM] * 4, [VMEM] * 2, flops=1 << 21)(tiles, signals, *tables)
     a, b = swap_z(a, b)
     corner_room = [pltpu.VMEM((2, 2, LONG, 128), BF16), pltpu.SemaphoreType.DMA((2, 2))]
     s, x = call(
@@ -611,18 +622,19 @@
     )(a, b, *in_vmem(s, x))
     s, x = swap_x(s, x)
 
-    weights, table, scale_table = call(
+    corner_tiles, own_tiles, table, scale_table = call(
         turn_tiles,
         [
-            shape((ROWS, COLS, 384, 128)),
+            shape((ROWS, COLS, 128, 128)),
+            shape((ROWS, COLS, 256, 128)),
             pltpu.SMEM((ROWS, SLOTS + 2, COLS), jnp.int32),
             pltpu.SMEM(scale_coeffs.shape, F32),
         ],
-        [VMEM] + [HBM] * 5,
-        [VMEM, SMEM, SMEM],
-        rooms[2:6] + [pltpu.SemaphoreType.DMA((5,))],
-        flops=1 << 24,
-    )(tiles, *in_hbm(*local[2:], scale_coeffs))
+        [VMEM] + [SMEM] * 4 + [HBM],
+        [VMEM, VMEM, SMEM, SMEM],
+        [pltpu.SemaphoreType.DMA],
+        flops=1 << 23,
+    )(tiles, *tables, *in_hbm(scale_coeffs))
     table, scale_table = in_smem(table, scale_table)
     half = shape((COLS, channels, 128), F32)
     extra = shape((COLS + 4, channels, 128), F32)
@@ -631,19 +643,19 @@
     short_z, short_x = pltpu.VMEM((ROWS, 32, 128), BF16), pltpu.VMEM((COLS + 2, 32, 128), BF16)
     full = shape((ROWS, COLS, channels, 128), F32)
     room_1, room_2, degree_a, first_a, ghost_degree_a, ghost_first_a = call(
-        step_1a, [wide_room, room, half, half, extra, extra], [VMEM] * 2 + [SMEM] * 2 + [VMEM] * 3, [VMEM] * 6, flops=1 << 25
-    )(weights, signals, table, spectral_bound, a, b, s)
+        step_1a, [wide_room, room, half, half, extra, extra], [VMEM] * 3 + [SMEM] * 2 + [VMEM] * 3, [VMEM] * 6, flops=1 << 25
+    )(own_tiles, corner_tiles, signals, table, spectral_bound, a, b, s)
     degree_b, first_b, ghost_degree_b, ghost_first_b, second, a2, b2 = call(
         step_1b,
         [half, half, extra, extra, full, short_z, short_z],
-        [VMEM] * 2 + [SMEM] * 2 + [VMEM] * 7,
+        [VMEM] * 3 + [SMEM] * 2 + [VMEM] * 7,
         [VMEM] * 7,
         [wide_scratch, scratch],
         flops=1 << 26,
-    )(weights, signals, table, spectral_bound, a, b, x, room_1, room_2, degree_a, first_a)
+    )(own_tiles, corner_tiles, signals, table, spectral_bound, a, b, x, room_1, room_2, degree_a, first_a)
     s2, x2, products = call(
         pack_x2, [short_x] * 2 + [full], [VMEM, VMEM, SMEM], [VMEM] * 3, flops=1 << 20
-    )(second, weights, table)
+    )(second, own_tiles, table)
     a2, b2 = swap_z(a2, b2)
     corner_room = [pltpu.VMEM((2, 2, 32, 128), BF16), pltpu.SemaphoreType.DMA((2, 2))]
     s2, x2 = call(
@@ -651,20 +663,20 @@
     )(a2, b2, *in_vmem(s2, x2))
     s2, x2 = swap_x(s2, x2)
     room_1, room_2, third_a = call(
-        step_3a, [room, room, half], [VMEM, SMEM, SMEM] + [VMEM] * 12, [VMEM] * 3, flops=1 << 25
+        step_3a, [room, room, half], [VMEM, VMEM, SMEM, SMEM] + [VMEM] * 12, [VMEM] * 3, flops=1 << 25
     )(
-        weights, table, spectral_bound, a, b, s, a2, b2, s2, degree_a, first_a, second, products,
+        own_tiles, corner_tiles, table, spectral_bound, a, b, s, a2, b2, s2, degree_a, first_a, second, products,
         ghost_degree_a, ghost_first_a,
     )
     partial, third_b, fourth = call(
         step_3b,
         [pltpu.VMEM((devices, 1, 128), F32), half, full],
-        [VMEM] * 2 + [SMEM] * 3 + [VMEM] * 17,
+        [VMEM] * 3 + [SMEM] * 3 + [VMEM] * 17,
         [VMEM] * 3,
         [scratch, scratch],
         flops=1 << 26,
     )(
-        weights, signals, table, spectral_bound, scale_table, a, b, x, a2, b2, x2, room_1, room_2,
+        own_tiles, corner_tiles, signals, table, spectral_bound, scale_table, a, b, x, a2, b2, x2, room_1, room_2,
         degree_a, degree_b, first_a, first_b, second, products, ghost_degree_b, ghost_first_b, third_a,
     )
     totals = call(
@@ -675,7 +687,14 @@
         flops=1 << 24,
     )(signals, table, scale_table, first_a, first_b, second, third_a, third_b, fourth)[0]
     gathered = lax.all_to_all(partial, GX_GY, 0, 0)
-    energy = jnp.sum(gathered, axis=(0, 1))[: scales * channels].reshape(scales, channels) / nodes
+    energy = pl.pallas_call(
+        functools.partial(finish, nodes=nodes),
+        out_shape=shape((scales, channels), F32),
+        in_specs=[VMEM],
+        out_specs=VMEM,
+        compiler_params=params(8),
+        name="finish",
+    )(gathered)
     return (totals, energy)
 
 

time: 57.4 us -> 57.2 us (level)
  Pallas kernels: 13.3 us -> 11.3 us
  starting transfers between devices: 31.5 us -> 33.3 us
  waiting for transfers between devices: 10.1 us -> 10.9 us
  local copies, waits for them, and re-layouts: 0.68 us -> 0.01 us
    pallas_call x5 -> x6, Pallas kernels: 7.95 us -> 6 us  [the longest x1 1.51 us: shards(): call(turn_tiles, [shape((ROWS, COLS, 128, 128)), shape((ROWS, COLS, 256,...]
    ppermute x2, waiting for transfers between devices: 1.49 us -> 2.29 us  [swap_x(): far = lax.ppermute(x, GX, neighbour_pairs(devices_x, 1))]
    div x1 -> x0, local copies, waits for them, and re-layouts: 0.67 us -> none  [shards(): jnp.sum(gathered, axis=(0, 1))[:scales * channels].reshape(scales, channels)]
  transfers between devices with their start and end apart: 9 -> 9, of which waited for: 3 -> 4; matrix products, arithmetic and copies ran while one was open for 0% -> 0% of each run, Pallas kernels for 14% -> 9%
where the time goes in v5:
time: 57.2 us; the launch traced here: 56.9 us
  starting transfers between devices  33.3 us (58%)
  Pallas kernels  11.3 us (20%)
  waiting for transfers between devices  10.9 us (19%)
  between operations  1.44 us (3%)
    all_to_all x1, starting transfers between devices, shards(): gathered = lax.all_to_all(partial, GX_GY, 0, 0)  15.5 us
    all_to_all x1, waiting for transfers between devices, shards(): gathered = lax.all_to_all(partial, GX_GY, 0, 0)  8.44 us
    ppermute x2, starting transfers between devices, swap_z(): return (lax.ppermute(a, 'gy', neighbour_pairs(devices_z, 0)), b)  7.72 us
    ppermute x2, starting transfers between devices, swap_x(): far = lax.ppermute(x, GX, neighbour_pairs(devices_x, 1))  7.19 us
    ppermute x2, waiting for transfers between devices, swap_x(): far = lax.ppermute(x, GX, neighbour_pairs(devices_x, 1))  2.29 us
    pallas_call x1, Pallas kernels, shards(): call(step_3b, [pltpu.VMEM((devices, 1, 128), F32), half, full], [VMEM] *...  1.94 us
    ppermute x2, starting transfers between devices, swap_x(): return (lax.ppermute(s, 'gx_2', [(0, 1), (1, 0)]), far)  1.6 us
    pallas_call x1, Pallas kernels, shards(): call(turn_tiles, [shape((ROWS, COLS, 128, 128)), shape((ROWS, COLS, 256,...  1.51 us
  transfers between devices with their start and end apart: 9, of which 4 were waited for; matrix products, arithmetic and copies ran while one was open for 0% of the time, Pallas kernels for 9%

profile of v5, /device:TPU:1, one launch (start us, length us, event | category | flops | bytes accessed | tf_op | source)
XLA Modules:
  0.0 56.9 jit_solution(7305883247208486246)
XLA Ops:
  0.7 1.4 %shard_map.95 = (bf16[2,80,128]{2,1,0:T(8,128)(2,1)S(1)}, bf16[2,80,128]{2,1,0:T(8,128)(2,1)S(1)}, s32[2,4,8]{2,1,0:T(4,128)S(4)}, s32[2,4,8]{2,1,0:T(4,128)S(4)...) custom-call(bf16[2,8,4,128,128]{4,3,2,1,0:T(8,128)(2,1)} %tiles.5, f32[2,8,16,128]{3,2,1,0:T(8,128)} %signals.11, ...), custom_call_target="tpu_custom_call" | custom-call | flops 1000 | bytes 1048576 | tf_op jit(solution)/shard_map/pallas_call | solution.py:604
  2.1 2.5 %collective-permute-start = (bf16[2,80,128]{2,1,0:T(8,128)(2,1)S(1)}, bf16[2,80,128]{2,1,0:T(8,128)(2,1)S(1)}, u32[]{:S(2)}, u32[]{:S(2)}) collective-permute-start(bf16[2,80,128]{2,1,0:T(8,128)(2,1)S(1)} %get-tuple-element.48), channel_id=1, source_target_pairs={{0,1},{2,3},{1,0},{3,2},{4,5},{6,7},{5,4},{7,6},{8,9},{10,11},{9,8... | collective-permute-start | bytes 122888 | tf_op jit(solution)/shard_map/ppermute | solution.py:583
  4.6 0.7 %collective-permute-start.1 = (bf16[2,80,128]{2,1,0:T(8,128)(2,1)S(1)}, bf16[2,80,128]{2,1,0:T(8,128)(2,1)S(1)}, u32[]{:S(2)}, u32[]{:S(2)}) collective-permute-start(bf16[2,80,128]{2,1,0:T(8,128)(2,1)S(1)} %get-tuple-element.49), channel_id=1, source_target_pairs={{1,2},{2,1},{5,6},{6,5},{9,10},{10,9},{13,14},{14,13},{17,18},{18,... | collective-permute-start | bytes 122888 | tf_op jit(solution)/shard_map/ppermute | solution.py:582
  5.3 0.8 %shard_map.97 = (bf16[10,80,128]{2,1,0:T(8,128)(2,1)S(1)}, bf16[10,80,128]{2,1,0:T(8,128)(2,1)S(1)}) custom-call(bf16[2,8,4,128,128]{4,3,2,1,0:T(8,128)(2,1)S(1)} %copy-done, f32[2,8,16,128]{3,2,1,0:T(8,128)S(1)} %copy-done.1, s32[2,4,8]{2,1,0:T(4,128)S(4)} %get-tuple-element.40.dirs_s.dirs, s32[2,4,8]{2,1,0:T(4,128)S(4)} %get-tuple-element.41.masks_s.masks, ...), custom_call_target="tpu_custom_call" | custom-call | flops 2097152 | bytes 1048576 | tf_op jit(solution)/shard_map/pallas_call | solution.py:617
  6.1 0.2 shard_map.98
  6.4 1.5 %collective-permute-start.2 = (bf16[10,80,128]{2,1,0:T(8,128)(2,1)S(1)}, bf16[10,80,128]{2,1,0:T(8,128)(2,1)S(1)}, u32[]{:S(2)}, u32[]{:S(2)}) collective-permute-start(bf16[10,80,128]{2,1,0:T(8,128)(2,1)S(1)} %get-tuple-element.52), channel_id=1, source_target_pairs={{0,4},{4,0},{1,5},{5,1},{2,6},{6,2},{3,7},{7,3},{8,12},{12,8},{9,1... | collective-permute-start | bytes 614408 | tf_op jit(solution)/shard_map/ppermute | solution.py:587
  7.9 3.2 %collective-permute-start.3 = (bf16[10,80,128]{2,1,0:T(8,128)(2,1)S(1)}, bf16[10,80,128]{2,1,0:T(8,128)(2,1)S(1)}, u32[]{:S(2)}, u32[]{:S(2)}) collective-permute-start(bf16[10,80,128]{2,1,0:T(8,128)(2,1)S(1)} %get-tuple-element.54), channel_id=1, source_target_pairs={{4,8},{12,16},{20,24},{28,32},{36,40},{44,48},{52,56},{60,64},{68,... | collective-permute-start | bytes 614408 | tf_op jit(solution)/shard_map/ppermute | solution.py:586
  11.7 1.5 %shard_map.96 = (bf16[2,8,128,128]{3,2,1,0:T(8,128)(2,1)S(1)}, bf16[2,8,256,128]{3,2,1,0:T(8,128)(2,1)S(1)}, s32[2,6,8]{2,1,0:T(8,128)S(4)}, f32[6,5]{1,0:T(8,128)S(4)}) custom-call(bf16[2,8,4,128,128]{4,3,2,1,0:T(8,128)(2,1)S(1)} %copy-done, s32[2,4,8]{2,1,0:T(4,128)S(4)} %get-tuple-element.40.dirs_s.dirs, s32[2,4,8]{2,1,0:T(4,128)S(4)} %get-tuple-element.41.masks_s.masks, ...), custom_call_target="tpu_custom_call" | custom-call | flops 8388608 | bytes 1048576 | tf_op jit(solution)/shard_map/pallas_call | solution.py:625
  13.3 0.8 %shard_map.99 = (bf16[73,32,128]{2,1,0:T(8,128)(2,1)S(1)}, bf16[73,16,128]{2,1,0:T(8,128)(2,1)S(1)}, f32[8,16,128]{2,1,0:T(8,128)S(1)}, f32[8,16,128]{2,1,0:T(8,...) custom-call(bf16[2,8,256,128]{3,2,1,0:T(8,128)(2,1)S(1)} %get-tuple-element.46.own_tiles, ...), custom_call_target="tpu_custom_call" | custom-call | flops 33554432 | bytes 1048576 | tf_op jit(solution)/shard_map/pallas_call | solution.py:645
  14.1 0.9 %collective-permute-done.3.from_x = bf16[10,80,128]{2,1,0:T(8,128)(2,1)S(1)} collective-permute-done((bf16[10,80,128]{2,1,0:T(8,128)(2,1)S(1)}, bf16[10,80,128]{2,1,0:T(8,128)(2,1)S(1)}, u32[]{:S(2)}, u32[]{:S(2)}) %collective-permute-start.3) | collective-permute-done | bytes 204832 | tf_op jit(solution)/shard_map/ppermute | solution.py:586
  14.9 1.3 %shard_map.100 = (f32[8,16,128]{2,1,0:T(8,128)S(1)}, f32[8,16,128]{2,1,0:T(8,128)S(1)}, f32[12,16,128]{2,1,0:T(8,128)S(1)}, f32[12,16,128]{2,1,0:T(8,128)S(1)}, ...) custom-call(bf16[2,8,256,128]{3,2,1,0:T(8,128)(2,1)S(1)} %get-tuple-element.46.own_ti, ...), custom_call_target="tpu_custom_call" | custom-call | flops 67108864 | bytes 1048576 | tf_op jit(solution)/shard_map/pallas_call | solution.py:648
  16.3 5.2 %collective-permute-start.4 = (bf16[2,32,128]{2,1,0:T(8,128)(2,1)S(1)}, bf16[2,32,128]{2,1,0:T(8,128)(2,1)S(1)}, u32[]{:S(2)}, u32[]{:S(2)}) collective-permute-start(bf16[2,32,128]{2,1,0:T(8,128)(2,1)S(1)} %get-tuple-element.60), channel_id=1, source_target_pairs={{0,1},{2,3},{1,0},{3,2},{4,5},{6,7},{5,4},{7,6},{8,9},{10,11},{9,8... | collective-permute-start | bytes 49160 | tf_op jit(solution)/shard_map/ppermute | solution.py:583
  21.5 0.7 %collective-permute-start.5 = (bf16[2,32,128]{2,1,0:T(8,128)(2,1)S(1)}, bf16[2,32,128]{2,1,0:T(8,128)(2,1)S(1)}, u32[]{:S(2)}, u32[]{:S(2)}) collective-permute-start(bf16[2,32,128]{2,1,0:T(8,128)(2,1)S(1)} %get-tuple-element.61), channel_id=1, source_target_pairs={{1,2},{2,1},{5,6},{6,5},{9,10},{10,9},{13,14},{14,13},{17,18},{18,... | collective-permute-start | bytes 49160 | tf_op jit(solution)/shard_map/ppermute | solution.py:582
  22.1 0.3 shard_map.101
  22.5 0.1 collective-permute-done.4.from_a.new_a
  22.6 0.2 shard_map.102
  22.9 4.0 %collective-permute-start.7 = (bf16[10,32,128]{2,1,0:T(8,128)(2,1)S(1)}, bf16[10,32,128]{2,1,0:T(8,128)(2,1)S(1)}, u32[]{:S(2)}, u32[]{:S(2)}) collective-permute-start(bf16[10,32,128]{2,1,0:T(8,128)(2,1)S(1)} %get-tuple-element.69), channel_id=1, source_target_pairs={{4,8},{12,16},{20,24},{28,32},{36,40},{44,48},{52,56},{60,64},{68,... | collective-permute-start | bytes 245768 | tf_op jit(solution)/shard_map/ppermute | solution.py:586
  26.9 0.7 %shard_map.103 = (bf16[73,16,128]{2,1,0:T(8,128)(2,1)S(1)}, bf16[73,16,128]{2,1,0:T(8,128)(2,1)S(1)}, f32[8,16,128]{2,1,0:T(8,128)S(1)}) custom-call(bf16[2,8,256,128]{3,2,1,0:T(8,128)(2,1)S(1)} %get-tuple-element.46.own_tiles, bf16[2,8,128,128]{3,2,1,0:T(8,128)(2,1)S(1)} %get-tuple-element.47.corner_tiles, s32[2,6,8]{2,1,0:T(8,128)S(4)} %get-tuple-element.44.table, ...), custom_call_target="tpu_custom_call" | custom-call | flops 33554432 | bytes 1048576 | tf_op jit(solution)/shard_map/pallas_call | solution.py:665
  27.6 1.4 %collective-permute-done.7.new_x = bf16[10,32,128]{2,1,0:T(8,128)(2,1)S(1)} collective-permute-done((bf16[10,32,128]{2,1,0:T(8,128)(2,1)S(1)}, bf16[10,32,128]{2,1,0:T(8,128)(2,1)S(1)}, u32[]{:S(2)}, u32[]{:S(2)}) %collective-permute-start.7) | collective-permute-done | bytes 81952 | tf_op jit(solution)/shard_map/ppermute | solution.py:586
  29.0 1.9 %shard_map.104 = (f32[128,1,128]{2,1,0:T(1,128)}, f32[8,16,128]{2,1,0:T(8,128)S(1)}, f32[2,8,16,128]{3,2,1,0:T(8,128)S(1)}) custom-call(bf16[2,8,256,128]{3,2,1,0:T(8,128)(2,1)S(1)} %get-tuple-element.46.own_tiles, bf16[2,8,128,128]{3,2,1,0:T(8,128)(2,1)S(1)} %get-tuple-element.47.corner_tiles, f32[2,8,16,128]{3,2,1,0:T(8,128)S(1)} %copy-done.1, ...), custom_call_target="tpu_custom_call" | custom-call | flops 67108864 | bytes 1048576 | tf_op jit(solution)/shard_map/pallas_call | solution.py:671
  30.9 15.5 %all-to-all-start = ((f32[128,1,128]{2,1,0:T(1,128)}), f32[128,1,128]{2,1,0:T(1,128)S(1)}, u32[]{:S(2)}, u32[]{:S(2)}) async-start(f32[128,1,128]{2,1,0:T(1,128)} %get-tuple-element.77), calls=%async_computation | async-start | bytes 131072 | tf_op jit(solution)/shard_map/all_to_all | solution.py:689
  46.4 1.3 %shard_map.105 = f32[6,2,8,16,128]{4,3,2,1,0:T(8,128)} custom-call(f32[2,8,16,128]{3,2,1,0:T(8,128)S(1)} %copy-done.1, s32[2,6,8]{2,1,0:T(8,128)S(4)} %get-tuple-element.44.table, f32[6,5]{1,0:T(8,128)S(4)} %get-tuple-element.45.scales, f32[8,16,128]{2,1,0:T(8,128)S(1)} %get-tuple-element.53.first_a.first, ...), custom_call_target="tpu_custom_call" | custom-call | flops 16777216 | bytes 1048576 | tf_op jit(solution)/shard_map/pallas_call | solution.py:682
  47.7 8.4 %all-to-all-done.gathered = f32[128,1,128]{2,1,0:T(1,128)S(1)} async-done(((f32[128,1,128]{2,1,0:T(1,128)}), f32[128,1,128]{2,1,0:T(1,128)S(1)}, u32[]{:S(2)}, u32[]{:S(2)}) %all-to-all-start) | async-done | bytes 65568 | tf_op jit(solution)/shard_map/all_to_all | solution.py:689
  56.1 0.8 %finish.1 = f32[6,16]{1,0:T(8,128)} custom-call(f32[128,1,128]{2,1,0:T(1,128)S(1)} %all-to-all-done.gathered), custom_call_target="tpu_custom_call" | custom-call | tf_op jit(solution)/shard_map/finish/pallas_call | solution.py:690
  (10 shorter events, 0.1 us)
Async XLA Ops:
  0.6 4.7 %copy-start.1 = (f32[2,8,16,128]{3,2,1,0:T(8,128)S(1)}, f32[2,8,16,128]{3,2,1,0:T(8,128)}, u32[]{:S(2)}) copy-start(f32[2,8,16,128]{3,2,1,0:T(8,128)} %signals.11) | copy-start | bytes 393220
  0.6 4.7 %copy-start = (bf16[2,8,4,128,128]{4,3,2,1,0:T(8,128)(2,1)S(1)}, bf16[2,8,4,128,128]{4,3,2,1,0:T(8,128)(2,1)}, u32[]{:S(2)}) copy-start(bf16[2,8,4,128,128]{4,3,2,1,0:T(8,128)(2,1)} %tiles.5) | copy-start | bytes 6291460
  2.1 4.0 %collective-permute-start = (bf16[2,80,128]{2,1,0:T(8,128)(2,1)S(1)}, bf16[2,80,128]{2,1,0:T(8,128)(2,1)S(1)}, u32[]{:S(2)}, u32[]{:S(2)}) collective-permute-start(bf16[2,80,128]{2,1,0:T(8,128)(2,1)S(1)} %get-tuple-element.48), channel_id=1, source_target_pairs={{0,1},{2,3},{1,0},{3,2},{4,5},{6,7},{5,4},{7,6},{8,9},{10,11},{9,8... | collective-permute-start | bytes 122888 | tf_op jit(solution)/shard_map/ppermute | solution.py:583
  4.6 1.5 %collective-permute-start.1 = (bf16[2,80,128]{2,1,0:T(8,128)(2,1)S(1)}, bf16[2,80,128]{2,1,0:T(8,128)(2,1)S(1)}, u32[]{:S(2)}, u32[]{:S(2)}) collective-permute-start(bf16[2,80,128]{2,1,0:T(8,128)(2,1)S(1)} %get-tuple-element.49), channel_id=1, source_target_pairs={{1,2},{2,1},{5,6},{6,5},{9,10},{10,9},{13,14},{14,13},{17,18},{18,... | collective-permute-start | bytes 122888 | tf_op jit(solution)/shard_map/ppermute | solution.py:582
  6.4 6.9 %collective-permute-start.2 = (bf16[10,80,128]{2,1,0:T(8,128)(2,1)S(1)}, bf16[10,80,128]{2,1,0:T(8,128)(2,1)S(1)}, u32[]{:S(2)}, u32[]{:S(2)}) collective-permute-start(bf16[10,80,128]{2,1,0:T(8,128)(2,1)S(1)} %get-tuple-element.52), channel_id=1, source_target_pairs={{0,4},{4,0},{1,5},{5,1},{2,6},{6,2},{3,7},{7,3},{8,12},{12,8},{9,1... | collective-permute-start | bytes 614408 | tf_op jit(solution)/shard_map/ppermute | solution.py:587
  7.9 7.1 %collective-permute-start.3 = (bf16[10,80,128]{2,1,0:T(8,128)(2,1)S(1)}, bf16[10,80,128]{2,1,0:T(8,128)(2,1)S(1)}, u32[]{:S(2)}, u32[]{:S(2)}) collective-permute-start(bf16[10,80,128]{2,1,0:T(8,128)(2,1)S(1)} %get-tuple-element.54), channel_id=1, source_target_pairs={{4,8},{12,16},{20,24},{28,32},{36,40},{44,48},{52,56},{60,64},{68,... | collective-permute-start | bytes 614408 | tf_op jit(solution)/shard_map/ppermute | solution.py:586
  16.3 6.3 %collective-permute-start.4 = (bf16[2,32,128]{2,1,0:T(8,128)(2,1)S(1)}, bf16[2,32,128]{2,1,0:T(8,128)(2,1)S(1)}, u32[]{:S(2)}, u32[]{:S(2)}) collective-permute-start(bf16[2,32,128]{2,1,0:T(8,128)(2,1)S(1)} %get-tuple-element.60), channel_id=1, source_target_pairs={{0,1},{2,3},{1,0},{3,2},{4,5},{6,7},{5,4},{7,6},{8,9},{10,11},{9,8... | collective-permute-start | bytes 49160 | tf_op jit(solution)/shard_map/ppermute | solution.py:583
  21.5 1.1 %collective-permute-start.5 = (bf16[2,32,128]{2,1,0:T(8,128)(2,1)S(1)}, bf16[2,32,128]{2,1,0:T(8,128)(2,1)S(1)}, u32[]{:S(2)}, u32[]{:S(2)}) collective-permute-start(bf16[2,32,128]{2,1,0:T(8,128)(2,1)S(1)} %get-tuple-element.61), channel_id=1, source_target_pairs={{1,2},{2,1},{5,6},{6,5},{9,10},{10,9},{13,14},{14,13},{17,18},{18,... | collective-permute-start | bytes 49160 | tf_op jit(solution)/shard_map/ppermute | solution.py:582
  22.8 4.1 %collective-permute-start.6 = (bf16[10,32,128]{2,1,0:T(8,128)(2,1)S(1)}, bf16[10,32,128]{2,1,0:T(8,128)(2,1)S(1)}, u32[]{:S(2)}, u32[]{:S(2)}) collective-permute-start(bf16[10,32,128]{2,1,0:T(8,128)(2,1)S(1)} %get-tuple-element.64), channel_id=1, source_target_pairs={{0,4},{4,0},{1,5},{5,1},{2,6},{6,2},{3,7},{7,3},{8,12},{12,8},{9,1... | collective-permute-start | bytes 245768 | tf_op jit(solution)/shard_map/ppermute | solution.py:587
  22.9 6.1 %collective-permute-start.7 = (bf16[10,32,128]{2,1,0:T(8,128)(2,1)S(1)}, bf16[10,32,128]{2,1,0:T(8,128)(2,1)S(1)}, u32[]{:S(2)}, u32[]{:S(2)}) collective-permute-start(bf16[10,32,128]{2,1,0:T(8,128)(2,1)S(1)} %get-tuple-element.69), channel_id=1, source_target_pairs={{4,8},{12,16},{20,24},{28,32},{36,40},{44,48},{52,56},{60,64},{68,... | collective-permute-start | bytes 245768 | tf_op jit(solution)/shard_map/ppermute | solution.py:586
  30.9 25.2 %all-to-all-start = ((f32[128,1,128]{2,1,0:T(1,128)}), f32[128,1,128]{2,1,0:T(1,128)S(1)}, u32[]{:S(2)}, u32[]{:S(2)}) async-start(f32[128,1,128]{2,1,0:T(1,128)} %get-tuple-element.77), calls=%async_computation | async-start | bytes 131072 | tf_op jit(solution)/shard_map/all_to_all | solution.py:689

commit v6 on v5

--- a/solution.py
+++ b/solution.py
@@ -18,9 +18,10 @@
 SPOTS = (ROWS + 4) * WIDE
 ZERO = SPOTS
 SLOTS = 4
-NEAR, INFO, FAR, LONG = 32, 48, 64, 80
+NEAR, FAR, LONG = 32, 48, 64
 HIGH, LOW, OWN_HIGH, OWN_LOW = 0, 1, 2, 3
-DIRS, BOUND, DEGREE, BOUND2, BOUND3, BOUND4 = 0, 1, 2, 3, 4, 5
+INFO = 3
+BOUND, BOUND2, BOUND3, BOUND4, DEGREE, DIRS = 0, 1, 2, 3, 4, 6
 VMEM = pl.BlockSpec(memory_space=pltpu.VMEM)
 SMEM = pl.BlockSpec(memory_space=pltpu.SMEM)
 ANY = pl.BlockSpec(memory_space=pl.ANY)
@@ -53,7 +54,7 @@
     info = jnp.zeros((16, 128), F32)
     for row, value in rows.items():
         info = jnp.where(index == row, value, info)
-    return info.astype(BF16)
+    return info
 
 
 def odd_z():
@@ -118,19 +119,12 @@
     own_high = own_high.astype(F32)
     degree_high, degree_low = split(product[16:17])
     out[at, 0:NEAR] = merge([raw[slot].astype(F32) for slot in range(SLOTS)]).astype(BF16)
-    out[at, NEAR:INFO] = merge([high.astype(F32), low, own_high, own_low]).astype(BF16)
+    out[at, NEAR:FAR] = merge([high.astype(F32), low, own_high, own_low]).astype(BF16)
     inside2 = below(bound[row2, col2])
-    lane = lanes()
-    rows = {
-        DIRS: jnp.where(
-            lane < EDGE, sides[0], jnp.where(lane < 2 * EDGE, sides[1], jnp.where(lane < 3 * EDGE, sides[2], sides[3]))
-        ),
-        BOUND: repeat(inside),
-        DEGREE: jnp.broadcast_to(degree_high.astype(F32) + pltpu.roll(degree_low, EDGE, 1), (16, 128)),
-        BOUND2: repeat(inside2),
-    }
-    out[at, INFO:FAR] = info_of(rows)
-    out[at, FAR:LONG] = (signals[row2, col2] * inside2).astype(BF16)
+    rows = {BOUND: inside, BOUND2: inside2, DEGREE: degree_high.astype(F32), DEGREE + 1: degree_low}
+    rows.update({DIRS + slot: side for slot, side in enumerate(sides)})
+    second = signals[row2, col2] * inside2
+    out[at, FAR:LONG] = merge([second, jnp.zeros_like(second), jnp.zeros_like(second), info_of(rows)]).astype(BF16)
 
 
 def fetch(refs, rooms, sems):
@@ -169,29 +163,23 @@
             block_message(out, 1 + col, refs, raw, row, col, 1 - row, col)
 
 
-def place_corners(from_a, from_b, out_s, out_b, room, sem, far, info_at):
+def place_corners(from_a, from_b, out_s, out_b, room, sem, near, far, with_info):
     odd, core = odd_z(), odd_core()
     copies = []
     for side, halo in enumerate((from_a, from_b)):
         at = jnp.where(odd == side, COLS + 1, 0)
         for which, out in enumerate((out_s, out_b)):
             row = jnp.where(core == which, 1, 0)
-            near = far - 16 if info_at is None else info_at - 16
             first, other = halo[row, far : far + 16].astype(F32), halo[1 - row, far : far + 16].astype(F32)
-            pack = merge([halo[1 - row, near : near + 16].astype(F32), first, other])
+            parts = [halo[1 - row, near : near + 16].astype(F32), first, other]
+            if with_info:
+                info, info2 = piece(first, INFO), piece(other, INFO)
+                index = lax.broadcasted_iota(jnp.int32, (16, 128), 0)
+                for line, source in ((BOUND4, info2[BOUND2 : BOUND2 + 1]), (BOUND3, info[BOUND2 : BOUND2 + 1])):
+                    info = jnp.where(index == line, source, info)
+                parts.append(jnp.where(index == BOUND2, info2[BOUND : BOUND + 1], info))
             room[which, side, 0:far] = halo[row, 0:far]
-            room[which, side, far : far + 16] = pack.astype(BF16)
-            if info_at is not None:
-                info = halo[row, info_at : info_at + 16].astype(F32)
-                info2 = halo[1 - row, info_at : info_at + 16].astype(F32)
-                index = lax.broadcasted_iota(jnp.int32, (16, 128), 0)
-                for place_at, source in (
-                    (BOUND2, info2[BOUND : BOUND + 1]),
-                    (BOUND3, info[BOUND2 : BOUND2 + 1]),
-                    (BOUND4, info2[BOUND2 : BOUND2 + 1]),
-                ):
-                    info = jnp.where(index == place_at, source, info)
-                room[which, side, info_at : info_at + 16] = info.astype(BF16)
+            room[which, side, far : far + 16] = merge(parts).astype(BF16)
             copies.append(pltpu.make_async_copy(room.at[which, side], out.at[at], sem.at[which, side]))
     for copy in copies:
         copy.start()
@@ -201,12 +189,12 @@
 
 def corners_1(from_a, from_b, in_s, in_b, out_s, out_b, room, sem):
     del in_s, in_b
-    place_corners(from_a, from_b, out_s, out_b, room, sem, FAR, INFO)
+    place_corners(from_a, from_b, out_s, out_b, room, sem, NEAR, FAR, True)
 
 
 def corners_2(from_a, from_b, in_s, in_b, out_s, out_b, room, sem):
     del in_s, in_b
-    place_corners(from_a, from_b, out_s, out_b, room, sem, 16, None)
+    place_corners(from_a, from_b, out_s, out_b, room, sem, 0, 16, False)
 
 
 def place(u, v):
@@ -232,12 +220,16 @@
     return found + [(halo_x, frame.col(v) + 1, 1 if u == 2 else 4, v) for v in range(-1, COLS + 1)]
 
 
-def ghost_product(frame, halo, at, spot_at, room, height):
-    info = halo[at, INFO:FAR].astype(F32)
-    step = jnp.where(info > 5.5, 1.0, jnp.where(info > 2.5, 0.0, -1.0))
-    turned = 3.0 * (frame.up.astype(F32) * step) + frame.right.astype(F32) * (info - 3.0 * step - 4.0) + 4.0
-    turned = jnp.where(info > 8.5, 9.0, turned)
-    turn = jnp.broadcast_to(turned[DIRS : DIRS + 1], (16, 128)).astype(BF16)
+def info_part(halo, at):
+    return piece(halo[at, FAR:LONG].astype(F32), INFO)
+
+
+def ghost_product(frame, halo, at, info, spot_at, room, height):
+    side = merge([info[DIRS + slot : DIRS + slot + 1] for slot in range(SLOTS)])
+    step = jnp.where(side > 5.5, 1.0, jnp.where(side > 2.5, 0.0, -1.0))
+    turned = 3.0 * (frame.up.astype(F32) * step) + frame.right.astype(F32) * (side - 3.0 * step - 4.0) + 4.0
+    turned = jnp.where(side > 8.5, 9.0, turned)
+    turn = jnp.broadcast_to(turned, (16, 128)).astype(BF16)
     halves = [jnp.zeros((16, 128), BF16) for _ in range(height // 16)]
     for d in (0, 1, 2, 3, 5, 6, 7, 8):
         near = room[spot_at + (d // 3 - 1) * WIDE + d % 3 - 1]
@@ -280,10 +272,6 @@
 
 def place_edge(room, at, value):
     room[at, 0:16] = repeat(value).astype(BF16)
-
-
-def bound_row(halo, at):
-    return halo[at, INFO:FAR].astype(F32)[BOUND : BOUND + 1]
 
 
 def message_2(out, at, second, weights, table, u, v, u2, v2, frame):
@@ -340,19 +328,19 @@
     copy.wait()
 
 
-def fill(room, halo, near, info, far, at, near_at, far_at, corner):
+def fill(room, halo, near, far, with_info, at, near_at, far_at, corner):
     place_edge(room, near_at, piece(halo[at, near : near + 16].astype(F32), HIGH))
     beyond = halo[at, far : far + 16].astype(F32)
     places = (far_at,) + corner
     for index, spot_at in enumerate(places):
         place_edge(room, spot_at, piece(beyond, index))
-    if info is not None:
-        lines = halo[at, info : info + 16].astype(F32)
+    if with_info:
+        lines = repeat(piece(beyond, INFO))
         for spot_at, line in zip((near_at,) + places, (BOUND, BOUND2, BOUND3, BOUND4)):
             room[spot_at, 16:32] = jnp.where(heads(), lines[line : line + 1], 0.0).astype(BF16)
 
 
-FIRST, SECOND = (NEAR, INFO, FAR), (0, None, 16)
+FIRST, SECOND = (NEAR, FAR, True), (0, 16, False)
 
 
 def fill_z(frame, room, rows, halo_a, halo_b):
@@ -370,16 +358,16 @@
 
 def half_1(frame, u, weights, signals, table, factor, halos, room, room2, degree, first, ghost_degree, ghost_first):
     for number, (halo, at, gu, gv) in enumerate(ghost_blocks(frame, u, *halos)):
-        pack = halo[at, NEAR:INFO].astype(F32)
+        pack, info = halo[at, NEAR:FAR].astype(F32), info_part(halo, at)
         value = piece(pack, HIGH) + piece(pack, LOW)
-        near = ghost_product(frame, halo, at, place(gu, gv), room, 32)
+        near = ghost_product(frame, halo, at, info, place(gu, gv), room, 32)
         sums = near[0:16] + (piece(pack, OWN_HIGH) + piece(pack, OWN_LOW))
-        line = jnp.broadcast_to(halo[at, INFO:FAR].astype(F32)[DEGREE : DEGREE + 1], (16, 128))
-        around = jnp.broadcast_to(near[16:17], (16, 128)) + (piece(line, 0) + piece(line, 1))
+        around = near[16:17] + (info[DEGREE : DEGREE + 1] + info[DEGREE + 1 : DEGREE + 2])
+        around = jnp.broadcast_to(around, (16, 128))
         result = factor * (around * value - sums) - value
         ghost_degree[number] = around
         ghost_first[number] = result
-        place_edge(room2, place(gu, gv), jnp.where(lanes() < EDGE, result * bound_row(halo, at), 0.0))
+        place_edge(room2, place(gu, gv), jnp.where(lanes() < EDGE, result * info[BOUND : BOUND + 1], 0.0))
     row = frame.row(u)
     for v in range(COLS):
         col = frame.col(v)
@@ -396,11 +384,11 @@
 def half_3(frame, u, weights, table, factor, halos, fresh, room, room2, degree, first, second, products, third, ghost_degree, ghost_first):
     values = ghost_blocks(frame, u, *fresh)
     for number, (halo, at, gu, gv) in enumerate(ghost_blocks(frame, u, *halos)):
-        pack = values[number][0][at, 0:16].astype(F32)
+        pack, info = values[number][0][at, 0:16].astype(F32), info_part(halo, at)
         value = piece(pack, HIGH) + piece(pack, LOW)
-        sums = ghost_product(frame, halo, at, place(gu, gv), room, 16) + (piece(pack, OWN_HIGH) + piece(pack, OWN_LOW))
+        sums = ghost_product(frame, halo, at, info, place(gu, gv), room, 16) + (piece(pack, OWN_HIGH) + piece(pack, OWN_LOW))
         result = 2.0 * (factor * (ghost_degree[number] * value - sums) - value) - ghost_first[number]
-        place_edge(room2, place(gu, gv), jnp.where(lanes() < EDGE, result * bound_row(halo, at), 0.0))
+        place_edge(room2, place(gu, gv), jnp.where(lanes() < EDGE, result * info[BOUND : BOUND + 1], 0.0))
     row = frame.row(u)
     for v in range(COLS):
         col = frame.col(v)

time: 57.2 us -> 56.8 us (level)
    ppermute x2, waiting for transfers between devices: 2.29 us -> 1.72 us  [swap_x(): far = lax.ppermute(x, GX, neighbour_pairs(devices_x, 1))]
  transfers between devices with their start and end apart: 9 -> 9, of which waited for: 4 -> 5; matrix products, arithmetic and copies ran while one was open for 0% -> 0% of each run, Pallas kernels for 9% -> 9%
where the time goes in v6:
time: 56.8 us; the launch traced here: 56.5 us
  starting transfers between devices  33.4 us (59%)
  Pallas kernels  11.2 us (20%)
  waiting for transfers between devices  10.5 us (18%)
  between operations  1.42 us (2%)
    all_to_all x1, starting transfers between devices, shards(): gathered = lax.all_to_all(partial, GX_GY, 0, 0)  15.5 us
    all_to_all x1, waiting for transfers between devices, shards(): gathered = lax.all_to_all(partial, GX_GY, 0, 0)  8.44 us
    ppermute x2, starting transfers between devices, swap_z(): return (lax.ppermute(a, 'gy', neighbour_pairs(devices_z, 0)), b)  7.72 us
    ppermute x2, starting transfers between devices, swap_x(): far = lax.ppermute(x, GX, neighbour_pairs(devices_x, 1))  7.2 us
    pallas_call x1, Pallas kernels, shards(): call(step_3b, [pltpu.VMEM((devices, 1, 128), F32), half, full], [VMEM] *...  1.97 us
    ppermute x2, waiting for transfers between devices, swap_x(): far = lax.ppermute(x, GX, neighbour_pairs(devices_x, 1))  1.72 us
    ppermute x2, starting transfers between devices, swap_x(): return (lax.ppermute(s, 'gx_2', [(0, 1), (1, 0)]), far)  1.71 us
    pallas_call x1, Pallas kernels, shards(): call(turn_tiles, [shape((ROWS, COLS, 128, 128)), shape((ROWS, COLS, 256,...  1.51 us
  transfers between devices with their start and end apart: 9, of which 5 were waited for; matrix products, arithmetic and copies ran while one was open for 0% of the time, Pallas kernels for 9%

profile of v6, /device:TPU:1, one launch (start us, length us, event | category | flops | bytes accessed | tf_op | source)
XLA Modules:
  0.0 56.5 jit_solution(10965259118516784762)
XLA Ops:
  0.7 1.4 %shard_map.95 = (bf16[2,64,128]{2,1,0:T(8,128)(2,1)S(1)}, bf16[2,64,128]{2,1,0:T(8,128)(2,1)S(1)}, s32[2,4,8]{2,1,0:T(4,128)S(4)}, s32[2,4,8]{2,1,0:T(4,128)S(4)...) custom-call(bf16[2,8,4,128,128]{4,3,2,1,0:T(8,128)(2,1)} %tiles.5, f32[2,8,16,128]{3,2,1,0:T(8,128)} %signals.11, ...), custom_call_target="tpu_custom_call" | custom-call | flops 1000 | bytes 1048576 | tf_op jit(solution)/shard_map/pallas_call | solution.py:592
  2.1 2.5 %collective-permute-start = (bf16[2,64,128]{2,1,0:T(8,128)(2,1)S(1)}, bf16[2,64,128]{2,1,0:T(8,128)(2,1)S(1)}, u32[]{:S(2)}, u32[]{:S(2)}) collective-permute-start(bf16[2,64,128]{2,1,0:T(8,128)(2,1)S(1)} %get-tuple-element.48), channel_id=1, source_target_pairs={{0,1},{2,3},{1,0},{3,2},{4,5},{6,7},{5,4},{7,6},{8,9},{10,11},{9,8... | collective-permute-start | bytes 98312 | tf_op jit(solution)/shard_map/ppermute | solution.py:571
  4.6 0.7 %collective-permute-start.1 = (bf16[2,64,128]{2,1,0:T(8,128)(2,1)S(1)}, bf16[2,64,128]{2,1,0:T(8,128)(2,1)S(1)}, u32[]{:S(2)}, u32[]{:S(2)}) collective-permute-start(bf16[2,64,128]{2,1,0:T(8,128)(2,1)S(1)} %get-tuple-element.49), channel_id=1, source_target_pairs={{1,2},{2,1},{5,6},{6,5},{9,10},{10,9},{13,14},{14,13},{17,18},{18,... | collective-permute-start | bytes 98312 | tf_op jit(solution)/shard_map/ppermute | solution.py:570
  5.3 0.4 shard_map.97
  5.7 0.2 collective-permute-done.from_a
  5.9 0.3 shard_map.98
  6.2 1.6 %collective-permute-start.2 = (bf16[10,64,128]{2,1,0:T(8,128)(2,1)S(1)}, bf16[10,64,128]{2,1,0:T(8,128)(2,1)S(1)}, u32[]{:S(2)}, u32[]{:S(2)}) collective-permute-start(bf16[10,64,128]{2,1,0:T(8,128)(2,1)S(1)} %get-tuple-element.52), channel_id=1, source_target_pairs={{0,4},{4,0},{1,5},{5,1},{2,6},{6,2},{3,7},{7,3},{8,12},{12,8},{9,1... | collective-permute-start | bytes 491528 | tf_op jit(solution)/shard_map/ppermute | solution.py:575
  7.8 3.2 %collective-permute-start.3 = (bf16[10,64,128]{2,1,0:T(8,128)(2,1)S(1)}, bf16[10,64,128]{2,1,0:T(8,128)(2,1)S(1)}, u32[]{:S(2)}, u32[]{:S(2)}) collective-permute-start(bf16[10,64,128]{2,1,0:T(8,128)(2,1)S(1)} %get-tuple-element.54), channel_id=1, source_target_pairs={{4,8},{12,16},{20,24},{28,32},{36,40},{44,48},{52,56},{60,64},{68,... | collective-permute-start | bytes 491528 | tf_op jit(solution)/shard_map/ppermute | solution.py:574
  11.7 1.5 %shard_map.96 = (bf16[2,8,128,128]{3,2,1,0:T(8,128)(2,1)S(1)}, bf16[2,8,256,128]{3,2,1,0:T(8,128)(2,1)S(1)}, s32[2,6,8]{2,1,0:T(8,128)S(4)}, f32[6,5]{1,0:T(8,128)S(4)}) custom-call(bf16[2,8,4,128,128]{4,3,2,1,0:T(8,128)(2,1)S(1)} %copy-done, s32[2,4,8]{2,1,0:T(4,128)S(4)} %get-tuple-element.40.dirs_s.dirs, s32[2,4,8]{2,1,0:T(4,128)S(4)} %get-tuple-element.41.masks_s.masks, ...), custom_call_target="tpu_custom_call" | custom-call | flops 8388608 | bytes 1048576 | tf_op jit(solution)/shard_map/pallas_call | solution.py:613
  13.2 0.9 %shard_map.99 = (bf16[73,32,128]{2,1,0:T(8,128)(2,1)S(1)}, bf16[73,16,128]{2,1,0:T(8,128)(2,1)S(1)}, f32[8,16,128]{2,1,0:T(8,128)S(1)}, f32[8,16,128]{2,1,0:T(8,...) custom-call(bf16[2,8,256,128]{3,2,1,0:T(8,128)(2,1)S(1)} %get-tuple-element.46.own_tiles, ...), custom_call_target="tpu_custom_call" | custom-call | flops 33554432 | bytes 1048576 | tf_op jit(solution)/shard_map/pallas_call | solution.py:633
  14.1 0.4 collective-permute-done.3.from_x
  14.4 1.4 %shard_map.100 = (f32[8,16,128]{2,1,0:T(8,128)S(1)}, f32[8,16,128]{2,1,0:T(8,128)S(1)}, f32[12,16,128]{2,1,0:T(8,128)S(1)}, f32[12,16,128]{2,1,0:T(8,128)S(1)}, ...) custom-call(bf16[2,8,256,128]{3,2,1,0:T(8,128)(2,1)S(1)} %get-tuple-element.46.own_ti, ...), custom_call_target="tpu_custom_call" | custom-call | flops 67108864 | bytes 1048576 | tf_op jit(solution)/shard_map/pallas_call | solution.py:636
  15.9 5.2 %collective-permute-start.4 = (bf16[2,32,128]{2,1,0:T(8,128)(2,1)S(1)}, bf16[2,32,128]{2,1,0:T(8,128)(2,1)S(1)}, u32[]{:S(2)}, u32[]{:S(2)}) collective-permute-start(bf16[2,32,128]{2,1,0:T(8,128)(2,1)S(1)} %get-tuple-element.60), channel_id=1, source_target_pairs={{0,1},{2,3},{1,0},{3,2},{4,5},{6,7},{5,4},{7,6},{8,9},{10,11},{9,8... | collective-permute-start | bytes 49160 | tf_op jit(solution)/shard_map/ppermute | solution.py:571
  21.0 0.7 %collective-permute-start.5 = (bf16[2,32,128]{2,1,0:T(8,128)(2,1)S(1)}, bf16[2,32,128]{2,1,0:T(8,128)(2,1)S(1)}, u32[]{:S(2)}, u32[]{:S(2)}) collective-permute-start(bf16[2,32,128]{2,1,0:T(8,128)(2,1)S(1)} %get-tuple-element.61), channel_id=1, source_target_pairs={{1,2},{2,1},{5,6},{6,5},{9,10},{10,9},{13,14},{14,13},{17,18},{18,... | collective-permute-start | bytes 49160 | tf_op jit(solution)/shard_map/ppermute | solution.py:570
  21.7 0.3 shard_map.101
  22.2 0.2 shard_map.102
  22.4 4.0 %collective-permute-start.7 = (bf16[10,32,128]{2,1,0:T(8,128)(2,1)S(1)}, bf16[10,32,128]{2,1,0:T(8,128)(2,1)S(1)}, u32[]{:S(2)}, u32[]{:S(2)}) collective-permute-start(bf16[10,32,128]{2,1,0:T(8,128)(2,1)S(1)} %get-tuple-element.69), channel_id=1, source_target_pairs={{4,8},{12,16},{20,24},{28,32},{36,40},{44,48},{52,56},{60,64},{68,... | collective-permute-start | bytes 245768 | tf_op jit(solution)/shard_map/ppermute | solution.py:574
  26.5 0.7 %shard_map.103 = (bf16[73,16,128]{2,1,0:T(8,128)(2,1)S(1)}, bf16[73,16,128]{2,1,0:T(8,128)(2,1)S(1)}, f32[8,16,128]{2,1,0:T(8,128)S(1)}) custom-call(bf16[2,8,256,128]{3,2,1,0:T(8,128)(2,1)S(1)} %get-tuple-element.46.own_tiles, bf16[2,8,128,128]{3,2,1,0:T(8,128)(2,1)S(1)} %get-tuple-element.47.corner_tiles, s32[2,6,8]{2,1,0:T(8,128)S(4)} %get-tuple-element.44.table, ...), custom_call_target="tpu_custom_call" | custom-call | flops 33554432 | bytes 1048576 | tf_op jit(solution)/shard_map/pallas_call | solution.py:653
  27.2 1.4 %collective-permute-done.7.new_x = bf16[10,32,128]{2,1,0:T(8,128)(2,1)S(1)} collective-permute-done((bf16[10,32,128]{2,1,0:T(8,128)(2,1)S(1)}, bf16[10,32,128]{2,1,0:T(8,128)(2,1)S(1)}, u32[]{:S(2)}, u32[]{:S(2)}) %collective-permute-start.7) | collective-permute-done | bytes 81952 | tf_op jit(solution)/shard_map/ppermute | solution.py:574
  28.6 2.0 %shard_map.104 = (f32[128,1,128]{2,1,0:T(1,128)}, f32[8,16,128]{2,1,0:T(8,128)S(1)}, f32[2,8,16,128]{3,2,1,0:T(8,128)S(1)}) custom-call(bf16[2,8,256,128]{3,2,1,0:T(8,128)(2,1)S(1)} %get-tuple-element.46.own_tiles, bf16[2,8,128,128]{3,2,1,0:T(8,128)(2,1)S(1)} %get-tuple-element.47.corner_tiles, f32[2,8,16,128]{3,2,1,0:T(8,128)S(1)} %copy-done.1, ...), custom_call_target="tpu_custom_call" | custom-call | flops 67108864 | bytes 1048576 | tf_op jit(solution)/shard_map/pallas_call | solution.py:659
  30.5 15.5 %all-to-all-start = ((f32[128,1,128]{2,1,0:T(1,128)}), f32[128,1,128]{2,1,0:T(1,128)S(1)}, u32[]{:S(2)}, u32[]{:S(2)}) async-start(f32[128,1,128]{2,1,0:T(1,128)} %get-tuple-element.77), calls=%async_computation | async-start | bytes 131072 | tf_op jit(solution)/shard_map/all_to_all | solution.py:677
  46.0 1.3 %shard_map.105 = f32[6,2,8,16,128]{4,3,2,1,0:T(8,128)} custom-call(f32[2,8,16,128]{3,2,1,0:T(8,128)S(1)} %copy-done.1, s32[2,6,8]{2,1,0:T(8,128)S(4)} %get-tuple-element.44.table, f32[6,5]{1,0:T(8,128)S(4)} %get-tuple-element.45.scales, f32[8,16,128]{2,1,0:T(8,128)S(1)} %get-tuple-element.53.first_a.first, ...), custom_call_target="tpu_custom_call" | custom-call | flops 16777216 | bytes 1048576 | tf_op jit(solution)/shard_map/pallas_call | solution.py:670
  47.3 8.4 %all-to-all-done.gathered = f32[128,1,128]{2,1,0:T(1,128)S(1)} async-done(((f32[128,1,128]{2,1,0:T(1,128)}), f32[128,1,128]{2,1,0:T(1,128)S(1)}, u32[]{:S(2)}, u32[]{:S(2)}) %all-to-all-start) | async-done | bytes 65568 | tf_op jit(solution)/shard_map/all_to_all | solution.py:677
  55.7 0.8 %finish.1 = f32[6,16]{1,0:T(8,128)} custom-call(f32[128,1,128]{2,1,0:T(1,128)S(1)} %all-to-all-done.gathered), custom_call_target="tpu_custom_call" | custom-call | tf_op jit(solution)/shard_map/finish/pallas_call | solution.py:678
  (10 shorter events, 0.2 us)
Async XLA Ops:
  0.6 4.6 %copy-start.1 = (f32[2,8,16,128]{3,2,1,0:T(8,128)S(1)}, f32[2,8,16,128]{3,2,1,0:T(8,128)}, u32[]{:S(2)}) copy-start(f32[2,8,16,128]{3,2,1,0:T(8,128)} %signals.11) | copy-start | bytes 393220
  0.6 4.6 %copy-start = (bf16[2,8,4,128,128]{4,3,2,1,0:T(8,128)(2,1)S(1)}, bf16[2,8,4,128,128]{4,3,2,1,0:T(8,128)(2,1)}, u32[]{:S(2)}) copy-start(bf16[2,8,4,128,128]{4,3,2,1,0:T(8,128)(2,1)} %tiles.5) | copy-start | bytes 6291460
  2.1 3.8 %collective-permute-start = (bf16[2,64,128]{2,1,0:T(8,128)(2,1)S(1)}, bf16[2,64,128]{2,1,0:T(8,128)(2,1)S(1)}, u32[]{:S(2)}, u32[]{:S(2)}) collective-permute-start(bf16[2,64,128]{2,1,0:T(8,128)(2,1)S(1)} %get-tuple-element.48), channel_id=1, source_target_pairs={{0,1},{2,3},{1,0},{3,2},{4,5},{6,7},{5,4},{7,6},{8,9},{10,11},{9,8... | collective-permute-start | bytes 98312 | tf_op jit(solution)/shard_map/ppermute | solution.py:571
  4.6 1.3 %collective-permute-start.1 = (bf16[2,64,128]{2,1,0:T(8,128)(2,1)S(1)}, bf16[2,64,128]{2,1,0:T(8,128)(2,1)S(1)}, u32[]{:S(2)}, u32[]{:S(2)}) collective-permute-start(bf16[2,64,128]{2,1,0:T(8,128)(2,1)S(1)} %get-tuple-element.49), channel_id=1, source_target_pairs={{1,2},{2,1},{5,6},{6,5},{9,10},{10,9},{13,14},{14,13},{17,18},{18,... | collective-permute-start | bytes 98312 | tf_op jit(solution)/shard_map/ppermute | solution.py:570
  6.2 7.0 %collective-permute-start.2 = (bf16[10,64,128]{2,1,0:T(8,128)(2,1)S(1)}, bf16[10,64,128]{2,1,0:T(8,128)(2,1)S(1)}, u32[]{:S(2)}, u32[]{:S(2)}) collective-permute-start(bf16[10,64,128]{2,1,0:T(8,128)(2,1)S(1)} %get-tuple-element.52), channel_id=1, source_target_pairs={{0,4},{4,0},{1,5},{5,1},{2,6},{6,2},{3,7},{7,3},{8,12},{12,8},{9,1... | collective-permute-start | bytes 491528 | tf_op jit(solution)/shard_map/ppermute | solution.py:575
  7.8 6.6 %collective-permute-start.3 = (bf16[10,64,128]{2,1,0:T(8,128)(2,1)S(1)}, bf16[10,64,128]{2,1,0:T(8,128)(2,1)S(1)}, u32[]{:S(2)}, u32[]{:S(2)}) collective-permute-start(bf16[10,64,128]{2,1,0:T(8,128)(2,1)S(1)} %get-tuple-element.54), channel_id=1, source_target_pairs={{4,8},{12,16},{20,24},{28,32},{36,40},{44,48},{52,56},{60,64},{68,... | collective-permute-start | bytes 491528 | tf_op jit(solution)/shard_map/ppermute | solution.py:574
  15.9 6.3 %collective-permute-start.4 = (bf16[2,32,128]{2,1,0:T(8,128)(2,1)S(1)}, bf16[2,32,128]{2,1,0:T(8,128)(2,1)S(1)}, u32[]{:S(2)}, u32[]{:S(2)}) collective-permute-start(bf16[2,32,128]{2,1,0:T(8,128)(2,1)S(1)} %get-tuple-element.60), channel_id=1, source_target_pairs={{0,1},{2,3},{1,0},{3,2},{4,5},{6,7},{5,4},{7,6},{8,9},{10,11},{9,8... | collective-permute-start | bytes 49160 | tf_op jit(solution)/shard_map/ppermute | solution.py:571
  21.0 1.1 %collective-permute-start.5 = (bf16[2,32,128]{2,1,0:T(8,128)(2,1)S(1)}, bf16[2,32,128]{2,1,0:T(8,128)(2,1)S(1)}, u32[]{:S(2)}, u32[]{:S(2)}) collective-permute-start(bf16[2,32,128]{2,1,0:T(8,128)(2,1)S(1)} %get-tuple-element.61), channel_id=1, source_target_pairs={{1,2},{2,1},{5,6},{6,5},{9,10},{10,9},{13,14},{14,13},{17,18},{18,... | collective-permute-start | bytes 49160 | tf_op jit(solution)/shard_map/ppermute | solution.py:570
  22.4 4.1 %collective-permute-start.6 = (bf16[10,32,128]{2,1,0:T(8,128)(2,1)S(1)}, bf16[10,32,128]{2,1,0:T(8,128)(2,1)S(1)}, u32[]{:S(2)}, u32[]{:S(2)}) collective-permute-start(bf16[10,32,128]{2,1,0:T(8,128)(2,1)S(1)} %get-tuple-element.64), channel_id=1, source_target_pairs={{0,4},{4,0},{1,5},{5,1},{2,6},{6,2},{3,7},{7,3},{8,12},{12,8},{9,1... | collective-permute-start | bytes 245768 | tf_op jit(solution)/shard_map/ppermute | solution.py:575
  22.4 6.1 %collective-permute-start.7 = (bf16[10,32,128]{2,1,0:T(8,128)(2,1)S(1)}, bf16[10,32,128]{2,1,0:T(8,128)(2,1)S(1)}, u32[]{:S(2)}, u32[]{:S(2)}) collective-permute-start(bf16[10,32,128]{2,1,0:T(8,128)(2,1)S(1)} %get-tuple-element.69), channel_id=1, source_target_pairs={{4,8},{12,16},{20,24},{28,32},{36,40},{44,48},{52,56},{60,64},{68,... | collective-permute-start | bytes 245768 | tf_op jit(solution)/shard_map/ppermute | solution.py:574
  30.5 25.2 %all-to-all-start = ((f32[128,1,128]{2,1,0:T(1,128)}), f32[128,1,128]{2,1,0:T(1,128)S(1)}, u32[]{:S(2)}, u32[]{:S(2)}) async-start(f32[128,1,128]{2,1,0:T(1,128)} %get-tuple-element.77), calls=%async_computation | async-start | bytes 131072 | tf_op jit(solution)/shard_map/all_to_all | solution.py:677

commit v7 on v6

--- a/solution.py
+++ b/solution.py
@@ -430,7 +430,7 @@
 
 def step_1b(
     own_tiles, corner_tiles, signals, table, spectral, from_a, from_b, from_x, room_in, room2_in, degree_a, first_a,
-    degree, first, ghost_degree, ghost_first, second, out_a, out_b, room, room2,
+    degree, first, ghost_degree, ghost_first, second, out_a, out_b, room2, room,
 ):
     frame, weights = Frame(), (own_tiles, corner_tiles)
     factor = 2.0 / jnp.full((16, 128), spectral[0])
@@ -440,22 +440,36 @@
     fill_x(frame, room, FIRST, from_x, 4, 5)
     halos = (from_a, from_b, from_x)
     half_1(frame, 3, weights, signals, table, factor, halos, room, room2, degree, first, ghost_degree, ghost_first)
-    for u, degrees, firsts in ((2, degree_a, first_a), (3, degree, first)):
+    rows = ((2, degree_a, first_a), (3, degree, first))
+    second_step(frame, (0, 1, COLS - 2, COLS - 1), weights, signals, table, factor, room2, rows, second)
+    for out, v, v2 in ((out_a, COLS - 1, COLS - 2), (out_b, 0, 1)):
+        for u in (2, 3):
+            message_2(out, frame.row(u), second, weights, table, u, v, u, v2, frame)
+
+
+def second_step(frame, cols, weights, signals, table, factor, room2, rows, second):
+    for u, degrees, firsts in rows:
         row = frame.row(u)
-        for v in range(COLS):
+        for v in cols:
             col = frame.col(v)
             value = firsts[v]
             sums = own_product(weights, table, row, col, room2, value.astype(BF16))
             alive = alive_of(table, row, col)
             result = 2.0 * (factor * (degrees[v] * value - sums * alive) - value)
             second[u - 2, v] = result - signals[row, col] * alive
-    for out, v, v2 in ((out_a, COLS - 1, COLS - 2), (out_b, 0, 1)):
-        for u in (2, 3):
-            message_2(out, frame.row(u), second, weights, table, u, v, u, v2, frame)
-
-
-def pack_x2(second, own_tiles, table, out_s, out_x, products):
-    frame, weights = Frame(), (own_tiles,)
+
+
+def pack_x2(
+    edges, own_tiles, corner_tiles, signals, table, spectral, room2, degree_a, degree, first_a, first,
+    out_s, out_x, products, second,
+):
+    frame, weights = Frame(), (own_tiles, corner_tiles)
+    factor = 2.0 / jnp.full((16, 128), spectral[0])
+    for u in (2, 3):
+        for v in (0, 1, COLS - 2, COLS - 1):
+            second[u - 2, v] = edges[u - 2, v]
+    rows = ((2, degree_a, first_a), (3, degree, first))
+    second_step(frame, range(2, COLS - 2), weights, signals, table, factor, room2, rows, second)
     for out, u in ((out_s, 2), (out_x, 3)):
         for v in range(COLS):
             products[u - 2, v] = message_2(out, frame.col(v) + 1, second, weights, table, u, v, 5 - u, v, frame)
@@ -633,17 +647,17 @@
     room_1, room_2, degree_a, first_a, ghost_degree_a, ghost_first_a = call(
         step_1a, [wide_room, room, half, half, extra, extra], [VMEM] * 3 + [SMEM] * 2 + [VMEM] * 3, [VMEM] * 6, flops=1 << 25
     )(own_tiles, corner_tiles, signals, table, spectral_bound, a, b, s)
-    degree_b, first_b, ghost_degree_b, ghost_first_b, second, a2, b2 = call(
+    degree_b, first_b, ghost_degree_b, ghost_first_b, edges, a2, b2, room_3 = call(
         step_1b,
-        [half, half, extra, extra, full, short_z, short_z],
+        [half, half, extra, extra, full, short_z, short_z, room],
         [VMEM] * 3 + [SMEM] * 2 + [VMEM] * 7,
-        [VMEM] * 7,
-        [wide_scratch, scratch],
+        [VMEM] * 8,
+        [wide_scratch],
         flops=1 << 26,
     )(own_tiles, corner_tiles, signals, table, spectral_bound, a, b, x, room_1, room_2, degree_a, first_a)
-    s2, x2, products = call(
-        pack_x2, [short_x] * 2 + [full], [VMEM, VMEM, SMEM], [VMEM] * 3, flops=1 << 20
-    )(second, own_tiles, table)
+    s2, x2, products, second = call(
+        pack_x2, [short_x] * 2 + [full] * 2, [VMEM] * 4 + [SMEM] * 2 + [VMEM] * 5, [VMEM] * 4, flops=1 << 20
+    )(edges, own_tiles, corner_tiles, signals, table, spectral_bound, room_3, degree_a, degree_b, first_a, first_b)
     a2, b2 = swap_z(a2, b2)
     corner_room = [pltpu.VMEM((2, 2, 32, 128), BF16), pltpu.SemaphoreType.DMA((2, 2))]
     s2, x2 = call(

time: 56.8 us -> 56.6 us (level)
  transfers between devices with their start and end apart: 9 -> 9, of which waited for: 5 -> 4; matrix products, arithmetic and copies ran while one was open for 0% -> 0% of each run, Pallas kernels for 9% -> 9%
where the time goes in v7:
time: 56.6 us; the launch traced here: 56.3 us
  starting transfers between devices  33.3 us (59%)
  Pallas kernels  11.2 us (20%)
  waiting for transfers between devices  10.4 us (18%)
  between operations  1.43 us (3%)
    all_to_all x1, starting transfers between devices, shards(): gathered = lax.all_to_all(partial, GX_GY, 0, 0)  15.5 us
    all_to_all x1, waiting for transfers between devices, shards(): gathered = lax.all_to_all(partial, GX_GY, 0, 0)  8.44 us
    ppermute x2, starting transfers between devices, swap_z(): return (lax.ppermute(a, 'gy', neighbour_pairs(devices_z, 0)), b)  7.72 us
    ppermute x2, starting transfers between devices, swap_x(): far = lax.ppermute(x, GX, neighbour_pairs(devices_x, 1))  7.14 us
    pallas_call x1, Pallas kernels, shards(): call(step_3b, [pltpu.VMEM((devices, 1, 128), F32), half, full], [VMEM] *...  1.96 us
    ppermute x2, waiting for transfers between devices, swap_x(): far = lax.ppermute(x, GX, neighbour_pairs(devices_x, 1))  1.73 us
    ppermute x2, starting transfers between devices, swap_x(): return (lax.ppermute(s, 'gx_2', [(0, 1), (1, 0)]), far)  1.71 us
    pallas_call x1, Pallas kernels, shards(): call(turn_tiles, [shape((ROWS, COLS, 128, 128)), shape((ROWS, COLS, 256,...  1.51 us
  transfers between devices with their start and end apart: 9, of which 4 were waited for; matrix products, arithmetic and copies ran while one was open for 0% of the time, Pallas kernels for 9%

profile of v7, /device:TPU:1, one launch (start us, length us, event | category | flops | bytes accessed | tf_op | source)
XLA Modules:
  0.0 56.3 jit_solution(15597637000357676418)
XLA Ops:
  0.7 1.4 %shard_map.95 = (bf16[2,64,128]{2,1,0:T(8,128)(2,1)S(1)}, bf16[2,64,128]{2,1,0:T(8,128)(2,1)S(1)}, s32[2,4,8]{2,1,0:T(4,128)S(4)}, s32[2,4,8]{2,1,0:T(4,128)S(4)...) custom-call(bf16[2,8,4,128,128]{4,3,2,1,0:T(8,128)(2,1)} %tiles.5, f32[2,8,16,128]{3,2,1,0:T(8,128)} %signals.13, ...), custom_call_target="tpu_custom_call" | custom-call | flops 1000 | bytes 1048576 | tf_op jit(solution)/shard_map/pallas_call | solution.py:606
  2.1 2.5 %collective-permute-start = (bf16[2,64,128]{2,1,0:T(8,128)(2,1)S(1)}, bf16[2,64,128]{2,1,0:T(8,128)(2,1)S(1)}, u32[]{:S(2)}, u32[]{:S(2)}) collective-permute-start(bf16[2,64,128]{2,1,0:T(8,128)(2,1)S(1)} %get-tuple-element.50), channel_id=1, source_target_pairs={{0,1},{2,3},{1,0},{3,2},{4,5},{6,7},{5,4},{7,6},{8,9},{10,11},{9,8... | collective-permute-start | bytes 98312 | tf_op jit(solution)/shard_map/ppermute | solution.py:585
  4.6 0.7 %collective-permute-start.1 = (bf16[2,64,128]{2,1,0:T(8,128)(2,1)S(1)}, bf16[2,64,128]{2,1,0:T(8,128)(2,1)S(1)}, u32[]{:S(2)}, u32[]{:S(2)}) collective-permute-start(bf16[2,64,128]{2,1,0:T(8,128)(2,1)S(1)} %get-tuple-element.51), channel_id=1, source_target_pairs={{1,2},{2,1},{5,6},{6,5},{9,10},{10,9},{13,14},{14,13},{17,18},{18,... | collective-permute-start | bytes 98312 | tf_op jit(solution)/shard_map/ppermute | solution.py:584
  5.3 0.4 shard_map.97
  5.7 0.2 collective-permute-done.from_a
  5.9 0.3 shard_map.98
  6.2 1.6 %collective-permute-start.2 = (bf16[10,64,128]{2,1,0:T(8,128)(2,1)S(1)}, bf16[10,64,128]{2,1,0:T(8,128)(2,1)S(1)}, u32[]{:S(2)}, u32[]{:S(2)}) collective-permute-start(bf16[10,64,128]{2,1,0:T(8,128)(2,1)S(1)} %get-tuple-element.54), channel_id=1, source_target_pairs={{0,4},{4,0},{1,5},{5,1},{2,6},{6,2},{3,7},{7,3},{8,12},{12,8},{9,1... | collective-permute-start | bytes 491528 | tf_op jit(solution)/shard_map/ppermute | solution.py:589
  7.8 3.2 %collective-permute-start.3 = (bf16[10,64,128]{2,1,0:T(8,128)(2,1)S(1)}, bf16[10,64,128]{2,1,0:T(8,128)(2,1)S(1)}, u32[]{:S(2)}, u32[]{:S(2)}) collective-permute-start(bf16[10,64,128]{2,1,0:T(8,128)(2,1)S(1)} %get-tuple-element.56), channel_id=1, source_target_pairs={{4,8},{12,16},{20,24},{28,32},{36,40},{44,48},{52,56},{60,64},{68,... | collective-permute-start | bytes 491528 | tf_op jit(solution)/shard_map/ppermute | solution.py:588
  11.7 1.5 %shard_map.96 = (bf16[2,8,128,128]{3,2,1,0:T(8,128)(2,1)S(1)}, bf16[2,8,256,128]{3,2,1,0:T(8,128)(2,1)S(1)}, s32[2,6,8]{2,1,0:T(8,128)S(4)}, f32[6,5]{1,0:T(8,128)S(4)}) custom-call(bf16[2,8,4,128,128]{4,3,2,1,0:T(8,128)(2,1)S(1)} %copy-done, s32[2,4,8]{2,1,0:T(4,128)S(4)} %get-tuple-element.42.dirs_s.dirs, s32[2,4,8]{2,1,0:T(4,128)S(4)} %get-tuple-element.43.masks_s.masks, ...), custom_call_target="tpu_custom_call" | custom-call | flops 8388608 | bytes 1048576 | tf_op jit(solution)/shard_map/pallas_call | solution.py:627
  13.2 0.9 %shard_map.99 = (bf16[73,32,128]{2,1,0:T(8,128)(2,1)S(1)}, bf16[73,16,128]{2,1,0:T(8,128)(2,1)S(1)}, f32[8,16,128]{2,1,0:T(8,128)S(1)}, f32[8,16,128]{2,1,0:T(8,...) custom-call(bf16[2,8,256,128]{3,2,1,0:T(8,128)(2,1)S(1)} %get-tuple-element.48.own_tiles, ...), custom_call_target="tpu_custom_call" | custom-call | flops 33554432 | bytes 1048576 | tf_op jit(solution)/shard_map/pallas_call | solution.py:647
  14.1 0.4 collective-permute-done.3.from_x
  14.4 1.2 %shard_map.100 = (f32[8,16,128]{2,1,0:T(8,128)S(1)}, f32[8,16,128]{2,1,0:T(8,128)S(1)}, f32[12,16,128]{2,1,0:T(8,128)S(1)}, f32[12,16,128]{2,1,0:T(8,128)S(1)}, ...) custom-call(bf16[2,8,256,128]{3,2,1,0:T(8,128)(2,1)S(1)} %get-tuple-, ...), custom_call_target="tpu_custom_call" | custom-call | flops 67108864 | bytes 1048576 | tf_op jit(solution)/shard_map/pallas_call | solution.py:650
  15.7 5.2 %collective-permute-start.4 = (bf16[2,32,128]{2,1,0:T(8,128)(2,1)S(1)}, bf16[2,32,128]{2,1,0:T(8,128)(2,1)S(1)}, u32[]{:S(2)}, u32[]{:S(2)}) collective-permute-start(bf16[2,32,128]{2,1,0:T(8,128)(2,1)S(1)} %get-tuple-element.65), channel_id=1, source_target_pairs={{0,1},{2,3},{1,0},{3,2},{4,5},{6,7},{5,4},{7,6},{8,9},{10,11},{9,8... | collective-permute-start | bytes 49160 | tf_op jit(solution)/shard_map/ppermute | solution.py:585
  20.9 0.7 %collective-permute-start.5 = (bf16[2,32,128]{2,1,0:T(8,128)(2,1)S(1)}, bf16[2,32,128]{2,1,0:T(8,128)(2,1)S(1)}, u32[]{:S(2)}, u32[]{:S(2)}) collective-permute-start(bf16[2,32,128]{2,1,0:T(8,128)(2,1)S(1)} %get-tuple-element.66), channel_id=1, source_target_pairs={{1,2},{2,1},{5,6},{6,5},{9,10},{10,9},{13,14},{14,13},{17,18},{18,... | collective-permute-start | bytes 49160 | tf_op jit(solution)/shard_map/ppermute | solution.py:584
  21.5 0.5 shard_map.101
  22.0 0.2 shard_map.102
  22.3 3.9 %collective-permute-start.7 = (bf16[10,32,128]{2,1,0:T(8,128)(2,1)S(1)}, bf16[10,32,128]{2,1,0:T(8,128)(2,1)S(1)}, u32[]{:S(2)}, u32[]{:S(2)}) collective-permute-start(bf16[10,32,128]{2,1,0:T(8,128)(2,1)S(1)} %get-tuple-element.74), channel_id=1, source_target_pairs={{4,8},{12,16},{20,24},{28,32},{36,40},{44,48},{52,56},{60,64},{68,... | collective-permute-start | bytes 245768 | tf_op jit(solution)/shard_map/ppermute | solution.py:588
  26.3 0.7 %shard_map.103 = (bf16[73,16,128]{2,1,0:T(8,128)(2,1)S(1)}, bf16[73,16,128]{2,1,0:T(8,128)(2,1)S(1)}, f32[8,16,128]{2,1,0:T(8,128)S(1)}) custom-call(bf16[2,8,256,128]{3,2,1,0:T(8,128)(2,1)S(1)} %get-tuple-element.48.own_tiles, bf16[2,8,128,128]{3,2,1,0:T(8,128)(2,1)S(1)} %get-tuple-element.49.corner_tiles, s32[2,6,8]{2,1,0:T(8,128)S(4)} %get-tuple-element.46.table, ...), custom_call_target="tpu_custom_call" | custom-call | flops 33554432 | bytes 1048576 | tf_op jit(solution)/shard_map/pallas_call | solution.py:667
  27.0 1.4 %collective-permute-done.7.new_x = bf16[10,32,128]{2,1,0:T(8,128)(2,1)S(1)} collective-permute-done((bf16[10,32,128]{2,1,0:T(8,128)(2,1)S(1)}, bf16[10,32,128]{2,1,0:T(8,128)(2,1)S(1)}, u32[]{:S(2)}, u32[]{:S(2)}) %collective-permute-start.7) | collective-permute-done | bytes 81952 | tf_op jit(solution)/shard_map/ppermute | solution.py:588
  28.4 2.0 %shard_map.104 = (f32[128,1,128]{2,1,0:T(1,128)}, f32[8,16,128]{2,1,0:T(8,128)S(1)}, f32[2,8,16,128]{3,2,1,0:T(8,128)S(1)}) custom-call(bf16[2,8,256,128]{3,2,1,0:T(8,128)(2,1)S(1)} %get-tuple-element.48.own_tiles, bf16[2,8,128,128]{3,2,1,0:T(8,128)(2,1)S(1)} %get-tuple-element.49.corner_tiles, f32[2,8,16,128]{3,2,1,0:T(8,128)S(1)} %copy-done.1, ...), custom_call_target="tpu_custom_call" | custom-call | flops 67108864 | bytes 1048576 | tf_op jit(solution)/shard_map/pallas_call | solution.py:673
  30.3 15.5 %all-to-all-start = ((f32[128,1,128]{2,1,0:T(1,128)}), f32[128,1,128]{2,1,0:T(1,128)S(1)}, u32[]{:S(2)}, u32[]{:S(2)}) async-start(f32[128,1,128]{2,1,0:T(1,128)} %get-tuple-element.81), calls=%async_computation | async-start | bytes 131072 | tf_op jit(solution)/shard_map/all_to_all | solution.py:691
  45.8 1.3 %shard_map.105 = f32[6,2,8,16,128]{4,3,2,1,0:T(8,128)} custom-call(f32[2,8,16,128]{3,2,1,0:T(8,128)S(1)} %copy-done.1, s32[2,6,8]{2,1,0:T(8,128)S(4)} %get-tuple-element.46.table, f32[6,5]{1,0:T(8,128)S(4)} %get-tuple-element.47.scales, f32[8,16,128]{2,1,0:T(8,128)S(1)} %get-tuple-element.55.first_a.first, ...), custom_call_target="tpu_custom_call" | custom-call | flops 16777216 | bytes 1048576 | tf_op jit(solution)/shard_map/pallas_call | solution.py:684
  47.1 8.4 %all-to-all-done.gathered = f32[128,1,128]{2,1,0:T(1,128)S(1)} async-done(((f32[128,1,128]{2,1,0:T(1,128)}), f32[128,1,128]{2,1,0:T(1,128)S(1)}, u32[]{:S(2)}, u32[]{:S(2)}) %all-to-all-start) | async-done | bytes 65568 | tf_op jit(solution)/shard_map/all_to_all | solution.py:691
  55.5 0.8 %finish.1 = f32[6,16]{1,0:T(8,128)} custom-call(f32[128,1,128]{2,1,0:T(1,128)S(1)} %all-to-all-done.gathered), custom_call_target="tpu_custom_call" | custom-call | tf_op jit(solution)/shard_map/finish/pallas_call | solution.py:692
  (10 shorter events, 0.1 us)
Async XLA Ops:
  0.6 4.6 %copy-start.1 = (f32[2,8,16,128]{3,2,1,0:T(8,128)S(1)}, f32[2,8,16,128]{3,2,1,0:T(8,128)}, u32[]{:S(2)}) copy-start(f32[2,8,16,128]{3,2,1,0:T(8,128)} %signals.13) | copy-start | bytes 393220
  0.6 4.6 %copy-start = (bf16[2,8,4,128,128]{4,3,2,1,0:T(8,128)(2,1)S(1)}, bf16[2,8,4,128,128]{4,3,2,1,0:T(8,128)(2,1)}, u32[]{:S(2)}) copy-start(bf16[2,8,4,128,128]{4,3,2,1,0:T(8,128)(2,1)} %tiles.5) | copy-start | bytes 6291460
  2.1 3.8 %collective-permute-start = (bf16[2,64,128]{2,1,0:T(8,128)(2,1)S(1)}, bf16[2,64,128]{2,1,0:T(8,128)(2,1)S(1)}, u32[]{:S(2)}, u32[]{:S(2)}) collective-permute-start(bf16[2,64,128]{2,1,0:T(8,128)(2,1)S(1)} %get-tuple-element.50), channel_id=1, source_target_pairs={{0,1},{2,3},{1,0},{3,2},{4,5},{6,7},{5,4},{7,6},{8,9},{10,11},{9,8... | collective-permute-start | bytes 98312 | tf_op jit(solution)/shard_map/ppermute | solution.py:585
  4.6 1.3 %collective-permute-start.1 = (bf16[2,64,128]{2,1,0:T(8,128)(2,1)S(1)}, bf16[2,64,128]{2,1,0:T(8,128)(2,1)S(1)}, u32[]{:S(2)}, u32[]{:S(2)}) collective-permute-start(bf16[2,64,128]{2,1,0:T(8,128)(2,1)S(1)} %get-tuple-element.51), channel_id=1, source_target_pairs={{1,2},{2,1},{5,6},{6,5},{9,10},{10,9},{13,14},{14,13},{17,18},{18,... | collective-permute-start | bytes 98312 | tf_op jit(solution)/shard_map/ppermute | solution.py:584
  6.2 7.0 %collective-permute-start.2 = (bf16[10,64,128]{2,1,0:T(8,128)(2,1)S(1)}, bf16[10,64,128]{2,1,0:T(8,128)(2,1)S(1)}, u32[]{:S(2)}, u32[]{:S(2)}) collective-permute-start(bf16[10,64,128]{2,1,0:T(8,128)(2,1)S(1)} %get-tuple-element.54), channel_id=1, source_target_pairs={{0,4},{4,0},{1,5},{5,1},{2,6},{6,2},{3,7},{7,3},{8,12},{12,8},{9,1... | collective-permute-start | bytes 491528 | tf_op jit(solution)/shard_map/ppermute | solution.py:589
  7.8 6.6 %collective-permute-start.3 = (bf16[10,64,128]{2,1,0:T(8,128)(2,1)S(1)}, bf16[10,64,128]{2,1,0:T(8,128)(2,1)S(1)}, u32[]{:S(2)}, u32[]{:S(2)}) collective-permute-start(bf16[10,64,128]{2,1,0:T(8,128)(2,1)S(1)} %get-tuple-element.56), channel_id=1, source_target_pairs={{4,8},{12,16},{20,24},{28,32},{36,40},{44,48},{52,56},{60,64},{68,... | collective-permute-start | bytes 491528 | tf_op jit(solution)/shard_map/ppermute | solution.py:588
  15.7 6.3 %collective-permute-start.4 = (bf16[2,32,128]{2,1,0:T(8,128)(2,1)S(1)}, bf16[2,32,128]{2,1,0:T(8,128)(2,1)S(1)}, u32[]{:S(2)}, u32[]{:S(2)}) collective-permute-start(bf16[2,32,128]{2,1,0:T(8,128)(2,1)S(1)} %get-tuple-element.65), channel_id=1, source_target_pairs={{0,1},{2,3},{1,0},{3,2},{4,5},{6,7},{5,4},{7,6},{8,9},{10,11},{9,8... | collective-permute-start | bytes 49160 | tf_op jit(solution)/shard_map/ppermute | solution.py:585
  20.9 1.2 %collective-permute-start.5 = (bf16[2,32,128]{2,1,0:T(8,128)(2,1)S(1)}, bf16[2,32,128]{2,1,0:T(8,128)(2,1)S(1)}, u32[]{:S(2)}, u32[]{:S(2)}) collective-permute-start(bf16[2,32,128]{2,1,0:T(8,128)(2,1)S(1)} %get-tuple-element.66), channel_id=1, source_target_pairs={{1,2},{2,1},{5,6},{6,5},{9,10},{10,9},{13,14},{14,13},{17,18},{18,... | collective-permute-start | bytes 49160 | tf_op jit(solution)/shard_map/ppermute | solution.py:584
  22.2 4.0 %collective-permute-start.6 = (bf16[10,32,128]{2,1,0:T(8,128)(2,1)S(1)}, bf16[10,32,128]{2,1,0:T(8,128)(2,1)S(1)}, u32[]{:S(2)}, u32[]{:S(2)}) collective-permute-start(bf16[10,32,128]{2,1,0:T(8,128)(2,1)S(1)} %get-tuple-element.69), channel_id=1, source_target_pairs={{0,4},{4,0},{1,5},{5,1},{2,6},{6,2},{3,7},{7,3},{8,12},{12,8},{9,1... | collective-permute-start | bytes 245768 | tf_op jit(solution)/shard_map/ppermute | solution.py:589
  22.3 6.1 %collective-permute-start.7 = (bf16[10,32,128]{2,1,0:T(8,128)(2,1)S(1)}, bf16[10,32,128]{2,1,0:T(8,128)(2,1)S(1)}, u32[]{:S(2)}, u32[]{:S(2)}) collective-permute-start(bf16[10,32,128]{2,1,0:T(8,128)(2,1)S(1)} %get-tuple-element.74), channel_id=1, source_target_pairs={{4,8},{12,16},{20,24},{28,32},{36,40},{44,48},{52,56},{60,64},{68,... | collective-permute-start | bytes 245768 | tf_op jit(solution)/shard_map/ppermute | solution.py:588
  30.3 25.2 %all-to-all-start = ((f32[128,1,128]{2,1,0:T(1,128)}), f32[128,1,128]{2,1,0:T(1,128)S(1)}, u32[]{:S(2)}, u32[]{:S(2)}) async-start(f32[128,1,128]{2,1,0:T(1,128)} %get-tuple-element.81), calls=%async_computation | async-start | bytes 131072 | tf_op jit(solution)/shard_map/all_to_all | solution.py:691

commit v8 on v7

--- a/solution.py
+++ b/solution.py
@@ -134,6 +134,14 @@
     return copies
 
 
+def no_message_outside(out):
+    z = lax.axis_index("gy")
+
+    @pl.when((z == 0) | (z == lax.axis_size("gy") - 1))
+    def _():
+        out[...] = jnp.zeros_like(out)
+
+
 def pack_z(
     tiles, signals, dirs, masks, live, bound, out_a, out_b, dirs_s, masks_s, live_s, bound_s, raw, signals_v, sem, sem2
 ):
@@ -151,6 +159,7 @@
         col, col2 = jnp.where(right, COLS - 1, 0), jnp.where(right, COLS - 2, 1)
         for row in range(ROWS):
             block_message(out, row, refs, [raw[which, row, slot] for slot in range(SLOTS)], row, col, row, col2)
+    no_message_outside(out_b)
 
 
 def pack_x(tiles, signals, dirs, masks, live, bound, out_s, out_b):
@@ -445,6 +454,7 @@
     for out, v, v2 in ((out_a, COLS - 1, COLS - 2), (out_b, 0, 1)):
         for u in (2, 3):
             message_2(out, frame.row(u), second, weights, table, u, v, u, v2, frame)
+    no_message_outside(out_b)
 
 
 def second_step(frame, cols, weights, signals, table, factor, room2, rows, second):
@@ -581,7 +591,8 @@
     nodes = ROWS * COLS * 128 * devices
 
     def swap_z(a, b):
-        b = lax.ppermute(b, "gy", neighbour_pairs(devices_z, 1))
+        ends = [(0, 0), (devices_z - 1, devices_z - 1)]
+        b = lax.ppermute(b, "gy", neighbour_pairs(devices_z, 1) + ends)
         return lax.ppermute(a, "gy", neighbour_pairs(devices_z, 0)), b
 
     def swap_x(s, x):

time: 56.6 us -> 56.6 us (level)
  no operation moved by 1% of the time
where the time goes in v8:
time: 56.6 us; the launch traced here: 56.3 us
  starting transfers between devices  33.3 us (59%)
  Pallas kernels  11.2 us (20%)
  waiting for transfers between devices  10.4 us (18%)
  between operations  1.43 us (3%)
    all_to_all x1, starting transfers between devices, shards(): gathered = lax.all_to_all(partial, GX_GY, 0, 0)  15.5 us
    all_to_all x1, waiting for transfers between devices, shards(): gathered = lax.all_to_all(partial, GX_GY, 0, 0)  8.44 us
    ppermute x2, starting transfers between devices, swap_z(): return (lax.ppermute(a, 'gy', neighbour_pairs(devices_z, 0)), b)  7.72 us
    ppermute x2, starting transfers between devices, swap_x(): far = lax.ppermute(x, GX, neighbour_pairs(devices_x, 1))  7.15 us
    pallas_call x1, Pallas kernels, shards(): call(step_3b, [pltpu.VMEM((devices, 1, 128), F32), half, full], [VMEM] *...  1.96 us
    ppermute x2, waiting for transfers between devices, swap_x(): far = lax.ppermute(x, GX, neighbour_pairs(devices_x, 1))  1.72 us
    ppermute x2, starting transfers between devices, swap_x(): return (lax.ppermute(s, 'gx_2', [(0, 1), (1, 0)]), far)  1.71 us
    pallas_call x1, Pallas kernels, shards(): call(turn_tiles, [shape((ROWS, COLS, 128, 128)), shape((ROWS, COLS, 256,...  1.51 us
  transfers between devices with their start and end apart: 9, of which 4 were waited for; matrix products, arithmetic and copies ran while one was open for 0% of the time, Pallas kernels for 9%

profile of v8, /device:TPU:1, one launch (start us, length us, event | category | flops | bytes accessed | tf_op | source)
XLA Modules:
  0.0 56.3 jit_solution(17490583130389539474)
XLA Ops:
  0.7 1.4 %shard_map.95 = (bf16[2,64,128]{2,1,0:T(8,128)(2,1)S(1)}, bf16[2,64,128]{2,1,0:T(8,128)(2,1)S(1)}, s32[2,4,8]{2,1,0:T(4,128)S(4)}, s32[2,4,8]{2,1,0:T(4,128)S(4)...) custom-call(bf16[2,8,4,128,128]{4,3,2,1,0:T(8,128)(2,1)} %tiles.5, f32[2,8,16,128]{3,2,1,0:T(8,128)} %signals.13, ...), custom_call_target="tpu_custom_call" | custom-call | flops 1000 | bytes 1048576 | tf_op jit(solution)/shard_map/pallas_call | solution.py:617
  2.1 2.5 %collective-permute-start = (bf16[2,64,128]{2,1,0:T(8,128)(2,1)S(1)}, bf16[2,64,128]{2,1,0:T(8,128)(2,1)S(1)}, u32[]{:S(2)}, u32[]{:S(2)}) collective-permute-start(bf16[2,64,128]{2,1,0:T(8,128)(2,1)S(1)} %get-tuple-element.50), channel_id=1, source_target_pairs={{0,1},{2,3},{1,0},{3,2},{4,5},{6,7},{5,4},{7,6},{8,9},{10,11},{9,8... | collective-permute-start | bytes 98312 | tf_op jit(solution)/shard_map/ppermute | solution.py:596
  4.6 0.7 %collective-permute-start.1 = (bf16[2,64,128]{2,1,0:T(8,128)(2,1)S(1)}, bf16[2,64,128]{2,1,0:T(8,128)(2,1)S(1)}, u32[]{:S(2)}, u32[]{:S(2)}) collective-permute-start(bf16[2,64,128]{2,1,0:T(8,128)(2,1)S(1)} %get-tuple-element.51), channel_id=1, source_target_pairs={{1,2},{2,1},{0,0},{3,3},{5,6},{6,5},{4,4},{7,7},{9,10},{10,9},{8,8... | collective-permute-start | bytes 98312 | tf_op jit(solution)/shard_map/ppermute | solution.py:595
  5.3 0.4 shard_map.97
  5.7 0.2 collective-permute-done.from_a
  5.9 0.3 shard_map.98
  6.2 1.6 %collective-permute-start.2 = (bf16[10,64,128]{2,1,0:T(8,128)(2,1)S(1)}, bf16[10,64,128]{2,1,0:T(8,128)(2,1)S(1)}, u32[]{:S(2)}, u32[]{:S(2)}) collective-permute-start(bf16[10,64,128]{2,1,0:T(8,128)(2,1)S(1)} %get-tuple-element.54), channel_id=1, source_target_pairs={{0,4},{4,0},{1,5},{5,1},{2,6},{6,2},{3,7},{7,3},{8,12},{12,8},{9,1... | collective-permute-start | bytes 491528 | tf_op jit(solution)/shard_map/ppermute | solution.py:600
  7.8 3.2 %collective-permute-start.3 = (bf16[10,64,128]{2,1,0:T(8,128)(2,1)S(1)}, bf16[10,64,128]{2,1,0:T(8,128)(2,1)S(1)}, u32[]{:S(2)}, u32[]{:S(2)}) collective-permute-start(bf16[10,64,128]{2,1,0:T(8,128)(2,1)S(1)} %get-tuple-element.56), channel_id=1, source_target_pairs={{4,8},{12,16},{20,24},{28,32},{36,40},{44,48},{52,56},{60,64},{68,... | collective-permute-start | bytes 491528 | tf_op jit(solution)/shard_map/ppermute | solution.py:599
  11.7 1.5 %shard_map.96 = (bf16[2,8,128,128]{3,2,1,0:T(8,128)(2,1)S(1)}, bf16[2,8,256,128]{3,2,1,0:T(8,128)(2,1)S(1)}, s32[2,6,8]{2,1,0:T(8,128)S(4)}, f32[6,5]{1,0:T(8,128)S(4)}) custom-call(bf16[2,8,4,128,128]{4,3,2,1,0:T(8,128)(2,1)S(1)} %copy-done, s32[2,4,8]{2,1,0:T(4,128)S(4)} %get-tuple-element.42.dirs_s.dirs, s32[2,4,8]{2,1,0:T(4,128)S(4)} %get-tuple-element.43.masks_s.masks, ...), custom_call_target="tpu_custom_call" | custom-call | flops 8388608 | bytes 1048576 | tf_op jit(solution)/shard_map/pallas_call | solution.py:638
  13.2 0.9 %shard_map.99 = (bf16[73,32,128]{2,1,0:T(8,128)(2,1)S(1)}, bf16[73,16,128]{2,1,0:T(8,128)(2,1)S(1)}, f32[8,16,128]{2,1,0:T(8,128)S(1)}, f32[8,16,128]{2,1,0:T(8,...) custom-call(bf16[2,8,256,128]{3,2,1,0:T(8,128)(2,1)S(1)} %get-tuple-element.48.own_tiles, ...), custom_call_target="tpu_custom_call" | custom-call | flops 33554432 | bytes 1048576 | tf_op jit(solution)/shard_map/pallas_call | solution.py:658
  14.1 0.4 collective-permute-done.3.from_x
  14.4 1.2 %shard_map.100 = (f32[8,16,128]{2,1,0:T(8,128)S(1)}, f32[8,16,128]{2,1,0:T(8,128)S(1)}, f32[12,16,128]{2,1,0:T(8,128)S(1)}, f32[12,16,128]{2,1,0:T(8,128)S(1)}, ...) custom-call(bf16[2,8,256,128]{3,2,1,0:T(8,128)(2,1)S(1)} %get-tuple-, ...), custom_call_target="tpu_custom_call" | custom-call | flops 67108864 | bytes 1048576 | tf_op jit(solution)/shard_map/pallas_call | solution.py:661
  15.7 5.2 %collective-permute-start.4 = (bf16[2,32,128]{2,1,0:T(8,128)(2,1)S(1)}, bf16[2,32,128]{2,1,0:T(8,128)(2,1)S(1)}, u32[]{:S(2)}, u32[]{:S(2)}) collective-permute-start(bf16[2,32,128]{2,1,0:T(8,128)(2,1)S(1)} %get-tuple-element.65), channel_id=1, source_target_pairs={{0,1},{2,3},{1,0},{3,2},{4,5},{6,7},{5,4},{7,6},{8,9},{10,11},{9,8... | collective-permute-start | bytes 49160 | tf_op jit(solution)/shard_map/ppermute | solution.py:596
  20.9 0.7 %collective-permute-start.5 = (bf16[2,32,128]{2,1,0:T(8,128)(2,1)S(1)}, bf16[2,32,128]{2,1,0:T(8,128)(2,1)S(1)}, u32[]{:S(2)}, u32[]{:S(2)}) collective-permute-start(bf16[2,32,128]{2,1,0:T(8,128)(2,1)S(1)} %get-tuple-element.66), channel_id=1, source_target_pairs={{1,2},{2,1},{0,0},{3,3},{5,6},{6,5},{4,4},{7,7},{9,10},{10,9},{8,8... | collective-permute-start | bytes 49160 | tf_op jit(solution)/shard_map/ppermute | solution.py:595
  21.5 0.5 shard_map.101
  22.1 0.2 shard_map.102
  22.3 3.9 %collective-permute-start.7 = (bf16[10,32,128]{2,1,0:T(8,128)(2,1)S(1)}, bf16[10,32,128]{2,1,0:T(8,128)(2,1)S(1)}, u32[]{:S(2)}, u32[]{:S(2)}) collective-permute-start(bf16[10,32,128]{2,1,0:T(8,128)(2,1)S(1)} %get-tuple-element.74), channel_id=1, source_target_pairs={{4,8},{12,16},{20,24},{28,32},{36,40},{44,48},{52,56},{60,64},{68,... | collective-permute-start | bytes 245768 | tf_op jit(solution)/shard_map/ppermute | solution.py:599
  26.3 0.7 %shard_map.103 = (bf16[73,16,128]{2,1,0:T(8,128)(2,1)S(1)}, bf16[73,16,128]{2,1,0:T(8,128)(2,1)S(1)}, f32[8,16,128]{2,1,0:T(8,128)S(1)}) custom-call(bf16[2,8,256,128]{3,2,1,0:T(8,128)(2,1)S(1)} %get-tuple-element.48.own_tiles, bf16[2,8,128,128]{3,2,1,0:T(8,128)(2,1)S(1)} %get-tuple-element.49.corner_tiles, s32[2,6,8]{2,1,0:T(8,128)S(4)} %get-tuple-element.46.table, ...), custom_call_target="tpu_custom_call" | custom-call | flops 33554432 | bytes 1048576 | tf_op jit(solution)/shard_map/pallas_call | solution.py:678
  27.0 1.4 %collective-permute-done.7.new_x = bf16[10,32,128]{2,1,0:T(8,128)(2,1)S(1)} collective-permute-done((bf16[10,32,128]{2,1,0:T(8,128)(2,1)S(1)}, bf16[10,32,128]{2,1,0:T(8,128)(2,1)S(1)}, u32[]{:S(2)}, u32[]{:S(2)}) %collective-permute-start.7) | collective-permute-done | bytes 81952 | tf_op jit(solution)/shard_map/ppermute | solution.py:599
  28.4 2.0 %shard_map.104 = (f32[128,1,128]{2,1,0:T(1,128)}, f32[8,16,128]{2,1,0:T(8,128)S(1)}, f32[2,8,16,128]{3,2,1,0:T(8,128)S(1)}) custom-call(bf16[2,8,256,128]{3,2,1,0:T(8,128)(2,1)S(1)} %get-tuple-element.48.own_tiles, bf16[2,8,128,128]{3,2,1,0:T(8,128)(2,1)S(1)} %get-tuple-element.49.corner_tiles, f32[2,8,16,128]{3,2,1,0:T(8,128)S(1)} %copy-done.1, ...), custom_call_target="tpu_custom_call" | custom-call | flops 67108864 | bytes 1048576 | tf_op jit(solution)/shard_map/pallas_call | solution.py:684
  30.3 15.5 %all-to-all-start = ((f32[128,1,128]{2,1,0:T(1,128)}), f32[128,1,128]{2,1,0:T(1,128)S(1)}, u32[]{:S(2)}, u32[]{:S(2)}) async-start(f32[128,1,128]{2,1,0:T(1,128)} %get-tuple-element.81), calls=%async_computation | async-start | bytes 131072 | tf_op jit(solution)/shard_map/all_to_all | solution.py:702
  45.8 1.3 %shard_map.105 = f32[6,2,8,16,128]{4,3,2,1,0:T(8,128)} custom-call(f32[2,8,16,128]{3,2,1,0:T(8,128)S(1)} %copy-done.1, s32[2,6,8]{2,1,0:T(8,128)S(4)} %get-tuple-element.46.table, f32[6,5]{1,0:T(8,128)S(4)} %get-tuple-element.47.scales, f32[8,16,128]{2,1,0:T(8,128)S(1)} %get-tuple-element.55.first_a.first, ...), custom_call_target="tpu_custom_call" | custom-call | flops 16777216 | bytes 1048576 | tf_op jit(solution)/shard_map/pallas_call | solution.py:695
  47.1 8.4 %all-to-all-done.gathered = f32[128,1,128]{2,1,0:T(1,128)S(1)} async-done(((f32[128,1,128]{2,1,0:T(1,128)}), f32[128,1,128]{2,1,0:T(1,128)S(1)}, u32[]{:S(2)}, u32[]{:S(2)}) %all-to-all-start) | async-done | bytes 65568 | tf_op jit(solution)/shard_map/all_to_all | solution.py:702
  55.5 0.8 %finish.1 = f32[6,16]{1,0:T(8,128)} custom-call(f32[128,1,128]{2,1,0:T(1,128)S(1)} %all-to-all-done.gathered), custom_call_target="tpu_custom_call" | custom-call | tf_op jit(solution)/shard_map/finish/pallas_call | solution.py:703
  (10 shorter events, 0.1 us)
Async XLA Ops:
  0.6 4.6 %copy-start.1 = (f32[2,8,16,128]{3,2,1,0:T(8,128)S(1)}, f32[2,8,16,128]{3,2,1,0:T(8,128)}, u32[]{:S(2)}) copy-start(f32[2,8,16,128]{3,2,1,0:T(8,128)} %signals.13) | copy-start | bytes 393220
  0.6 4.6 %copy-start = (bf16[2,8,4,128,128]{4,3,2,1,0:T(8,128)(2,1)S(1)}, bf16[2,8,4,128,128]{4,3,2,1,0:T(8,128)(2,1)}, u32[]{:S(2)}) copy-start(bf16[2,8,4,128,128]{4,3,2,1,0:T(8,128)(2,1)} %tiles.5) | copy-start | bytes 6291460
  2.1 3.8 %collective-permute-start = (bf16[2,64,128]{2,1,0:T(8,128)(2,1)S(1)}, bf16[2,64,128]{2,1,0:T(8,128)(2,1)S(1)}, u32[]{:S(2)}, u32[]{:S(2)}) collective-permute-start(bf16[2,64,128]{2,1,0:T(8,128)(2,1)S(1)} %get-tuple-element.50), channel_id=1, source_target_pairs={{0,1},{2,3},{1,0},{3,2},{4,5},{6,7},{5,4},{7,6},{8,9},{10,11},{9,8... | collective-permute-start | bytes 98312 | tf_op jit(solution)/shard_map/ppermute | solution.py:596
  4.6 1.3 %collective-permute-start.1 = (bf16[2,64,128]{2,1,0:T(8,128)(2,1)S(1)}, bf16[2,64,128]{2,1,0:T(8,128)(2,1)S(1)}, u32[]{:S(2)}, u32[]{:S(2)}) collective-permute-start(bf16[2,64,128]{2,1,0:T(8,128)(2,1)S(1)} %get-tuple-element.51), channel_id=1, source_target_pairs={{1,2},{2,1},{0,0},{3,3},{5,6},{6,5},{4,4},{7,7},{9,10},{10,9},{8,8... | collective-permute-start | bytes 98312 | tf_op jit(solution)/shard_map/ppermute | solution.py:595
  6.2 7.0 %collective-permute-start.2 = (bf16[10,64,128]{2,1,0:T(8,128)(2,1)S(1)}, bf16[10,64,128]{2,1,0:T(8,128)(2,1)S(1)}, u32[]{:S(2)}, u32[]{:S(2)}) collective-permute-start(bf16[10,64,128]{2,1,0:T(8,128)(2,1)S(1)} %get-tuple-element.54), channel_id=1, source_target_pairs={{0,4},{4,0},{1,5},{5,1},{2,6},{6,2},{3,7},{7,3},{8,12},{12,8},{9,1... | collective-permute-start | bytes 491528 | tf_op jit(solution)/shard_map/ppermute | solution.py:600
  7.8 6.6 %collective-permute-start.3 = (bf16[10,64,128]{2,1,0:T(8,128)(2,1)S(1)}, bf16[10,64,128]{2,1,0:T(8,128)(2,1)S(1)}, u32[]{:S(2)}, u32[]{:S(2)}) collective-permute-start(bf16[10,64,128]{2,1,0:T(8,128)(2,1)S(1)} %get-tuple-element.56), channel_id=1, source_target_pairs={{4,8},{12,16},{20,24},{28,32},{36,40},{44,48},{52,56},{60,64},{68,... | collective-permute-start | bytes 491528 | tf_op jit(solution)/shard_map/ppermute | solution.py:599
  15.7 6.3 %collective-permute-start.4 = (bf16[2,32,128]{2,1,0:T(8,128)(2,1)S(1)}, bf16[2,32,128]{2,1,0:T(8,128)(2,1)S(1)}, u32[]{:S(2)}, u32[]{:S(2)}) collective-permute-start(bf16[2,32,128]{2,1,0:T(8,128)(2,1)S(1)} %get-tuple-element.65), channel_id=1, source_target_pairs={{0,1},{2,3},{1,0},{3,2},{4,5},{6,7},{5,4},{7,6},{8,9},{10,11},{9,8... | collective-permute-start | bytes 49160 | tf_op jit(solution)/shard_map/ppermute | solution.py:596
  20.9 1.2 %collective-permute-start.5 = (bf16[2,32,128]{2,1,0:T(8,128)(2,1)S(1)}, bf16[2,32,128]{2,1,0:T(8,128)(2,1)S(1)}, u32[]{:S(2)}, u32[]{:S(2)}) collective-permute-start(bf16[2,32,128]{2,1,0:T(8,128)(2,1)S(1)} %get-tuple-element.66), channel_id=1, source_target_pairs={{1,2},{2,1},{0,0},{3,3},{5,6},{6,5},{4,4},{7,7},{9,10},{10,9},{8,8... | collective-permute-start | bytes 49160 | tf_op jit(solution)/shard_map/ppermute | solution.py:595
  22.2 4.0 %collective-permute-start.6 = (bf16[10,32,128]{2,1,0:T(8,128)(2,1)S(1)}, bf16[10,32,128]{2,1,0:T(8,128)(2,1)S(1)}, u32[]{:S(2)}, u32[]{:S(2)}) collective-permute-start(bf16[10,32,128]{2,1,0:T(8,128)(2,1)S(1)} %get-tuple-element.69), channel_id=1, source_target_pairs={{0,4},{4,0},{1,5},{5,1},{2,6},{6,2},{3,7},{7,3},{8,12},{12,8},{9,1... | collective-permute-start | bytes 245768 | tf_op jit(solution)/shard_map/ppermute | solution.py:600
  22.3 6.1 %collective-permute-start.7 = (bf16[10,32,128]{2,1,0:T(8,128)(2,1)S(1)}, bf16[10,32,128]{2,1,0:T(8,128)(2,1)S(1)}, u32[]{:S(2)}, u32[]{:S(2)}) collective-permute-start(bf16[10,32,128]{2,1,0:T(8,128)(2,1)S(1)} %get-tuple-element.74), channel_id=1, source_target_pairs={{4,8},{12,16},{20,24},{28,32},{36,40},{44,48},{52,56},{60,64},{68,... | collective-permute-start | bytes 245768 | tf_op jit(solution)/shard_map/ppermute | solution.py:599
  30.3 25.2 %all-to-all-start = ((f32[128,1,128]{2,1,0:T(1,128)}), f32[128,1,128]{2,1,0:T(1,128)S(1)}, u32[]{:S(2)}, u32[]{:S(2)}) async-start(f32[128,1,128]{2,1,0:T(1,128)} %get-tuple-element.81), calls=%async_computation | async-start | bytes 131072 | tf_op jit(solution)/shard_map/all_to_all | solution.py:702
